TPU v7x, 32 devices: a whole 2x2x4 slice. The times are simulated.
32 devices in a mesh: rows: 8 (over z, x), leaf: 4 (over y, core).
Axes of the slice: x: 2, y: 2, z: 4, core: 2. Of those that a mesh axis runs over, the one named last changes fastest.
Arguments:
- right_sides: float32 [65536, 128], P(('rows', 'leaf')), may hold values from -30 to 30
- near_blocks: bfloat16 [2, 128, 512, 512], P(None, ('rows', 'leaf')), may hold values from -1 to 2.4
- leaf_bases: bfloat16 [2, 128, 2, 512, 128], P(None, ('rows', 'leaf')), may hold values from -1.5 to 1.5
- local_factors: bfloat16 [2, 224, 3, 128, 128], P(None, ('rows', 'leaf')), may hold values from -1.7 to 1.7
- upper_factors: bfloat16 [2, 32, 3, 3, 128, 128], P(None, ('rows', 'leaf')), may hold values from -1.7 to 1.7, as said below
- top_couplings: bfloat16 [2, 2, 128, 128], replicated, may hold values from -0.5 to 0.5
Outputs:
- solution: float32 [65536, 128], P(('rows', 'leaf'))
- residual_norms: float32 [3, 128], replicated
Inputs may be any that keep to these rules, and one draw needn't show every extreme that they name: upper_factors[s, d, h] is the same for all devices d with the same d // 2 ** (h + 1): the factors of the node h + 1 levels above device d's own node.
All inputs are finite; a program needn't handle non-finite values.
Results may differ from a plain program's by a relative error of at most 0.00095.
Values sent between devices are 32-bit elements; how exact they have to be, the bound alone decides.
No kernel may reach another device: no remote copies, remote signals or barrier semaphores. Data moves between devices by JAX's collectives and lax.ppermute only.
A program may use at most 128 MiB of HBM per device.

v0:
```python
import jax
import jax.numpy as jnp
from jax import lax
from jax.sharding import PartitionSpec as P

STEPS = 3


HIGHEST = lax.Precision.HIGHEST


def swapped(value, axis, distance):
    mask = 2**distance
    pairs = [(source, source ^ mask) for source in range(lax.axis_size(axis))]
    return lax.ppermute(value, axis, pairs)


def split_pair(values):
    upper_half = lax.optimization_barrier(values.astype(jnp.bfloat16))
    lower_half = (values - upper_half.astype(jnp.float32)).astype(jnp.bfloat16)
    return (upper_half, lower_half)


def sibling_of(values):
    shaped = values.reshape((values.shape[0] // 2, 2) + values.shape[1:])
    return shaped[:, ::-1].reshape(values.shape)


def parity(position, shift):
    return position // 2**shift % 2


def apply_device(operand_set, pieces, split_far, positions):
    near_set, basis_set, local_set, upper_set, top_set = operand_set
    leaf_position, row_position, bits_leaf, bits_rows = positions
    near_field = None
    coefficient = None
    for piece_value in pieces:
        near_term = jnp.einsum(
            "lij,ljc->lic", near_set, piece_value, preferred_element_type=jnp.float32
        )
        coefficient_term = jnp.einsum(
            "lir,lic->lrc", basis_set[:, 1], piece_value, preferred_element_type=jnp.float32
        )
        if near_field is None:
            near_field = near_term
            coefficient = coefficient_term
        else:
            near_field = near_field + near_term
            coefficient = coefficient + coefficient_term
    factors = local_set.astype(jnp.float32)
    lower_list = []
    table_list = []
    offset = 0
    node_count = near_set.shape[0]
    while node_count > 1:
        factor_table = factors[offset : offset + node_count]
        lower_list.append(coefficient)
        table_list.append(factor_table)
        projected = jnp.einsum("nab,nac->nbc", factor_table[:, 0], coefficient, precision=HIGHEST)
        coefficient = projected[0::2] + projected[1::2]
        offset = offset + node_count
        node_count = node_count // 2
    coefficient = coefficient[0]
    cross_tables = [factors[offset]] + [
        upper_set[upper_index] for upper_index in range(upper_set.shape[0])
    ]
    levels_up = bits_leaf + bits_rows
    sibling_list = []
    for height in range(bits_leaf):
        projected = jnp.dot(cross_tables[height][0].T, coefficient, precision=HIGHEST)
        sibling, sibling_projected = swapped((coefficient, projected), "leaf", height)
        sibling_list.append(sibling)
        coefficient = projected + sibling_projected
    for height in range(bits_leaf, levels_up):
        if height == levels_up - 1:
            sibling_list.append(swapped(coefficient, "rows", bits_rows - 1))
        else:
            projected = jnp.dot(cross_tables[height][0].T, coefficient, precision=HIGHEST)
            sibling, sibling_projected = swapped(
                (coefficient, projected), "rows", height - bits_leaf
            )
            sibling_list.append(sibling)
            coefficient = projected + sibling_projected
    top_position = parity(row_position, bits_rows - 1)
    top_block = lax.dynamic_index_in_dim(top_set, top_position, 0, keepdims=False).astype(
        jnp.float32
    )
    far_field = jnp.dot(top_block, sibling_list[levels_up - 1], precision=HIGHEST)
    for height in range(levels_up - 2, -1, -1):
        factor_table = cross_tables[height]
        far_field = jnp.dot(factor_table[1], far_field, precision=HIGHEST) + jnp.dot(
            factor_table[2], sibling_list[height], precision=HIGHEST
        )
    far_field = far_field[None]
    for factor_table, lower_value in zip(table_list[::-1], lower_list[::-1]):
        far_field = jnp.einsum(
            "nab,nbc->nac", factor_table[:, 1], jnp.repeat(far_field, 2, axis=0), precision=HIGHEST
        ) + jnp.einsum(
            "nab,nbc->nac", factor_table[:, 2], sibling_of(lower_value), precision=HIGHEST
        )
    if split_far:
        far_parts = split_pair(far_field)
    else:
        far_parts = (far_field.astype(jnp.bfloat16),)
    output = near_field
    for piece_value in far_parts:
        output = output + jnp.einsum(
            "lir,lrc->lic", basis_set[:, 0], piece_value, preferred_element_type=jnp.float32
        )
    return output


def body(right_sides, near_blocks, leaf_bases, local_factors, upper_factors, top_couplings):
    bits_leaf = lax.axis_size("leaf").bit_length() - 1
    bits_rows = lax.axis_size("rows").bit_length() - 1
    positions = (lax.axis_index("leaf"), lax.axis_index("rows"), bits_leaf, bits_rows)
    leaf_count = near_blocks.shape[1]
    column_count = right_sides.shape[1]
    right_side = right_sides.reshape(leaf_count, -1, column_count)
    operand_sets = []
    for member in range(2):
        operand_sets.append(
            (
                near_blocks[member],
                leaf_bases[member],
                local_factors[member],
                upper_factors[member, 0].astype(jnp.float32),
                top_couplings[member],
            )
        )
    solution = apply_device(operand_sets[1], (right_side.astype(jnp.bfloat16),), False, positions)
    norm_list = []
    for refine_step in range(STEPS):
        residual = right_side - apply_device(operand_sets[0], split_pair(solution), True, positions)
        partial_norm = jnp.sum(residual * residual, axis=(0, 1))
        norm_list.append(lax.psum(partial_norm, ("rows", "leaf")))
        solution = solution + apply_device(
            operand_sets[1], (residual.astype(jnp.bfloat16),), False, positions
        )
    norm_table = jnp.stack(norm_list)
    return (solution.reshape(-1, column_count), norm_table)


def solution(mesh):
    placed = (
        P(("rows", "leaf"), None),
        P(None, ("rows", "leaf"), None, None),
        P(None, ("rows", "leaf"), None, None, None),
        P(None, ("rows", "leaf"), None, None, None),
        P(None, ("rows", "leaf"), None, None, None, None),
        P(),
    )
    return jax.shard_map(
        body,
        mesh=mesh,
        in_specs=placed,
        out_specs=(P(("rows", "leaf"), None), P()),
        check_vma=False,
    )
```

profile of v0, /device:TPU:0, one launch (start us, length us, event | category | flops | bytes accessed | tf_op | source)
XLA Modules:
  0.0 351.0 jit_solution(10490166994885296596)
XLA Ops:
  0.6 1.9 fusion.341
  2.6 2.1 fusion.342
  6.4 2.0 copy_bitcast_fusion.1
  14.0 2.9 collective-permute-start.1
  16.9 2.4 collective-permute-done.1
  20.2 1.9 collective-permute-start.2
  22.1 2.4 collective-permute-done.2
  25.3 2.0 collective-permute-start.3
  30.3 2.9 collective-permute-start.4
  60.6 3.8 %collective-permute-done.10 = f32[128,128]{0,1:T(8,128)S(1)} collective-permute-done((f32[128,128]{0,1:T(8,128)S(1)}, f32[128,128]{0,1:T(8,128)S(1)}, u32[]{:S(2)}, u32[]{:S(2)}) %collective-permute-start.10) | collective-permute-done | bytes 65568 | tf_op jit(solution)/shard_map/ppermute | solution.py:15
  67.1 2.5 copy.61
  74.7 2.6 fusion.8
  105.9 2.7 collective-permute-done.19
  111.2 2.7 collective-permute-done.20
  116.6 2.6 collective-permute-done.21
  119.9 2.7 collective-permute-start.22
  154.4 3.8 %collective-permute-done.28 = f32[128,128]{0,1:T(8,128)S(1)} collective-permute-done((f32[128,128]{0,1:T(8,128)S(1)}, f32[128,128]{0,1:T(8,128)S(1)}, u32[]{:S(2)}, u32[]{:S(2)}) %collective-permute-start.28) | collective-permute-done | bytes 65568 | tf_op jit(solution)/shard_map/ppermute | solution.py:15
  159.0 3.7 %collective-permute-done.29 = f32[128,128]{0,1:T(8,128)S(1)} collective-permute-done((f32[128,128]{0,1:T(8,128)S(1)}, f32[128,128]{0,1:T(8,128)S(1)}, u32[]{:S(2)}, u32[]{:S(2)}) %collective-permute-start.29) | collective-permute-done | bytes 65568 | tf_op jit(solution)/shard_map/ppermute | solution.py:15
  192.4 2.7 collective-permute-done.37
  197.7 2.7 collective-permute-done.38
  203.1 2.6 collective-permute-done.39
  206.3 2.7 collective-permute-start.40
  217.0 1.9 collective-permute-start.41
  243.0 3.7 %collective-permute-done.46 = f32[128,128]{0,1:T(8,128)S(1)} collective-permute-done((f32[128,128]{0,1:T(8,128)S(1)}, f32[128,128]{0,1:T(8,128)S(1)}, u32[]{:S(2)}, u32[]{:S(2)}) %collective-permute-start.46) | collective-permute-done | bytes 65568 | tf_op jit(solution)/shard_map/ppermute | solution.py:15
  248.4 3.7 %collective-permute-done.47 = f32[128,128]{0,1:T(8,128)S(1)} collective-permute-done((f32[128,128]{0,1:T(8,128)S(1)}, f32[128,128]{0,1:T(8,128)S(1)}, u32[]{:S(2)}, u32[]{:S(2)}) %collective-permute-start.47) | collective-permute-done | bytes 65568 | tf_op jit(solution)/shard_map/ppermute | solution.py:15
  253.1 2.0 collective-permute-start.48
  283.6 2.7 collective-permute-done.55
  288.1 2.7 collective-permute-done.56
  294.4 40.9 %all-reduce = (f32[1,128]{1,0:T(1,128)S(1)}, f32[1,128]{1,0:T(1,128)S(1)}, f32[1,128]{1,0:T(1,128)S(1)}) all-reduce(f32[1,128]{1,0:T(1,128)S(1)} %bitcast.750, f32[1,128]{1,0:T(1,128)S(1)} %bitcast.749, f32[1,128]{1,0:T(1,128)S(1)} %bitcast.748), channel_id=1, replica_groups=mesh['rows'=8,'leaf'=4] {'rows','leaf'}, use_global_device_ids=true, to_apply=%region_5.6 | all-reduce | flops 384 | bytes 3072 | tf_op jit(solution)/shard_map/psum | solution.py:137
  336.8 2.3 collective-permute-start.61
  339.6 2.0 collective-permute-start.59
  348.4 2.5 fusion.21
  (501 shorter events, 225.1 us)
Async XLA Ops:
  14.0 5.3 %collective-permute-start.1 = (f32[128,128]{0,1:T(8,128)S(1)}, f32[128,128]{0,1:T(8,128)S(1)}, u32[]{:S(2)}, u32[]{:S(2)}) collective-permute-start(f32[128,128]{0,1:T(8,128)S(1)} %convolution_bitcast_fusion.41), channel_id=1, source_target_pairs={{0,2},{1,3},{2,0},{3,1},{4,6},{5,7},{6,4},{7,5},{8,10},{9,11},{10,... | collective-permute-start | bytes 196616 | tf_op jit(solution)/shard_map/ppermute | solution.py:15
  22.0 25.0 %collective-permute-start.8 = (f32[128,128]{0,1:T(8,128)}, f32[128,128]{0,1:T(8,128)}, u32[]{:S(2)}, u32[]{:S(2)}) collective-permute-start(f32[128,128]{0,1:T(8,128)} %fusion.101), channel_id=1, source_target_pairs={{0,1},{1,0},{2,3},{3,2},{4,5},{5,4},{6,7},{7,6},{8,9},{9,8},{10,11... | collective-permute-start | bytes 196616 | tf_op jit(solution)/shard_map/ppermute | solution.py:15
  30.3 11.8 %collective-permute-start.4 = (f32[128,128]{0,1:T(8,128)}, f32[128,128]{0,1:T(8,128)}, u32[]{:S(2)}, u32[]{:S(2)}) collective-permute-start(f32[128,128]{0,1:T(8,128)} %add.452), channel_id=1, source_target_pairs={{0,16},{4,20},{8,24},{12,28},{16,0},{20,4},{24,8},{28,12},{1,17},{... | collective-permute-start | bytes 196616 | tf_op jit(solution)/shard_map/ppermute | solution.py:15
  37.5 8.4 %collective-permute-start.7 = (f32[128,128]{0,1:T(8,128)}, f32[128,128]{0,1:T(8,128)S(1)}, u32[]{:S(2)}, u32[]{:S(2)}) collective-permute-start(f32[128,128]{0,1:T(8,128)} %copy-done.59), channel_id=1, source_target_pairs={{0,2},{1,3},{2,0},{3,1},{4,6},{5,7},{6,4},{7,5},{8,10},{9,11},{10,... | collective-permute-start | bytes 196616 | tf_op jit(solution)/shard_map/ppermute | solution.py:15
  39.0 6.4 %collective-permute-start.6 = (f32[128,128]{0,1:T(8,128)}, f32[128,128]{0,1:T(8,128)S(1)}, u32[]{:S(2)}, u32[]{:S(2)}) collective-permute-start(f32[128,128]{0,1:T(8,128)} %copy-done.60), channel_id=1, source_target_pairs={{0,4},{4,0},{8,12},{12,8},{16,20},{20,16},{24,28},{28,24},{1,5},{5... | collective-permute-start | bytes 196616 | tf_op jit(solution)/shard_map/ppermute | solution.py:15
  66.6 4.6 %collective-permute-start.11 = (f32[128,128]{0,1:T(8,128)}, f32[128,128]{0,1:T(8,128)}, u32[]{:S(2)}, u32[]{:S(2)}) collective-permute-start(f32[128,128]{0,1:T(8,128)} %convolution_bitcast_fusion.36), channel_id=1, source_target_pairs={{0,4},{4,0},{8,12},{12,8},{16,20},{20,16},{24,28},{28,24},{1,5},{5... | collective-permute-start | bytes 196616 | tf_op jit(solution)/shard_map/ppermute | solution.py:15
  78.0 8.0 %collective-permute-start.13 = (f32[128,128]{0,1:T(8,128)}, f32[128,128]{0,1:T(8,128)}, u32[]{:S(2)}, u32[]{:S(2)}) collective-permute-start(f32[128,128]{0,1:T(8,128)} %add.469), channel_id=1, source_target_pairs={{0,16},{4,20},{8,24},{12,28},{16,0},{20,4},{24,8},{28,12},{1,17},{... | collective-permute-start | bytes 196616 | tf_op jit(solution)/shard_map/ppermute | solution.py:15
  81.7 13.0 %collective-permute-start.17 = (f32[128,128]{0,1:T(8,128)}, f32[128,128]{0,1:T(8,128)}, u32[]{:S(2)}, u32[]{:S(2)}) collective-permute-start(f32[128,128]{0,1:T(8,128)} %copy-done.62), channel_id=1, source_target_pairs={{0,1},{1,0},{2,3},{3,2},{4,5},{5,4},{6,7},{7,6},{8,9},{9,8},{10,11... | collective-permute-start | bytes 196616 | tf_op jit(solution)/shard_map/ppermute | solution.py:15
  83.4 9.4 %collective-permute-start.16 = (f32[128,128]{0,1:T(8,128)}, f32[128,128]{0,1:T(8,128)S(1)}, u32[]{:S(2)}, u32[]{:S(2)}) collective-permute-start(f32[128,128]{0,1:T(8,128)} %copy-done.67), channel_id=1, source_target_pairs={{0,2},{1,3},{2,0},{3,1},{4,6},{5,7},{6,4},{7,5},{8,10},{9,11},{10,... | collective-permute-start | bytes 196616 | tf_op jit(solution)/shard_map/ppermute | solution.py:15
  83.9 6.9 %collective-permute-start.15 = (f32[128,128]{0,1:T(8,128)}, f32[128,128]{0,1:T(8,128)S(1)}, u32[]{:S(2)}, u32[]{:S(2)}) collective-permute-start(f32[128,128]{0,1:T(8,128)} %copy-done.72), channel_id=1, source_target_pairs={{0,4},{4,0},{8,12},{12,8},{16,20},{20,16},{24,28},{28,24},{1,5},{5... | collective-permute-start | bytes 196616 | tf_op jit(solution)/shard_map/ppermute | solution.py:15
  84.4 4.5 %collective-permute-start.14 = (f32[128,128]{0,1:T(8,128)}, f32[128,128]{0,1:T(8,128)S(1)}, u32[]{:S(2)}, u32[]{:S(2)}) collective-permute-start(f32[128,128]{0,1:T(8,128)} %copy-done.77), channel_id=1, source_target_pairs={{0,8},{4,12},{8,0},{12,4},{16,24},{20,28},{24,16},{28,20},{1,9},{5... | collective-permute-start | bytes 196616 | tf_op jit(solution)/shard_map/ppermute | solution.py:15
  119.9 12.7 %collective-permute-start.22 = (f32[128,128]{0,1:T(8,128)}, f32[128,128]{0,1:T(8,128)}, u32[]{:S(2)}, u32[]{:S(2)}) collective-permute-start(f32[128,128]{0,1:T(8,128)} %add.488), channel_id=1, source_target_pairs={{0,16},{4,20},{8,24},{12,28},{16,0},{20,4},{24,8},{28,12},{1,17},{... | collective-permute-start | bytes 196616 | tf_op jit(solution)/shard_map/ppermute | solution.py:15
  126.1 15.0 %collective-permute-start.26 = (f32[128,128]{0,1:T(8,128)}, f32[128,128]{0,1:T(8,128)}, u32[]{:S(2)}, u32[]{:S(2)}) collective-permute-start(f32[128,128]{0,1:T(8,128)} %copy-done.65), channel_id=1, source_target_pairs={{0,1},{1,0},{2,3},{3,2},{4,5},{5,4},{6,7},{7,6},{8,9},{9,8},{10,11... | collective-permute-start | bytes 196616 | tf_op jit(solution)/shard_map/ppermute | solution.py:15
  127.8 11.4 %collective-permute-start.25 = (f32[128,128]{0,1:T(8,128)}, f32[128,128]{0,1:T(8,128)S(1)}, u32[]{:S(2)}, u32[]{:S(2)}) collective-permute-start(f32[128,128]{0,1:T(8,128)} %copy-done.70), channel_id=1, source_target_pairs={{0,2},{1,3},{2,0},{3,1},{4,6},{5,7},{6,4},{7,5},{8,10},{9,11},{10,... | collective-permute-start | bytes 196616 | tf_op jit(solution)/shard_map/ppermute | solution.py:15
  129.3 7.9 %collective-permute-start.24 = (f32[128,128]{0,1:T(8,128)}, f32[128,128]{0,1:T(8,128)S(1)}, u32[]{:S(2)}, u32[]{:S(2)}) collective-permute-start(f32[128,128]{0,1:T(8,128)} %copy-done.75), channel_id=1, source_target_pairs={{0,4},{4,0},{8,12},{12,8},{16,20},{20,16},{24,28},{28,24},{1,5},{5... | collective-permute-start | bytes 196616 | tf_op jit(solution)/shard_map/ppermute | solution.py:15
  168.3 8.0 %collective-permute-start.31 = (f32[128,128]{0,1:T(8,128)}, f32[128,128]{0,1:T(8,128)}, u32[]{:S(2)}, u32[]{:S(2)}) collective-permute-start(f32[128,128]{0,1:T(8,128)} %add.507), channel_id=1, source_target_pairs={{0,16},{4,20},{8,24},{12,28},{16,0},{20,4},{24,8},{28,12},{1,17},{... | collective-permute-start | bytes 196616 | tf_op jit(solution)/shard_map/ppermute | solution.py:15
  172.0 9.2 %collective-permute-start.35 = (f32[128,128]{0,1:T(8,128)}, f32[128,128]{0,1:T(8,128)}, u32[]{:S(2)}, u32[]{:S(2)}) collective-permute-start(f32[128,128]{0,1:T(8,128)} %copy-done.64), channel_id=1, source_target_pairs={{0,1},{1,0},{2,3},{3,2},{4,5},{5,4},{6,7},{7,6},{8,9},{9,8},{10,11... | collective-permute-start | bytes 196616 | tf_op jit(solution)/shard_map/ppermute | solution.py:15
  173.7 6.3 %collective-permute-start.34 = (f32[128,128]{0,1:T(8,128)}, f32[128,128]{0,1:T(8,128)S(1)}, u32[]{:S(2)}, u32[]{:S(2)}) collective-permute-start(f32[128,128]{0,1:T(8,128)} %copy-done.69), channel_id=1, source_target_pairs={{0,2},{1,3},{2,0},{3,1},{4,6},{5,7},{6,4},{7,5},{8,10},{9,11},{10,... | collective-permute-start | bytes 196616 | tf_op jit(solution)/shard_map/ppermute | solution.py:15
  174.2 5.4 %collective-permute-start.33 = (f32[128,128]{0,1:T(8,128)}, f32[128,128]{0,1:T(8,128)S(1)}, u32[]{:S(2)}, u32[]{:S(2)}) collective-permute-start(f32[128,128]{0,1:T(8,128)} %copy-done.74), channel_id=1, source_target_pairs={{0,4},{4,0},{8,12},{12,8},{16,20},{20,16},{24,28},{28,24},{1,5},{5... | collective-permute-start | bytes 196616 | tf_op jit(solution)/shard_map/ppermute | solution.py:15
  206.3 12.6 %collective-permute-start.40 = (f32[128,128]{0,1:T(8,128)}, f32[128,128]{0,1:T(8,128)}, u32[]{:S(2)}, u32[]{:S(2)}) collective-permute-start(f32[128,128]{0,1:T(8,128)} %add.526), channel_id=1, source_target_pairs={{0,16},{4,20},{8,24},{12,28},{16,0},{20,4},{24,8},{28,12},{1,17},{... | collective-permute-start | bytes 196616 | tf_op jit(solution)/shard_map/ppermute | solution.py:15
  212.3 15.0 %collective-permute-start.44 = (f32[128,128]{0,1:T(8,128)}, f32[128,128]{0,1:T(8,128)}, u32[]{:S(2)}, u32[]{:S(2)}) collective-permute-start(f32[128,128]{0,1:T(8,128)} %copy-done.66), channel_id=1, source_target_pairs={{0,1},{1,0},{2,3},{3,2},{4,5},{5,4},{6,7},{7,6},{8,9},{9,8},{10,11... | collective-permute-start | bytes 196616 | tf_op jit(solution)/shard_map/ppermute | solution.py:15
  214.0 11.4 %collective-permute-start.43 = (f32[128,128]{0,1:T(8,128)}, f32[128,128]{0,1:T(8,128)S(1)}, u32[]{:S(2)}, u32[]{:S(2)}) collective-permute-start(f32[128,128]{0,1:T(8,128)} %copy-done.71), channel_id=1, source_target_pairs={{0,2},{1,3},{2,0},{3,1},{4,6},{5,7},{6,4},{7,5},{8,10},{9,11},{10,... | collective-permute-start | bytes 196616 | tf_op jit(solution)/shard_map/ppermute | solution.py:15
  215.5 7.9 %collective-permute-start.42 = (f32[128,128]{0,1:T(8,128)}, f32[128,128]{0,1:T(8,128)S(1)}, u32[]{:S(2)}, u32[]{:S(2)}) collective-permute-start(f32[128,128]{0,1:T(8,128)} %copy-done.76), channel_id=1, source_target_pairs={{0,4},{4,0},{8,12},{12,8},{16,20},{20,16},{24,28},{28,24},{1,5},{5... | collective-permute-start | bytes 196616 | tf_op jit(solution)/shard_map/ppermute | solution.py:15
  258.1 8.1 %collective-permute-start.49 = (f32[128,128]{0,1:T(8,128)}, f32[128,128]{0,1:T(8,128)}, u32[]{:S(2)}, u32[]{:S(2)}) collective-permute-start(f32[128,128]{0,1:T(8,128)} %add.545), channel_id=1, source_target_pairs={{0,16},{4,20},{8,24},{12,28},{16,0},{20,4},{24,8},{28,12},{1,17},{... | collective-permute-start | bytes 196616 | tf_op jit(solution)/shard_map/ppermute | solution.py:15
  261.8 13.0 %collective-permute-start.53 = (f32[128,128]{0,1:T(8,128)}, f32[128,128]{0,1:T(8,128)}, u32[]{:S(2)}, u32[]{:S(2)}) collective-permute-start(f32[128,128]{0,1:T(8,128)} %copy-done.63), channel_id=1, source_target_pairs={{0,1},{1,0},{2,3},{3,2},{4,5},{5,4},{6,7},{7,6},{8,9},{9,8},{10,11... | collective-permute-start | bytes 196616 | tf_op jit(solution)/shard_map/ppermute | solution.py:15
  263.5 9.4 %collective-permute-start.52 = (f32[128,128]{0,1:T(8,128)}, f32[128,128]{0,1:T(8,128)S(1)}, u32[]{:S(2)}, u32[]{:S(2)}) collective-permute-start(f32[128,128]{0,1:T(8,128)} %copy-done.68), channel_id=1, source_target_pairs={{0,2},{1,3},{2,0},{3,1},{4,6},{5,7},{6,4},{7,5},{8,10},{9,11},{10,... | collective-permute-start | bytes 196616 | tf_op jit(solution)/shard_map/ppermute | solution.py:15
  264.0 6.9 %collective-permute-start.51 = (f32[128,128]{0,1:T(8,128)}, f32[128,128]{0,1:T(8,128)S(1)}, u32[]{:S(2)}, u32[]{:S(2)}) collective-permute-start(f32[128,128]{0,1:T(8,128)} %copy-done.73), channel_id=1, source_target_pairs={{0,4},{4,0},{8,12},{12,8},{16,20},{20,16},{24,28},{28,24},{1,5},{5... | collective-permute-start | bytes 196616 | tf_op jit(solution)/shard_map/ppermute | solution.py:15
  288.1 57.9 %collective-permute-start.62 = (f32[128,128]{0,1:T(8,128)S(1)}, f32[128,128]{0,1:T(8,128)S(1)}, u32[]{:S(2)}, u32[]{:S(2)}) collective-permute-start(f32[128,128]{0,1:T(8,128)S(1)} %fusion.95), channel_id=1, source_target_pairs={{0,1},{1,0},{2,3},{3,2},{4,5},{5,4},{6,7},{7,6},{8,9},{9,8},{10,11... | collective-permute-start | bytes 196616 | tf_op jit(solution)/shard_map/ppermute | solution.py:15
  291.0 44.4 %collective-permute-start.57 = (f32[128,128]{0,1:T(8,128)S(1)}, f32[128,128]{0,1:T(8,128)S(1)}, u32[]{:S(2)}, u32[]{:S(2)}) collective-permute-start(f32[128,128]{0,1:T(8,128)S(1)} %convolution_bitcast_fusion.15), channel_id=1, source_target_pairs={{0,8},{4,12},{8,0},{12,4},{16,24},{20,28},{24,16},{28,20},{1,9},{5... | collective-permute-start | bytes 196616 | tf_op jit(solution)/shard_map/ppermute | solution.py:15
  335.4 6.3 %collective-permute-start.58 = (f32[128,128]{0,1:T(8,128)S(1)}, f32[128,128]{0,1:T(8,128)S(1)}, u32[]{:S(2)}, u32[]{:S(2)}) collective-permute-start(f32[128,128]{0,1:T(8,128)S(1)} %add.564), channel_id=1, source_target_pairs={{0,16},{4,20},{8,24},{12,28},{16,0},{20,4},{24,8},{28,12},{1,17},{... | collective-permute-start | bytes 196616 | tf_op jit(solution)/shard_map/ppermute | solution.py:15
  336.8 7.9 %collective-permute-start.61 = (f32[128,128]{0,1:T(8,128)S(1)}, f32[128,128]{0,1:T(8,128)S(1)}, u32[]{:S(2)}, u32[]{:S(2)}) collective-permute-start(f32[128,128]{0,1:T(8,128)S(1)} %add.561), channel_id=1, source_target_pairs={{0,2},{1,3},{2,0},{3,1},{4,6},{5,7},{6,4},{7,5},{8,10},{9,11},{10,... | collective-permute-start | bytes 196616 | tf_op jit(solution)/shard_map/ppermute | solution.py:15
  339.1 5.2 %collective-permute-start.60 = (f32[128,128]{0,1:T(8,128)S(1)}, f32[128,128]{0,1:T(8,128)S(1)}, u32[]{:S(2)}, u32[]{:S(2)}) collective-permute-start(f32[128,128]{0,1:T(8,128)S(1)} %add.562), channel_id=1, source_target_pairs={{0,4},{4,0},{8,12},{12,8},{16,20},{20,16},{24,28},{28,24},{1,5},{5... | collective-permute-start | bytes 196616 | tf_op jit(solution)/shard_map/ppermute | solution.py:15
  (114 other events, 895.0 us)
where the time goes:
time: 356 us; the launch traced here: 351 us
  matrix products  120 us (34%)
  starting transfers between devices  69.2 us (19%)
  waiting for transfers between devices  65.8 us (18%)
  local copies, waits for them, and re-layouts  46.1 us (13%)
  blocking collectives  40.9 us (11%)
  other arithmetic  6.28 us (2%)
    ppermute x63, starting transfers between devices, swapped(): return lax.ppermute(value, axis, pairs)  69.2 us
    ppermute x63, waiting for transfers between devices, swapped(): return lax.ppermute(value, axis, pairs)  65.8 us
    psum x1, blocking collectives, body(): norm_list.append(lax.psum(partial_norm, ('rows', 'leaf')))  40.9 us
    dot_general x28, matrix products, apply_device(): jnp.dot(factor_table[2], sibling_list[height], precision=HIGHEST)  20.8 us
    dot_general x28, matrix products, apply_device(): jnp.dot(factor_table[1], far_field, precision=HIGHEST)  20.6 us
    dot_general x28, matrix products, apply_device(): jnp.dot(cross_tables[height][0].T, coefficient, precision=HIGHEST)  20.3 us
    dot_general x10, matrix products, apply_device(): jnp.einsum('lij,ljc->lic', near_set, piece_value, preferred_element_type=...  16.6 us
    unnamed x168, local copies, waits for them, and re-layouts  10.8 us
  transfers between devices with their start and end apart: 63, of which 34 were waited for; matrix products, arithmetic and copies ran while one was open for 23% of the time, Pallas kernels for 0%

commit v1 on v0

v1 whole, which is shorter than its diff:
```python
import functools

import jax
import jax.numpy as jnp
from jax import lax
from jax.experimental import pallas as pl
from jax.experimental.pallas import tpu as pltpu
from jax.sharding import PartitionSpec as P

STEPS = 3
BF16 = jnp.bfloat16
F32 = jnp.float32
VMEM_LIMIT = 16 * 2**20


def mm(left, right):
    return jnp.dot(left, right, preferred_element_type=F32)


def pieces(value):
    high = value.astype(BF16)
    return high, (value - high.astype(F32)).astype(BF16)


def left_mul(table, value):
    high, low = pieces(value)
    width = value.shape[1]
    both = mm(table[0], jnp.concatenate([high, low], axis=1))
    return both[:, :width] + both[:, width:] + mm(table[1], high)


def right_mul(value, table):
    high, low = pieces(value)
    rows = value.shape[0]
    both = mm(jnp.concatenate([high, low], axis=0), table[0])
    return both[:rows] + both[rows:] + mm(high, table[1])


def mul(left, right):
    return left_mul(pieces(left), right)


def exact_left(table, value):
    high, low = pieces(value)
    width = value.shape[1]
    both = mm(table, jnp.concatenate([high, low], axis=1))
    return both[:, :width] + both[:, width:]


def exact_right(value, table):
    high, low = pieces(value)
    rows = value.shape[0]
    both = mm(jnp.concatenate([high, low], axis=0), table)
    return both[:rows] + both[rows:]


def put(ref, index, value):
    high, low = pieces(value)
    ref[(0,) + index] = high
    ref[(1,) + index] = low


def call(kernel, outs, args, flops):
    specs = [pl.BlockSpec(memory_space=pltpu.SMEM)]
    specs += [pl.BlockSpec(memory_space=pltpu.VMEM)] * (len(args) - 1)
    return pl.pallas_call(
        kernel,
        out_shape=[jax.ShapeDtypeStruct(shape, dtype) for shape, dtype in outs],
        in_specs=specs,
        out_specs=[pl.BlockSpec(memory_space=pltpu.VMEM)] * len(outs),
        compiler_params=pltpu.CompilerParams(vmem_limit_bytes=VMEM_LIMIT),
        cost_estimate=pl.CostEstimate(flops=flops, bytes_accessed=0, transcendentals=0),
    )(*args)


def level_offsets(leaf_count):
    offsets, count, offset = [], leaf_count, 0
    while count >= 1:
        offsets.append(offset)
        offset += count
        count //= 2
    return offsets


def send_parts(core, device, lifted, send_ref, keep_ref):
    columns = lifted.shape[1]
    half = columns // 2
    turned = lifted.T
    first = core == 0
    keep_ref[...] = jnp.where(first, turned[:half], turned[half:])
    send_ref[: device.shape[0]] = device
    send_ref[device.shape[0] :] = jnp.where(first, turned[half:], turned[:half])


def start_kernel(leaves, core_ref, right_ref, vt_ref, pt_ref, up_ref, coef_ref, send_ref, keep_ref):
    rank = pt_ref.shape[-1]
    offsets = level_offsets(leaves)
    for member in (1, 0):
        for leaf in range(leaves):
            trail = pt_ref[member, leaf].astype(F32)
            for depth in range(1, len(offsets)):
                table = pt_ref[member, offsets[depth] + (leaf >> depth)]
                if depth == len(offsets) - 1:
                    put(up_ref, (member, slice(0, rank), pl.ds(leaf * rank, rank)), trail)
                trail = exact_left(table, trail)
            put(up_ref, (member, slice(rank, 2 * rank), pl.ds(leaf * rank, rank)), trail)
    rows = right_ref.shape[0] // leaves
    for leaf in range(leaves):
        value = right_ref[leaf * rows : (leaf + 1) * rows].astype(BF16)
        coef_ref[leaf * rank : (leaf + 1) * rank] = mm(vt_ref[1, leaf], value)
    lifted = left_mul((up_ref[0, 1], up_ref[1, 1]), coef_ref[...])
    send_parts(core_ref[0], lifted[:rank], lifted[rank:], send_ref, keep_ref)


def stage_table_kernel(core_ref, own_ref, *refs):
    near_ref, far_ref, cross_ref, out_ref = refs
    rank = own_ref.shape[-1]
    for member in range(2):
        here = own_ref[member, 1].astype(BF16)
        there = far_ref[2 + member].astype(BF16)
        lowers = (own_ref[member, 0], near_ref[member], far_ref[member], cross_ref[member])
        for index, (lower, upper) in enumerate(zip(lowers, (here, here, there, there))):
            put(out_ref, (member, pl.ds(index * rank, rank)), mm(lower.astype(BF16), upper))


def local_table_kernel(
    leaves, core_ref, pt_ref, qc_ref, u_ref, vt_ref, up_ref, wide_ref, down_ref, feed_ref, chip_ref
):
    rank = pt_ref.shape[-1]
    offsets = level_offsets(leaves)
    own = offsets[-1]
    for member in range(2):
        other = 1 - member
        sign = 1.0 if member == 1 else -1.0
        total = None
        for leaf in range(leaves):
            rows = pl.ds(leaf * rank, rank)
            trail = None
            for depth in range(len(offsets) - 1):
                node = leaf >> depth
                step = qc_ref[member, offsets[depth] + node, 0]
                coupling = qc_ref[member, offsets[depth] + node, 1]
                coupled = coupling.astype(F32) if trail is None else exact_right(trail, coupling)
                for peer in range(leaves):
                    if peer >> depth != node ^ 1:
                        continue
                    entry = coupled
                    for lower in range(depth - 1, -1, -1):
                        entry = exact_right(entry, pt_ref[member, offsets[lower] + (peer >> lower)])
                    put(wide_ref, (member, rows, pl.ds((1 + peer) * rank, rank)), entry)
                trail = step.astype(F32) if trail is None else exact_right(trail, step)
            put(
                wide_ref,
                (member, rows, pl.ds((1 + leaf) * rank, rank)),
                jnp.zeros((rank, rank), F32),
            )
            put(wide_ref, (member, rows, pl.ds(0, rank)), exact_right(trail, qc_ref[member, own, 1]))
            below = exact_right(trail, qc_ref[member, own, 0])
            put(down_ref, (member, rows), below)
            feed = sign * mul(mm(vt_ref[other, leaf], u_ref[member, leaf]), below)
            put(feed_ref, (member, rows), feed)
            table = (
                up_ref[0, other, :, pl.ds(leaf * rank, rank)],
                up_ref[1, other, :, pl.ds(leaf * rank, rank)],
            )
            term = left_mul(table, feed)
            total = term if total is None else total + term
        chip_ref[2 * member] = total[:rank]
        chip_ref[2 * member + 1] = total[rank:].T


def far_table_kernel(plan, core_ref, qct_ref, top_ref, chip_ref, got_ref, *refs):
    lower_refs, (far_ref, sibling_ref) = refs[:-2], refs[-2:]
    rank = top_ref.shape[-1]
    for member in range(2):
        put(sibling_ref, (member,), got_ref[2 * member])
        loop = pieces(chip_ref[2 * member + 1] + got_ref[2 * member + 1])
        trail = None
        couplings = []
        levels = qct_ref.shape[1] + 1
        for level in range(levels):
            coupling = top_ref[member] if level == levels - 1 else qct_ref[member, level, 1]
            couplings.append(
                coupling.astype(F32) if trail is None else exact_left(coupling, trail)
            )
            if level < levels - 1:
                step = qct_ref[member, level, 0]
                trail = step.astype(F32) if trail is None else exact_left(step, trail)
        for index, (level, lower) in enumerate(plan):
            weight = couplings[level]
            if lower is not None:
                weight = exact_left(lower_refs[lower][member].astype(BF16), weight)
            rows = pl.ds(index * rank, rank)
            put(far_ref, (member, rows, slice(0, rank)), right_mul(weight, loop))
            put(far_ref, (member, rows, slice(rank, 2 * rank)), weight)


def stage_kernel(member, core_ref, table_ref, *refs):
    rank = table_ref.shape[-1]
    total = None
    for index, ref in enumerate(refs[:-1]):
        rows = pl.ds(index * rank, rank)
        term = right_mul(ref[...], (table_ref[0, member, rows], table_ref[1, member, rows]))
        total = term if total is None else total + term
    refs[-1][...] = total


def far_kernel(member, last, core_ref, table_ref, keep_ref, got_ref, *refs):
    count = len(refs) - (1 if last else 2)
    rank = table_ref.shape[-1] // 2
    total = None
    for index in range(count):
        rows = pl.ds(index * rank, rank)
        table = (table_ref[0, member, rows], table_ref[1, member, rows])
        term = right_mul(refs[index][...], table)
        total = term if total is None else total + term
    if not last:
        refs[count][...] = keep_ref[...] + got_ref[rank:] + total[:, :rank]
    refs[-1][...] = total[:, rank:]


def far_rows(core, mine_ref, theirs_ref):
    mine, theirs = mine_ref[...], theirs_ref[...]
    first = core == 0
    return jnp.concatenate(
        [jnp.where(first, mine, theirs), jnp.where(first, theirs, mine)], axis=0
    ).T


def expand(member, base, far):
    if member == 0:
        return exact_left(base, far)
    return mm(base, far.astype(BF16))


def local_kernel(member, leaves, first, *refs):
    refs = list(refs)
    core = refs.pop(0)[0]
    near_ref, u_ref, vt_ref, up_ref, wide_ref = (refs.pop(0) for _ in range(5))
    base_ref, other_ref, coef_ref, got_ref = (refs.pop(0) for _ in range(4))
    other = 1 - member
    rank = up_ref.shape[-1] // leaves
    rows = base_ref.shape[0] // leaves
    if first:
        coef = coef_ref[...]
        sibling = got_ref[:rank]
    else:
        down_ref, feed_ref, sibling_ref, mine_ref, theirs_ref = (refs.pop(0) for _ in range(5))
        far = far_rows(core, mine_ref, theirs_ref)
        coef = coef_ref[...] + left_mul((feed_ref[0, other], feed_ref[1, other]), far)
        sibling = got_ref[:rank] + left_mul((sibling_ref[0, other], sibling_ref[1, other]), far)
        leaf_far = left_mul((down_ref[0, other], down_ref[1, other]), far)
    out_ref, next_ref, send_ref, keep_ref = refs[:4]
    table = (wide_ref[0, member], wide_ref[1, member])
    inner = left_mul(table, jnp.concatenate([sibling, coef], axis=0))
    norm = None
    for leaf in range(leaves):
        part = slice(leaf * rows, (leaf + 1) * rows)
        small = slice(leaf * rank, (leaf + 1) * rank)
        value = base_ref[part]
        if not first:
            moved = expand(other, u_ref[other, leaf], leaf_far[small])
            value = value + moved if other == 1 else value - moved
            if other == 1:
                refs[4][part] = value
            else:
                term = jnp.sum(value * value, axis=0, keepdims=True)
                norm = term if norm is None else norm + term
        near = near_ref[member, leaf]
        if member == 0:
            result = exact_left(near, value)
        else:
            result = mm(near, value.astype(BF16))
        result = result + expand(member, u_ref[member, leaf], inner[small])
        if member == 0:
            result = other_ref[part] - result
        elif not first:
            result = other_ref[part] + result
        out_ref[part] = result
        if other == 0:
            next_ref[small] = exact_left(vt_ref[other, leaf], result)
        else:
            next_ref[small] = mm(vt_ref[other, leaf], result.astype(BF16))
    if norm is not None:
        refs[4][...] = norm
    lifted = left_mul((up_ref[0, other], up_ref[1, other]), next_ref[...])
    send_parts(core, lifted[:rank], lifted[rank:], send_ref, keep_ref)


def last_local_kernel(leaves, core_ref, near_ref, u_ref, vt_ref, up_ref, wide_ref, *refs):
    member, other = 1, 0
    base_ref, other_ref, coef_ref, got_ref = refs[:4]
    down_ref, feed_ref, sibling_ref, mine_ref, theirs_ref, out_ref, norm_ref = refs[4:]
    rank = up_ref.shape[-1] // leaves
    rows = base_ref.shape[0] // leaves
    far = far_rows(core_ref[0], mine_ref, theirs_ref)
    coef = coef_ref[...] + left_mul((feed_ref[0, other], feed_ref[1, other]), far)
    sibling = got_ref[:rank] + left_mul((sibling_ref[0, other], sibling_ref[1, other]), far)
    leaf_far = left_mul((down_ref[0, other], down_ref[1, other]), far)
    table = (wide_ref[0, member], wide_ref[1, member])
    inner = left_mul(table, jnp.concatenate([sibling, coef], axis=0))
    norm = None
    for leaf in range(leaves):
        part = slice(leaf * rows, (leaf + 1) * rows)
        small = slice(leaf * rank, (leaf + 1) * rank)
        value = base_ref[part] - expand(other, u_ref[other, leaf], leaf_far[small])
        term = jnp.sum(value * value, axis=0, keepdims=True)
        norm = term if norm is None else norm + term
        result = mm(near_ref[member, leaf], value.astype(BF16))
        result = result + expand(member, u_ref[member, leaf], inner[small])
        out_ref[part] = other_ref[part] + result
    norm_ref[...] = norm


def finish_kernel(leaves, core_ref, u_ref, down_ref, base_ref, mine_ref, theirs_ref, out_ref):
    rank = down_ref.shape[-1]
    rows = base_ref.shape[0] // leaves
    far = far_rows(core_ref[0], mine_ref, theirs_ref)
    leaf_far = left_mul((down_ref[0, 1], down_ref[1, 1]), far)
    for leaf in range(leaves):
        part = slice(leaf * rows, (leaf + 1) * rows)
        small = slice(leaf * rank, (leaf + 1) * rank)
        out_ref[part] = base_ref[part] + expand(1, u_ref[1, leaf], leaf_far[small])


def body(right_sides, near_blocks, leaf_bases, local_factors, upper_factors, top_couplings):
    bits_leaf = lax.axis_size("leaf").bit_length() - 1
    bits_rows = lax.axis_size("rows").bit_length() - 1
    levels_up = bits_leaf + bits_rows
    row_axis, leaf_size = lax.axis_size("rows"), lax.axis_size("leaf")
    leaves = near_blocks.shape[1]
    columns = right_sides.shape[1]
    rank = leaf_bases.shape[-1]
    half = columns // 2
    core = (lax.axis_index("leaf") % 2).astype(jnp.int32).reshape(1)
    top_position = lax.axis_index("rows") // 2 ** (bits_rows - 1) % 2

    def swap(value, mask):
        pairs = [(source, source ^ mask) for source in range(row_axis * leaf_size)]
        return lax.ppermute(value, ("rows", "leaf"), pairs)

    stages = []
    level = 1
    while level < levels_up:
        stages.append(tuple(range(level, min(level + 2, levels_up))))
        level += 2

    def masks_of(stage):
        low = 2 ** stage[0]
        return (low,) if len(stage) == 1 else (low, 2 * low, 3 * low)

    vt = jnp.swapaxes(leaf_bases[:, :, 1], -1, -2)
    u = leaf_bases[:, :, 0]
    pt = jnp.swapaxes(local_factors[:, :, 0], -1, -2)
    qc = local_factors[:, :, 1:]
    upper = upper_factors[:, 0]
    upper_p = upper[:, :, 0]
    qct = jnp.swapaxes(upper[:, :, 1:], -1, -2)
    top = lax.dynamic_index_in_dim(top_couplings, top_position, 1, keepdims=False)
    top = jnp.swapaxes(top, -1, -2)

    unit = rank * rank * columns
    up, coef, send, keep = call(
        functools.partial(start_kernel, leaves),
        [
            ((2, 2, 2 * rank, leaves * rank), BF16),
            ((leaves * rank, columns), F32),
            ((rank + half, rank), F32),
            ((half, rank), F32),
        ],
        [core, right_sides, vt, pt],
        150 * unit,
    )
    got = swap(send, 1)

    stage_tables, lower_refs, plan = [], [], []
    for stage in stages:
        low = 2 ** stage[0]
        base = stage[0] - 1
        if len(stage) == 1:
            plan.append((base, None))
            if stage[-1] == levels_up - 1:
                continue
        lower = upper_p[:, base].astype(F32)
        last = stage[-1] == levels_up - 1
        cross_got = swap(lower, 3 * low)
        if last:
            far_got = swap(lower, 2 * low)
        else:
            both = upper_p[:, base : base + 2].astype(F32)
            far_got = swap(
                jnp.swapaxes(both, 0, 1).reshape(4, rank, rank), 2 * low
            )
            near_got = swap(lower, low)
            stage_tables.append(
                call(
                    stage_table_kernel,
                    [((2, 2, 4 * rank, rank), BF16)],
                    [core, upper_p[:, base : base + 2], near_got, far_got, cross_got],
                    16 * unit,
                )[0]
            )
        plan.append((base, None))
        plan.append((base + 1, len(lower_refs)))
        plan.append((base + 1, len(lower_refs) + 1))
        lower_refs += [far_got, cross_got]

    wide, down, feed, chip_feed = call(
        functools.partial(local_table_kernel, leaves),
        [
            ((2, 2, leaves * rank, (leaves + 1) * rank), BF16),
            ((2, 2, leaves * rank, rank), BF16),
            ((2, 2, leaves * rank, rank), BF16),
            ((4, rank, rank), F32),
        ],
        [core, pt, qc, u, vt, up],
        300 * unit,
    )
    chip_got = swap(chip_feed, 1)
    far_table, sibling_table = call(
        functools.partial(far_table_kernel, plan),
        [((2, 2, len(plan) * rank, 2 * rank), BF16), ((2, 2, rank, rank), BF16)],
        [core, qct, top, chip_feed, chip_got] + lower_refs,
        100 * unit,
    )

    applies = 2 * STEPS + 1
    size = (right_sides.shape, F32)
    chip = keep + got[rank:]
    member = 1
    base = right_sides
    current = right_sides
    norms = []
    mine = theirs = None
    for index in range(applies):
        last = index == applies - 1
        shared = [core, near_blocks, u, vt, up, wide, base, current, coef, got]
        if index:
            shared += [down, feed, sibling_table, mine, theirs]
        arrived = []
        value = chip
        for number, stage in enumerate(stages):
            batch = [swap(value, mask) for mask in masks_of(stage)]
            arrived += batch
            if number < len(stages) - 1:
                value = call(
                    functools.partial(stage_kernel, member),
                    [((half, rank), F32)],
                    [core, stage_tables[number], value] + batch,
                    8 * unit,
                )[0]
        if last:
            base, norm = call(
                functools.partial(last_local_kernel, leaves),
                [size, ((1, columns), F32)],
                shared,
                200 * unit,
            )
            norms.append(norm)
        else:
            outs = [
                size,
                ((leaves * rank, columns), F32),
                ((rank + half, rank), F32),
                ((half, rank), F32),
            ]
            if index:
                outs.append(size if member == 0 else ((1, columns), F32))
            results = call(
                functools.partial(local_kernel, member, leaves, index == 0), outs, shared, 300 * unit
            )
            base, coef, send, keep = results[:4]
            got = swap(send, 1)
            if index and member == 0:
                current_solution = results[4]
            elif index:
                norms.append(results[4])
        outs = [((half, rank), F32)] * (1 if last else 2)
        results = call(
            functools.partial(far_kernel, member, last),
            outs,
            [core, far_table, keep, got] + arrived,
            20 * unit,
        )
        mine = results[-1]
        if not last:
            chip = results[0]
        theirs = swap(mine, 1)
        member = 1 - member
        if not last:
            current = right_sides if member == 0 else current_solution
    solution = call(
        functools.partial(finish_kernel, leaves),
        [size],
        [core, u, down, base, mine, theirs],
        30 * unit,
    )[0]
    norm_table = jnp.concatenate(norms)
    norm_table = norm_table + swap(norm_table, 1)
    for stage in stages:
        norm_table = sum([swap(norm_table, mask) for mask in masks_of(stage)], norm_table)
    return solution, norm_table


def solution(mesh):
    placed = (
        P(("rows", "leaf"), None),
        P(None, ("rows", "leaf"), None, None),
        P(None, ("rows", "leaf"), None, None, None),
        P(None, ("rows", "leaf"), None, None, None),
        P(None, ("rows", "leaf"), None, None, None, None),
        P(),
    )
    return jax.shard_map(
        body,
        mesh=mesh,
        in_specs=placed,
        out_specs=(P(("rows", "leaf"), None), P()),
        check_vma=False,
    )
```

time: 356 us -> 209 us (0.59); the launches traced: 351 us -> 208 us
  matrix products: 120 us -> 0 us
  blocking collectives: 40.9 us -> 0 us
  Pallas kernels: 0 us -> 40.2 us
  waiting for transfers between devices: 65.8 us -> 46.1 us
  starting transfers between devices: 69.2 us -> 75.2 us
  local copies, waits for them, and re-layouts: 46.1 us -> 42.1 us
    dot_general x163 -> x0, matrix products: 120 us -> none  [the longest x28 20.8 us: apply_device(): jnp.dot(factor_table[2], sibling_list[height], precision=HIGHEST)]
    psum x1 -> x0, blocking collectives: 40.9 us -> none  [body(): norm_list.append(lax.psum(partial_norm, ('rows', 'leaf')))]
    pallas_call x0 -> x26, Pallas kernels: none -> 40.2 us  [call(): pl.pallas_call(kernel, out_shape=[jax.ShapeDtypeStruct(shape, dtype) for...]
    unnamed x168 -> x105, local copies, waits for them, and re-layouts: 10.8 us -> 32.4 us
    ppermute x63 -> x69, waiting for transfers between devices: 65.8 us -> 46.1 us  [swap(): return lax.ppermute(value, ('rows', 'leaf'), pairs)]
    reshape x8 -> x0, local copies, waits for them, and re-layouts: 12 us -> none  [the longest x7 9.47 us: sibling_of(): return shaped[:, ::-1].reshape(values.shape)]
    rev x7 -> x0, local copies, waits for them, and re-layouts: 9.08 us -> none  [sibling_of(): return shaped[:, ::-1].reshape(values.shape)]
    ppermute x63 -> x69, starting transfers between devices: 69.2 us -> 75.2 us  [swap(): return lax.ppermute(value, ('rows', 'leaf'), pairs)]
  transfers between devices with their start and end apart: 63 -> 69, of which waited for: 34 -> 35; matrix products, arithmetic and copies ran while one was open for 23% -> 7% of each run, Pallas kernels for 0% -> 8%
where the time goes in v1:
time: 209 us; the launch traced here: 208 us
  starting transfers between devices  75.2 us (36%)
  waiting for transfers between devices  46.1 us (22%)
  local copies, waits for them, and re-layouts  42.1 us (20%)
  Pallas kernels  40.2 us (19%)
  other arithmetic  2.79 us (1%)
    ppermute x69, starting transfers between devices, swap(): return lax.ppermute(value, ('rows', 'leaf'), pairs)  75.2 us
    ppermute x69, waiting for transfers between devices, swap(): return lax.ppermute(value, ('rows', 'leaf'), pairs)  46.1 us
    pallas_call x26, Pallas kernels, call(): pl.pallas_call(kernel, out_shape=[jax.ShapeDtypeStruct(shape, dtype) for...  40.2 us
    unnamed x105, local copies, waits for them, and re-layouts  32.4 us
  transfers between devices with their start and end apart: 69, of which 35 were waited for; matrix products, arithmetic and copies ran while one was open for 7% of the time, Pallas kernels for 8%

profile of v1, /device:TPU:0, one launch (start us, length us, event | category | flops | bytes accessed | tf_op | source)
XLA Modules:
  0.0 207.6 jit_solution(7447858446889712547)
XLA Ops:
  3.4 4.1 %collective-permute-start.5 = (f32[2,128,128]{2,1,0:T(8,128)}, f32[2,128,128]{2,1,0:T(8,128)}, u32[]{:S(2)}, u32[]{:S(2)}) collective-permute-start(f32[2,128,128]{2,1,0:T(8,128)} %get-tuple-element.112), channel_id=1, source_target_pairs={{0,16},{1,17},{2,18},{3,19},{4,20},{5,21},{6,22},{7,23},{8,24},{9,... | collective-permute-start | bytes 393224 | tf_op jit(solution)/shard_map/ppermute | solution.py:340
  8.8 3.1 %fusion.3 = (bf16[2,4,1,512,128]{4,3,2,1,0:T(8,128)(2,1)}, bf16[2,4,512,128]{3,2,1,0:T(8,128)(2,1)}) fusion(bf16[2,4,2,512,128]{4,3,2,1,0:T(8,128)(2,1)} %param.8), kind=kLoop, calls=%fused_computation.15 | loop fusion | bytes 4194304 | tf_op jit(solution)/shard_map/slice | solution.py:352
  21.1 6.3 %shard_map.78 = (bf16[2,2,512,640]{3,2,1,0:T(8,128)(2,1)S(1)}, bf16[2,2,512,128]{3,2,1,0:T(8,128)(2,1)S(1)}, bf16[2,2,512,128]{3,2,1,0:T(8,128)(2,1)S(1)}, f32[4,128,128]{2,1,0:T(8,128)}) custom-call(s32[1]{0:T(128)} %bitcast.core_ref.refs_0_, bf16[2,7,128,128]{3,2,1,0:T(8,128)(2,1)S(1)} %bitcast.44, bf16[2,7,2,128,128]{4,3,2,1,0:T(8,128)(2,1)S(1)} %slice.33.qc_ref, ...), custom_call_target="tpu_custom_call" | custom-call | flops 629145600 | tf_op jit(solution)/shard_map/pallas_call | solution.py:66
  38.7 2.2 %copy-done.1 = bf16[2,4,512,512]{3,2,1,0:T(8,128)(2,1)S(1)} copy-done((bf16[2,4,512,512]{3,2,1,0:T(8,128)(2,1)S(1)}, bf16[2,4,512,512]{3,2,1,0:T(8,128)(2,1)}, u32[]{:S(2)}) %copy-start.1) | copy-done | bytes 4194328
  47.6 2.8 %shard_map.79 = (f32[2048,128]{1,0:T(8,128)S(1)}, f32[512,128]{1,0:T(8,128)S(1)}, f32[192,128]{1,0:T(8,128)}, f32[64,128]{1,0:T(8,128)S(1)}) custom-call(s32[1]{0:T(128)} %bitcast.core_ref.refs_0_, bf16[2,4,512,512]{3,2,1,0:T(8,128)(2,1)S(1)} %copy-done.1, bf16[2,4,512,128]{3,2,1,0:T(8,128)(2,1)S(1)} %copy-done.9, bf16[2,4,128,512]{3,2,1,0:T(8,128)(2,1)S(1)} %bitcast.36, ...), custom_call_target="tpu_custom_call" | custom-call | flops 629145600 | tf_op jit(solution)/shard_map/pallas_call | solution.py:66
  55.4 2.8 %collective-permute-start.12 = (f32[64,128]{1,0:T(8,128)}, f32[64,128]{1,0:T(8,128)}, u32[]{:S(2)}, u32[]{:S(2)}) collective-permute-start(f32[64,128]{1,0:T(8,128)} %shard_map.82), channel_id=1, source_target_pairs={{0,16},{1,17},{2,18},{3,19},{4,20},{5,21},{6,22},{7,23},{8,24},{9,... | collective-permute-start | bytes 98312 | tf_op jit(solution)/shard_map/ppermute | solution.py:340
  60.2 1.9 copy.13.qct_ref
  66.6 2.7 %shard_map.80 = (bf16[2,2,768,256]{3,2,1,0:T(8,128)(2,1)S(1)}, bf16[2,2,128,128]{3,2,1,0:T(8,128)(2,1)S(1)}) custom-call(s32[1]{0:T(128)} %bitcast.core_ref.refs_0_, bf16[2,3,2,128,128]{4,3,2,1,0:T(8,128)(2,1)S(1)} %copy-done.23, bf16[2,128,128]{2,1,0:T(8,128)(2,1)S(1)} %bitcast.45, f32[4,128,128]{2,1,0:T(8,128)} %get-tuple-element.64.chip_ref, ...), custom_call_target="tpu_custom_call" | custom-call | flops 209715200 | tf_op jit(solution)/shard_map/pallas_call | solution.py:66
  74.9 2.2 %copy-done.2 = bf16[2,4,512,512]{3,2,1,0:T(8,128)(2,1)S(1)} copy-done((bf16[2,4,512,512]{3,2,1,0:T(8,128)(2,1)S(1)}, bf16[2,4,512,512]{3,2,1,0:T(8,128)(2,1)}, u32[]{:S(2)}) %copy-start.2) | copy-done | bytes 4194328
  81.6 4.5 %shard_map.84 = (f32[2048,128]{1,0:T(8,128)S(1)}, f32[512,128]{1,0:T(8,128)S(1)}, f32[192,128]{1,0:T(8,128)S(1)}, f32[64,128]{1,0:T(8,128)S(1)}, f32[2048,128]{1,0:T(8,128)S(1)}) custom-call(s32[1]{0:T(128)} %bitcast.core_ref.refs_0_, bf16[2,4,512,512]{3,2,1,0:T(8,128)(2,1)S(1)} %copy-done.2, bf16[2,4,512,128]{3,2,1,0:T(8,128)(2,1)S(1)} %copy-done.10, ...), custom_call_target="tpu_custom_call" | custom-call | flops 629145600 | tf_op jit(solution)/shard_map/pallas_call | solution.py:66
  90.9 2.4 %collective-permute-done.18.refs_3_.refs_2_ = f32[64,128]{1,0:T(8,128)S(1)} collective-permute-done((f32[64,128]{1,0:T(8,128)S(1)}, f32[64,128]{1,0:T(8,128)S(1)}, u32[]{:S(2)}, u32[]{:S(2)}) %collective-permute-start.18) | collective-permute-done | bytes 32800 | tf_op jit(solution)/shard_map/ppermute | solution.py:340
  93.5 3.0 %collective-permute-start.20 = (f32[64,128]{1,0:T(8,128)S(1)}, f32[64,128]{1,0:T(8,128)S(1)}, u32[]{:S(2)}, u32[]{:S(2)}) collective-permute-start(f32[64,128]{1,0:T(8,128)S(1)} %shard_map.85), channel_id=1, source_target_pairs={{0,16},{1,17},{2,18},{3,19},{4,20},{5,21},{6,22},{7,23},{8,24},{9,... | collective-permute-start | bytes 98312 | tf_op jit(solution)/shard_map/ppermute | solution.py:340
  98.4 3.8 %collective-permute-done.21.refs_5_ = f32[64,128]{1,0:T(8,128)S(1)} collective-permute-done((f32[64,128]{1,0:T(8,128)S(1)}, f32[64,128]{1,0:T(8,128)S(1)}, u32[]{:S(2)}, u32[]{:S(2)}) %collective-permute-start.21) | collective-permute-done | bytes 32800 | tf_op jit(solution)/shard_map/ppermute | solution.py:340
  104.0 2.9 %shard_map.87 = (f32[2048,128]{1,0:T(8,128)S(1)}, f32[512,128]{1,0:T(8,128)S(1)}, f32[192,128]{1,0:T(8,128)S(1)}, f32[64,128]{1,0:T(8,128)S(1)}, f32[1,128]{1,0:T(1,128)S(1)}) custom-call(s32[1]{0:T(128)} %bitcast.core_ref.refs_0_, bf16[2,4,512,512]{3,2,1,0:T(8,128)(2,1)S(1)} %copy-done.3, bf16[2,4,512,128]{3,2,1,0:T(8,128)(2,1)S(1)} %copy-done.10, ...), custom_call_target="tpu_custom_call" | custom-call | flops 629145600 | tf_op jit(solution)/shard_map/pallas_call | solution.py:66
  114.2 1.9 collective-permute-start.28
  116.1 2.5 %collective-permute-start.29 = (f32[64,128]{1,0:T(8,128)S(1)}, f32[64,128]{1,0:T(8,128)S(1)}, u32[]{:S(2)}, u32[]{:S(2)}) collective-permute-start(f32[64,128]{1,0:T(8,128)S(1)} %shard_map.88), channel_id=1, source_target_pairs={{0,24},{1,25},{2,26},{3,27},{4,28},{5,29},{6,30},{7,31},{8,16},{9,... | collective-permute-start | bytes 98312 | tf_op jit(solution)/shard_map/ppermute | solution.py:340
  119.3 2.5 %collective-permute-done.29.refs_5_ = f32[64,128]{1,0:T(8,128)S(1)} collective-permute-done((f32[64,128]{1,0:T(8,128)S(1)}, f32[64,128]{1,0:T(8,128)S(1)}, u32[]{:S(2)}, u32[]{:S(2)}) %collective-permute-start.29) | collective-permute-done | bytes 32800 | tf_op jit(solution)/shard_map/ppermute | solution.py:340
  123.4 3.5 %shard_map.90 = (f32[2048,128]{1,0:T(8,128)S(1)}, f32[512,128]{1,0:T(8,128)S(1)}, f32[192,128]{1,0:T(8,128)S(1)}, f32[64,128]{1,0:T(8,128)S(1)}, f32[2048,128]{1,0:T(8,128)S(1)}) custom-call(s32[1]{0:T(128)} %bitcast.core_ref.refs_0_, bf16[2,4,512,512]{3,2,1,0:T(8,128)(2,1)S(1)} %copy-done.3, bf16[2,4,512,128]{3,2,1,0:T(8,128)(2,1)S(1)} %copy-done.10, ...), custom_call_target="tpu_custom_call" | custom-call | flops 629145600 | tf_op jit(solution)/shard_map/pallas_call | solution.py:66
  131.6 2.4 %collective-permute-done.34.refs_3_.refs_2_ = f32[64,128]{1,0:T(8,128)S(1)} collective-permute-done((f32[64,128]{1,0:T(8,128)S(1)}, f32[64,128]{1,0:T(8,128)S(1)}, u32[]{:S(2)}, u32[]{:S(2)}) %collective-permute-start.34) | collective-permute-done | bytes 32800 | tf_op jit(solution)/shard_map/ppermute | solution.py:340
  134.2 3.0 %collective-permute-start.36 = (f32[64,128]{1,0:T(8,128)S(1)}, f32[64,128]{1,0:T(8,128)S(1)}, u32[]{:S(2)}, u32[]{:S(2)}) collective-permute-start(f32[64,128]{1,0:T(8,128)S(1)} %shard_map.91), channel_id=1, source_target_pairs={{0,16},{1,17},{2,18},{3,19},{4,20},{5,21},{6,22},{7,23},{8,24},{9,... | collective-permute-start | bytes 98312 | tf_op jit(solution)/shard_map/ppermute | solution.py:340
  139.1 3.8 %collective-permute-done.37.refs_5_ = f32[64,128]{1,0:T(8,128)S(1)} collective-permute-done((f32[64,128]{1,0:T(8,128)S(1)}, f32[64,128]{1,0:T(8,128)S(1)}, u32[]{:S(2)}, u32[]{:S(2)}) %collective-permute-start.37) | collective-permute-done | bytes 32800 | tf_op jit(solution)/shard_map/ppermute | solution.py:340
  144.6 2.9 %shard_map.93 = (f32[2048,128]{1,0:T(8,128)S(1)}, f32[512,128]{1,0:T(8,128)S(1)}, f32[192,128]{1,0:T(8,128)S(1)}, f32[64,128]{1,0:T(8,128)S(1)}, f32[1,128]{1,0:T(1,128)S(1)}) custom-call(s32[1]{0:T(128)} %bitcast.core_ref.refs_0_, bf16[2,4,512,512]{3,2,1,0:T(8,128)(2,1)S(1)} %copy-done.3, bf16[2,4,512,128]{3,2,1,0:T(8,128)(2,1)S(1)} %copy-done.10, ...), custom_call_target="tpu_custom_call" | custom-call | flops 629145600 | tf_op jit(solution)/shard_map/pallas_call | solution.py:66
  156.7 2.5 %collective-permute-start.45 = (f32[64,128]{1,0:T(8,128)S(1)}, f32[64,128]{1,0:T(8,128)S(1)}, u32[]{:S(2)}, u32[]{:S(2)}) collective-permute-start(f32[64,128]{1,0:T(8,128)S(1)} %shard_map.94), channel_id=1, source_target_pairs={{0,24},{1,25},{2,26},{3,27},{4,28},{5,29},{6,30},{7,31},{8,16},{9,... | collective-permute-start | bytes 98312 | tf_op jit(solution)/shard_map/ppermute | solution.py:340
  159.9 2.5 %collective-permute-done.45.refs_5_ = f32[64,128]{1,0:T(8,128)S(1)} collective-permute-done((f32[64,128]{1,0:T(8,128)S(1)}, f32[64,128]{1,0:T(8,128)S(1)}, u32[]{:S(2)}, u32[]{:S(2)}) %collective-permute-start.45) | collective-permute-done | bytes 32800 | tf_op jit(solution)/shard_map/ppermute | solution.py:340
  164.0 3.7 %shard_map.96 = (f32[2048,128]{1,0:T(8,128)S(1)}, f32[512,128]{1,0:T(8,128)S(1)}, f32[192,128]{1,0:T(8,128)S(1)}, f32[64,128]{1,0:T(8,128)S(1)}, f32[2048,128]{1,0:T(8,128)S(1)}) custom-call(s32[1]{0:T(128)} %bitcast.core_ref.refs_0_, bf16[2,4,512,512]{3,2,1,0:T(8,128)(2,1)S(1)} %copy-done.3, bf16[2,4,512,128]{3,2,1,0:T(8,128)(2,1)S(1)} %copy-done.10, ...), custom_call_target="tpu_custom_call" | custom-call | flops 629145600 | tf_op jit(solution)/shard_map/pallas_call | solution.py:66
  172.4 2.4 %collective-permute-done.50.refs_3_.refs_2_ = f32[64,128]{1,0:T(8,128)S(1)} collective-permute-done((f32[64,128]{1,0:T(8,128)S(1)}, f32[64,128]{1,0:T(8,128)S(1)}, u32[]{:S(2)}, u32[]{:S(2)}) %collective-permute-start.50) | collective-permute-done | bytes 32800 | tf_op jit(solution)/shard_map/ppermute | solution.py:340
  175.0 3.0 %collective-permute-start.52 = (f32[64,128]{1,0:T(8,128)S(1)}, f32[64,128]{1,0:T(8,128)S(1)}, u32[]{:S(2)}, u32[]{:S(2)}) collective-permute-start(f32[64,128]{1,0:T(8,128)S(1)} %shard_map.97), channel_id=1, source_target_pairs={{0,16},{1,17},{2,18},{3,19},{4,20},{5,21},{6,22},{7,23},{8,24},{9,... | collective-permute-start | bytes 98312 | tf_op jit(solution)/shard_map/ppermute | solution.py:340
  179.9 3.8 %collective-permute-done.53.refs_5_ = f32[64,128]{1,0:T(8,128)S(1)} collective-permute-done((f32[64,128]{1,0:T(8,128)S(1)}, f32[64,128]{1,0:T(8,128)S(1)}, u32[]{:S(2)}, u32[]{:S(2)}) %collective-permute-start.53) | collective-permute-done | bytes 32800 | tf_op jit(solution)/shard_map/ppermute | solution.py:340
  185.3 2.2 %shard_map.99 = (f32[2048,128]{1,0:T(8,128)S(1)}, f32[1,128]{1,0:T(1,128)S(1)}) custom-call(s32[1]{0:T(128)} %bitcast.core_ref.refs_0_, bf16[2,4,512,512]{3,2,1,0:T(8,128)(2,1)S(1)} %copy-done.3, bf16[2,4,512,128]{3,2,1,0:T(8,128)(2,1)S(1)} %copy-done.10, bf16[2,4,128,512]{3,2,1,0:T(8,128)(2,1)S(1)} %bitcast.42, bf16[2,2,256,512]{3,2,1,0:T(8,128)(2,1)S(1)} %copy-done.13, ...), custom_call_target="tpu_custom_call" | custom-call | flops 419430400 | tf_op jit(solution)/shard_map/pallas_call | solution.py:66
  195.1 1.9 collective-permute-start.59
  197.0 2.5 %collective-permute-start.60 = (f32[64,128]{1,0:T(8,128)S(1)}, f32[64,128]{1,0:T(8,128)S(1)}, u32[]{:S(2)}, u32[]{:S(2)}) collective-permute-start(f32[64,128]{1,0:T(8,128)S(1)} %shard_map.100), channel_id=1, source_target_pairs={{0,24},{1,25},{2,26},{3,27},{4,28},{5,29},{6,30},{7,31},{8,16},{9,... | collective-permute-start | bytes 98312 | tf_op jit(solution)/shard_map/ppermute | solution.py:340
  200.9 3.0 %collective-permute-start.66 = (f32[3,128]{1,0:T(4,128)S(1)}, f32[3,128]{1,0:T(4,128)S(1)}, u32[]{:S(2)}, u32[]{:S(2)}) collective-permute-start(f32[3,128]{1,0:T(4,128)S(1)} %add_add_fusion.1), channel_id=1, source_target_pairs={{0,8},{1,9},{2,10},{3,11},{4,12},{5,13},{6,14},{7,15},{8,0},{9,1},... | collective-permute-start | bytes 4616 | tf_op jit(solution)/shard_map/ppermute | solution.py:340
  (254 shorter events, 111.5 us)
Async XLA Ops:
  3.4 52.0 %collective-permute-start.5 = (f32[2,128,128]{2,1,0:T(8,128)}, f32[2,128,128]{2,1,0:T(8,128)}, u32[]{:S(2)}, u32[]{:S(2)}) collective-permute-start(f32[2,128,128]{2,1,0:T(8,128)} %get-tuple-element.112), channel_id=1, source_target_pairs={{0,16},{1,17},{2,18},{3,19},{4,20},{5,21},{6,22},{7,23},{8,24},{9,... | collective-permute-start | bytes 393224 | tf_op jit(solution)/shard_map/ppermute | solution.py:340
  7.4 50.8 %collective-permute-start.6 = (f32[2,128,128]{2,1,0:T(8,128)}, f32[2,128,128]{2,1,0:T(8,128)}, u32[]{:S(2)}, u32[]{:S(2)}) collective-permute-start(f32[2,128,128]{2,1,0:T(8,128)} %get-tuple-element.112), channel_id=1, source_target_pairs={{0,24},{1,25},{2,26},{3,27},{4,28},{5,29},{6,30},{7,31},{8,16},{9,... | collective-permute-start | bytes 393224 | tf_op jit(solution)/shard_map/ppermute | solution.py:340
  15.7 21.5 %collective-permute-start.3 = (f32[4,128,128]{2,1,0:T(8,128)}, f32[4,128,128]{2,1,0:T(8,128)S(1)}, u32[]{:S(2)}, u32[]{:S(2)}) collective-permute-start(f32[4,128,128]{2,1,0:T(8,128)} %bitcast.14), channel_id=1, source_target_pairs={{0,4},{1,5},{2,6},{3,7},{4,0},{5,1},{6,2},{7,3},{8,12},{9,13},{10,... | collective-permute-start | bytes 786440 | tf_op jit(solution)/shard_map/ppermute | solution.py:340
  17.1 12.0 %collective-permute-start.4 = (f32[2,128,128]{2,1,0:T(8,128)}, f32[2,128,128]{2,1,0:T(8,128)S(1)}, u32[]{:S(2)}, u32[]{:S(2)}) collective-permute-start(f32[2,128,128]{2,1,0:T(8,128)} %get-tuple-element.113), channel_id=1, source_target_pairs={{0,6},{1,7},{2,4},{3,5},{4,2},{5,3},{6,0},{7,1},{8,14},{9,15},{10,... | collective-permute-start | bytes 393224 | tf_op jit(solution)/shard_map/ppermute | solution.py:340
  19.4 11.9 %collective-permute-start.7 = (f32[64,128]{1,0:T(8,128)}, f32[64,128]{1,0:T(8,128)S(1)}, u32[]{:S(2)}, u32[]{:S(2)}) collective-permute-start(f32[64,128]{1,0:T(8,128)} %slice_add_fusion.refs_0_), channel_id=1, source_target_pairs={{0,2},{1,3},{2,0},{3,1},{4,6},{5,7},{6,4},{7,5},{8,10},{9,11},{10,... | collective-permute-start | bytes 98312 | tf_op jit(solution)/shard_map/ppermute | solution.py:340
  29.8 5.3 %collective-permute-start.10 = (f32[2,128,128]{2,1,0:T(8,128)}, f32[2,128,128]{2,1,0:T(8,128)S(1)}, u32[]{:S(2)}, u32[]{:S(2)}) collective-permute-start(f32[2,128,128]{2,1,0:T(8,128)} %get-tuple-element.113), channel_id=1, source_target_pairs={{0,2},{1,3},{2,0},{3,1},{4,6},{5,7},{6,4},{7,5},{8,10},{9,11},{10,... | collective-permute-start | bytes 393224 | tf_op jit(solution)/shard_map/ppermute | solution.py:340
  31.3 32.4 %collective-permute-start.2 = (f32[4,128,128]{2,1,0:T(8,128)}, f32[4,128,128]{2,1,0:T(8,128)}, u32[]{:S(2)}, u32[]{:S(2)}) collective-permute-start(f32[4,128,128]{2,1,0:T(8,128)} %get-tuple-element.64.chip_ref), channel_id=1, source_target_pairs={{0,1},{1,0},{2,3},{3,2},{4,5},{5,4},{6,7},{7,6},{8,9},{9,8},{10,11... | collective-permute-start | bytes 786440 | tf_op jit(solution)/shard_map/ppermute | solution.py:340
  35.7 17.0 %collective-permute-start.8 = (f32[64,128]{1,0:T(8,128)}, f32[64,128]{1,0:T(8,128)S(1)}, u32[]{:S(2)}, u32[]{:S(2)}) collective-permute-start(f32[64,128]{1,0:T(8,128)} %slice_add_fusion.refs_0_), channel_id=1, source_target_pairs={{0,4},{1,5},{2,6},{3,7},{4,0},{5,1},{6,2},{7,3},{8,12},{9,13},{10,... | collective-permute-start | bytes 98312 | tf_op jit(solution)/shard_map/ppermute | solution.py:340
  37.2 15.6 %collective-permute-start.9 = (f32[64,128]{1,0:T(8,128)}, f32[64,128]{1,0:T(8,128)S(1)}, u32[]{:S(2)}, u32[]{:S(2)}) collective-permute-start(f32[64,128]{1,0:T(8,128)} %slice_add_fusion.refs_0_), channel_id=1, source_target_pairs={{0,6},{1,7},{2,4},{3,5},{4,2},{5,3},{6,0},{7,1},{8,14},{9,15},{10,... | collective-permute-start | bytes 98312 | tf_op jit(solution)/shard_map/ppermute | solution.py:340
  52.8 16.6 %collective-permute-start.1 = (f32[192,128]{1,0:T(8,128)}, f32[192,128]{1,0:T(8,128)}, u32[]{:S(2)}, u32[]{:S(2)}) collective-permute-start(f32[192,128]{1,0:T(8,128)} %get-tuple-element.62), channel_id=1, source_target_pairs={{0,1},{1,0},{2,3},{3,2},{4,5},{5,4},{6,7},{7,6},{8,9},{9,8},{10,11... | collective-permute-start | bytes 294920 | tf_op jit(solution)/shard_map/ppermute | solution.py:340
  55.1 14.2 %collective-permute-start.11 = (f32[64,128]{1,0:T(8,128)}, f32[64,128]{1,0:T(8,128)}, u32[]{:S(2)}, u32[]{:S(2)}) collective-permute-start(f32[64,128]{1,0:T(8,128)} %shard_map.82), channel_id=1, source_target_pairs={{0,8},{1,9},{2,10},{3,11},{4,12},{5,13},{6,14},{7,15},{8,0},{9,1},... | collective-permute-start | bytes 98312 | tf_op jit(solution)/shard_map/ppermute | solution.py:340
  55.4 14.0 %collective-permute-start.12 = (f32[64,128]{1,0:T(8,128)}, f32[64,128]{1,0:T(8,128)}, u32[]{:S(2)}, u32[]{:S(2)}) collective-permute-start(f32[64,128]{1,0:T(8,128)} %shard_map.82), channel_id=1, source_target_pairs={{0,16},{1,17},{2,18},{3,19},{4,20},{5,21},{6,22},{7,23},{8,24},{9,... | collective-permute-start | bytes 98312 | tf_op jit(solution)/shard_map/ppermute | solution.py:340
  58.2 11.2 %collective-permute-start.13 = (f32[64,128]{1,0:T(8,128)}, f32[64,128]{1,0:T(8,128)}, u32[]{:S(2)}, u32[]{:S(2)}) collective-permute-start(f32[64,128]{1,0:T(8,128)} %shard_map.82), channel_id=1, source_target_pairs={{0,24},{1,25},{2,26},{3,27},{4,28},{5,29},{6,30},{7,31},{8,16},{9,... | collective-permute-start | bytes 98312 | tf_op jit(solution)/shard_map/ppermute | solution.py:340
  86.2 16.0 %collective-permute-start.15 = (f32[192,128]{1,0:T(8,128)S(1)}, f32[192,128]{1,0:T(8,128)S(1)}, u32[]{:S(2)}, u32[]{:S(2)}) collective-permute-start(f32[192,128]{1,0:T(8,128)S(1)} %get-tuple-element.73), channel_id=1, source_target_pairs={{0,1},{1,0},{2,3},{3,2},{4,5},{5,4},{6,7},{7,6},{8,9},{9,8},{10,11... | collective-permute-start | bytes 294920 | tf_op jit(solution)/shard_map/ppermute | solution.py:340
  96.5 5.7 %collective-permute-start.21 = (f32[64,128]{1,0:T(8,128)S(1)}, f32[64,128]{1,0:T(8,128)S(1)}, u32[]{:S(2)}, u32[]{:S(2)}) collective-permute-start(f32[64,128]{1,0:T(8,128)S(1)} %shard_map.85), channel_id=1, source_target_pairs={{0,24},{1,25},{2,26},{3,27},{4,28},{5,29},{6,30},{7,31},{8,16},{9,... | collective-permute-start | bytes 98312 | tf_op jit(solution)/shard_map/ppermute | solution.py:340
  106.9 14.9 %collective-permute-start.23 = (f32[192,128]{1,0:T(8,128)S(1)}, f32[192,128]{1,0:T(8,128)S(1)}, u32[]{:S(2)}, u32[]{:S(2)}) collective-permute-start(f32[192,128]{1,0:T(8,128)S(1)} %get-tuple-element.79), channel_id=1, source_target_pairs={{0,1},{1,0},{2,3},{3,2},{4,5},{5,4},{6,7},{7,6},{8,9},{9,8},{10,11... | collective-permute-start | bytes 294920 | tf_op jit(solution)/shard_map/ppermute | solution.py:340
  116.1 5.7 %collective-permute-start.29 = (f32[64,128]{1,0:T(8,128)S(1)}, f32[64,128]{1,0:T(8,128)S(1)}, u32[]{:S(2)}, u32[]{:S(2)}) collective-permute-start(f32[64,128]{1,0:T(8,128)S(1)} %shard_map.88), channel_id=1, source_target_pairs={{0,24},{1,25},{2,26},{3,27},{4,28},{5,29},{6,30},{7,31},{8,16},{9,... | collective-permute-start | bytes 98312 | tf_op jit(solution)/shard_map/ppermute | solution.py:340
  127.0 16.0 %collective-permute-start.31 = (f32[192,128]{1,0:T(8,128)S(1)}, f32[192,128]{1,0:T(8,128)S(1)}, u32[]{:S(2)}, u32[]{:S(2)}) collective-permute-start(f32[192,128]{1,0:T(8,128)S(1)} %get-tuple-element.86), channel_id=1, source_target_pairs={{0,1},{1,0},{2,3},{3,2},{4,5},{5,4},{6,7},{7,6},{8,9},{9,8},{10,11... | collective-permute-start | bytes 294920 | tf_op jit(solution)/shard_map/ppermute | solution.py:340
  137.2 5.7 %collective-permute-start.37 = (f32[64,128]{1,0:T(8,128)S(1)}, f32[64,128]{1,0:T(8,128)S(1)}, u32[]{:S(2)}, u32[]{:S(2)}) collective-permute-start(f32[64,128]{1,0:T(8,128)S(1)} %shard_map.91), channel_id=1, source_target_pairs={{0,24},{1,25},{2,26},{3,27},{4,28},{5,29},{6,30},{7,31},{8,16},{9,... | collective-permute-start | bytes 98312 | tf_op jit(solution)/shard_map/ppermute | solution.py:340
  147.5 14.9 %collective-permute-start.39 = (f32[192,128]{1,0:T(8,128)S(1)}, f32[192,128]{1,0:T(8,128)S(1)}, u32[]{:S(2)}, u32[]{:S(2)}) collective-permute-start(f32[192,128]{1,0:T(8,128)S(1)} %get-tuple-element.92), channel_id=1, source_target_pairs={{0,1},{1,0},{2,3},{3,2},{4,5},{5,4},{6,7},{7,6},{8,9},{9,8},{10,11... | collective-permute-start | bytes 294920 | tf_op jit(solution)/shard_map/ppermute | solution.py:340
  156.7 5.7 %collective-permute-start.45 = (f32[64,128]{1,0:T(8,128)S(1)}, f32[64,128]{1,0:T(8,128)S(1)}, u32[]{:S(2)}, u32[]{:S(2)}) collective-permute-start(f32[64,128]{1,0:T(8,128)S(1)} %shard_map.94), channel_id=1, source_target_pairs={{0,24},{1,25},{2,26},{3,27},{4,28},{5,29},{6,30},{7,31},{8,16},{9,... | collective-permute-start | bytes 98312 | tf_op jit(solution)/shard_map/ppermute | solution.py:340
  167.7 16.0 %collective-permute-start.47 = (f32[192,128]{1,0:T(8,128)S(1)}, f32[192,128]{1,0:T(8,128)S(1)}, u32[]{:S(2)}, u32[]{:S(2)}) collective-permute-start(f32[192,128]{1,0:T(8,128)S(1)} %get-tuple-element.99), channel_id=1, source_target_pairs={{0,1},{1,0},{2,3},{3,2},{4,5},{5,4},{6,7},{7,6},{8,9},{9,8},{10,11... | collective-permute-start | bytes 294920 | tf_op jit(solution)/shard_map/ppermute | solution.py:340
  178.0 5.7 %collective-permute-start.53 = (f32[64,128]{1,0:T(8,128)S(1)}, f32[64,128]{1,0:T(8,128)S(1)}, u32[]{:S(2)}, u32[]{:S(2)}) collective-permute-start(f32[64,128]{1,0:T(8,128)S(1)} %shard_map.97), channel_id=1, source_target_pairs={{0,24},{1,25},{2,26},{3,27},{4,28},{5,29},{6,30},{7,31},{8,16},{9,... | collective-permute-start | bytes 98312 | tf_op jit(solution)/shard_map/ppermute | solution.py:340
  187.8 6.6 %collective-permute-start.55 = (f32[64,128]{1,0:T(8,128)S(1)}, f32[64,128]{1,0:T(8,128)S(1)}, u32[]{:S(2)}, u32[]{:S(2)}) collective-permute-start(f32[64,128]{1,0:T(8,128)S(1)} %get-tuple-element.104.refs_0_), channel_id=1, source_target_pairs={{0,2},{1,3},{2,0},{3,1},{4,6},{5,7},{6,4},{7,5},{8,10},{9,11},{10,... | collective-permute-start | bytes 98312 | tf_op jit(solution)/shard_map/ppermute | solution.py:340
  189.3 5.5 %collective-permute-start.56 = (f32[64,128]{1,0:T(8,128)S(1)}, f32[64,128]{1,0:T(8,128)S(1)}, u32[]{:S(2)}, u32[]{:S(2)}) collective-permute-start(f32[64,128]{1,0:T(8,128)S(1)} %get-tuple-element.104.refs_0_), channel_id=1, source_target_pairs={{0,4},{1,5},{2,6},{3,7},{4,0},{5,1},{6,2},{7,3},{8,12},{9,13},{10,... | collective-permute-start | bytes 98312 | tf_op jit(solution)/shard_map/ppermute | solution.py:340
  191.3 5.7 %collective-permute-start.65 = (f32[3,128]{1,0:T(4,128)S(1)}, f32[3,128]{1,0:T(4,128)S(1)}, u32[]{:S(2)}, u32[]{:S(2)}) collective-permute-start(f32[3,128]{1,0:T(4,128)S(1)} %fusion.2), channel_id=1, source_target_pairs={{0,6},{1,7},{2,4},{3,5},{4,2},{5,3},{6,0},{7,1},{8,14},{9,15},{10,... | collective-permute-start | bytes 4616 | tf_op jit(solution)/shard_map/ppermute | solution.py:340
  192.8 6.6 %collective-permute-start.64 = (f32[3,128]{1,0:T(4,128)S(1)}, f32[3,128]{1,0:T(4,128)S(1)}, u32[]{:S(2)}, u32[]{:S(2)}) collective-permute-start(f32[3,128]{1,0:T(4,128)S(1)} %fusion.2), channel_id=1, source_target_pairs={{0,4},{1,5},{2,6},{3,7},{4,0},{5,1},{6,2},{7,3},{8,12},{9,13},{10,... | collective-permute-start | bytes 4616 | tf_op jit(solution)/shard_map/ppermute | solution.py:340
  194.3 5.1 %collective-permute-start.63 = (f32[3,128]{1,0:T(4,128)S(1)}, f32[3,128]{1,0:T(4,128)S(1)}, u32[]{:S(2)}, u32[]{:S(2)}) collective-permute-start(f32[3,128]{1,0:T(4,128)S(1)} %fusion.2), channel_id=1, source_target_pairs={{0,2},{1,3},{2,0},{3,1},{4,6},{5,7},{6,4},{7,5},{8,10},{9,11},{10,... | collective-permute-start | bytes 4616 | tf_op jit(solution)/shard_map/ppermute | solution.py:340
  195.0 5.9 %collective-permute-start.58 = (f32[64,128]{1,0:T(8,128)S(1)}, f32[64,128]{1,0:T(8,128)S(1)}, u32[]{:S(2)}, u32[]{:S(2)}) collective-permute-start(f32[64,128]{1,0:T(8,128)S(1)} %shard_map.100), channel_id=1, source_target_pairs={{0,8},{1,9},{2,10},{3,11},{4,12},{5,13},{6,14},{7,15},{8,0},{9,1},... | collective-permute-start | bytes 98312 | tf_op jit(solution)/shard_map/ppermute | solution.py:340
  195.1 8.9 %collective-permute-start.59 = (f32[64,128]{1,0:T(8,128)S(1)}, f32[64,128]{1,0:T(8,128)S(1)}, u32[]{:S(2)}, u32[]{:S(2)}) collective-permute-start(f32[64,128]{1,0:T(8,128)S(1)} %shard_map.100), channel_id=1, source_target_pairs={{0,16},{1,17},{2,18},{3,19},{4,20},{5,21},{6,22},{7,23},{8,24},{9,... | collective-permute-start | bytes 98312 | tf_op jit(solution)/shard_map/ppermute | solution.py:340
  197.0 7.0 %collective-permute-start.60 = (f32[64,128]{1,0:T(8,128)S(1)}, f32[64,128]{1,0:T(8,128)S(1)}, u32[]{:S(2)}, u32[]{:S(2)}) collective-permute-start(f32[64,128]{1,0:T(8,128)S(1)} %shard_map.100), channel_id=1, source_target_pairs={{0,24},{1,25},{2,26},{3,27},{4,28},{5,29},{6,30},{7,31},{8,16},{9,... | collective-permute-start | bytes 98312 | tf_op jit(solution)/shard_map/ppermute | solution.py:340
  199.5 5.4 %collective-permute-start.68 = (f32[3,128]{1,0:T(4,128)S(1)}, f32[3,128]{1,0:T(4,128)S(1)}, u32[]{:S(2)}, u32[]{:S(2)}) collective-permute-start(f32[3,128]{1,0:T(4,128)S(1)} %add_add_fusion.1), channel_id=1, source_target_pairs={{0,24},{1,25},{2,26},{3,27},{4,28},{5,29},{6,30},{7,31},{8,16},{9,... | collective-permute-start | bytes 4616 | tf_op jit(solution)/shard_map/ppermute | solution.py:340
  (89 other events, 403.9 us)

commit v2 on v1

v2 whole, which is shorter than its diff:
```python
import functools

import jax
import jax.numpy as jnp
from jax import lax
from jax.experimental import pallas as pl
from jax.experimental.pallas import tpu as pltpu
from jax.sharding import PartitionSpec as P


STEPS = 3
BF16 = jnp.bfloat16
F32 = jnp.float32
VMEM_LIMIT = 16 * 2**20
START_LIMIT = 50 * 2**20


def mm(left, right):
    return jnp.dot(left, right, preferred_element_type=F32)


def pieces(value):
    high = value.astype(BF16)
    return high, (value - high.astype(F32)).astype(BF16)


def left_mul(table, value):
    high, low = pieces(value)
    width = value.shape[1]
    both = mm(table[0], jnp.concatenate([high, low], axis=1))
    return both[:, :width] + both[:, width:] + mm(table[1], high)


def right_mul(value, table):
    high, low = pieces(value)
    rows = value.shape[0]
    both = mm(jnp.concatenate([high, low], axis=0), table[0])
    return both[:rows] + both[rows:] + mm(high, table[1])


def mul(left, right):
    return left_mul(pieces(left), right)


def exact_left(table, value):
    high, low = pieces(value)
    width = value.shape[1]
    both = mm(table, jnp.concatenate([high, low], axis=1))
    return both[:, :width] + both[:, width:]


def exact_right(value, table):
    high, low = pieces(value)
    rows = value.shape[0]
    both = mm(jnp.concatenate([high, low], axis=0), table)
    return both[:rows] + both[rows:]


def put(ref, index, value):
    high, low = pieces(value)
    ref[(0,) + index] = high
    ref[(1,) + index] = low


def call(kernel, outs, args, flops, hbm=False, scratch=()):
    specs = [pl.BlockSpec(memory_space=pltpu.HBM if hbm else pltpu.VMEM)] * len(args)
    return pl.pallas_call(
        kernel,
        out_shape=[jax.ShapeDtypeStruct(shape, dtype) for shape, dtype in outs],
        in_specs=specs,
        out_specs=[pl.BlockSpec(memory_space=pltpu.VMEM)] * len(outs),
        scratch_shapes=list(scratch),
        compiler_params=pltpu.CompilerParams(vmem_limit_bytes=START_LIMIT if hbm else VMEM_LIMIT),
        cost_estimate=pl.CostEstimate(flops=flops, bytes_accessed=0, transcendentals=0),
    )(*args)


def level_offsets(leaf_count):
    offsets, count, offset = [], leaf_count, 0
    while count >= 1:
        offsets.append(offset)
        offset += count
        count //= 2
    return offsets


def send_parts(device, lifted, send_ref, keep_ref):
    columns = lifted.shape[1]
    half = columns // 2
    turned = lifted.T
    first = lax.axis_index("leaf") % 2 == 0
    keep_ref[...] = jnp.where(first, turned[:half], turned[half:])
    send_ref[: device.shape[0]] = device
    send_ref[device.shape[0] :] = jnp.where(first, turned[half:], turned[:half])


def start_kernel(leaves, *refs):
    right_hbm, near_hbm, bases_hbm, local_hbm, upper_hbm, top_hbm = refs[:6]
    right_ref, near_ref, bases_ref, local_ref, upper_ref, top_ref = refs[6:12]
    vt_ref, up_ref, coef_ref, send_ref, keep_ref, semaphores = refs[12:]
    position = lax.axis_index("rows") // (lax.axis_size("rows") // 2)
    copies = [
        pltpu.make_async_copy(source, target, semaphores.at[index])
        for index, (source, target) in enumerate(
            [
                (local_hbm, local_ref),
                (bases_hbm, bases_ref),
                (right_hbm, right_ref),
                (upper_hbm.at[:, 0], upper_ref),
                (top_hbm.at[:, position], top_ref),
                (near_hbm, near_ref),
            ]
        )
    ]
    for copy in copies:
        copy.start()
    copies[0].wait()
    rank = local_ref.shape[-1]
    up_table(1, leaves, local_ref, up_ref)
    copies[1].wait()
    copies[2].wait()
    rows = right_ref.shape[0] // leaves
    for leaf in range(leaves):
        turned = bases_ref[1, leaf, 1].T
        vt_ref[leaf] = turned
        value = right_ref[leaf * rows : (leaf + 1) * rows].astype(BF16)
        coef_ref[leaf * rank : (leaf + 1) * rank] = mm(turned, value)
    lifted = left_mul((up_ref[0], up_ref[1]), coef_ref[...])
    send_parts(lifted[:rank], lifted[rank:], send_ref, keep_ref)
    for copy in copies[3:]:
        copy.wait()


def up_table(member, leaves, local_ref, up_ref):
    rank = local_ref.shape[-1]
    offsets = level_offsets(leaves)
    turned = {}

    def transfer(node):
        if node not in turned:
            turned[node] = local_ref[member, node, 0].T
        return turned[node]

    for leaf in range(leaves):
        trail = transfer(leaf).astype(F32)
        for depth in range(1, len(offsets)):
            if depth == len(offsets) - 1:
                put(up_ref, (slice(0, rank), pl.ds(leaf * rank, rank)), trail)
            trail = exact_left(transfer(offsets[depth] + (leaf >> depth)), trail)
        put(up_ref, (slice(rank, 2 * rank), pl.ds(leaf * rank, rank)), trail)


def pack_kernel(base, last, upper_ref, *refs):
    near_ref, far_ref, cross_ref = refs[-3:]
    half = near_ref.shape[0] if last else near_ref.shape[0] - 2 * upper_ref.shape[-1]
    rank = upper_ref.shape[-1]
    value = refs[0][...]
    if len(refs) == 5:
        value = value + refs[1][rank:]
    for ref in (near_ref, far_ref, cross_ref):
        ref[:half] = value
    for member in range(2):
        lower = upper_ref[member, base, 0].astype(F32)
        rows = pl.ds(half + member * rank, rank)
        far_ref[rows] = lower
        cross_ref[rows] = lower
        if not last:
            near_ref[rows] = lower
            far_ref[pl.ds(half + (2 + member) * rank, rank)] = upper_ref[
                member, base + 1, 0
            ].astype(F32)


def stage_table_kernel(base, upper_ref, near_ref, far_ref, cross_ref, out_ref):
    rank = upper_ref.shape[-1]
    half = near_ref.shape[0] - 2 * rank
    for member in range(2):
        rows = pl.ds(half + member * rank, rank)
        here = upper_ref[member, base + 1, 0]
        there = far_ref[pl.ds(half + (2 + member) * rank, rank)].astype(BF16)
        lowers = [upper_ref[member, base, 0]]
        lowers += [ref[rows].astype(BF16) for ref in (near_ref, far_ref, cross_ref)]
        for index, (lower, upper) in enumerate(zip(lowers, (here, here, there, there))):
            put(out_ref, (member, pl.ds(index * rank, rank)), mm(lower, upper))


def local_table_kernel(leaves, local_ref, bases_ref, vt1_ref, up1_ref, *refs):
    vt0_ref, up0_ref, wide_ref, down_ref, feed_ref, chip_ref = refs
    vt_refs, up_refs = (vt0_ref, vt1_ref), (up0_ref, up1_ref)
    rank = local_ref.shape[-1]
    offsets = level_offsets(leaves)
    own = offsets[-1]
    up_table(0, leaves, local_ref, up0_ref)
    for leaf in range(leaves):
        vt0_ref[leaf] = bases_ref[0, leaf, 1].T
    for member in (1, 0):
        other = 1 - member
        sign = 1.0 if member == 1 else -1.0
        total = None
        turned = {}

        def transfer(node):
            if node not in turned:
                turned[node] = local_ref[member, node, 0].T
            return turned[node]

        for leaf in range(leaves):
            rows = pl.ds(leaf * rank, rank)
            trail = None
            for depth in range(len(offsets) - 1):
                node = leaf >> depth
                step = local_ref[member, offsets[depth] + node, 1]
                coupling = local_ref[member, offsets[depth] + node, 2]
                coupled = coupling.astype(F32) if trail is None else exact_right(trail, coupling)
                for peer in range(leaves):
                    if peer >> depth != node ^ 1:
                        continue
                    entry = coupled
                    for lower in range(depth - 1, -1, -1):
                        entry = exact_right(entry, transfer(offsets[lower] + (peer >> lower)))
                    put(wide_ref, (member, rows, pl.ds((1 + peer) * rank, rank)), entry)
                trail = step.astype(F32) if trail is None else exact_right(trail, step)
            put(
                wide_ref,
                (member, rows, pl.ds((1 + leaf) * rank, rank)),
                jnp.zeros((rank, rank), F32),
            )
            put(
                wide_ref,
                (member, rows, pl.ds(0, rank)),
                exact_right(trail, local_ref[member, own, 2]),
            )
            below = exact_right(trail, local_ref[member, own, 1])
            put(down_ref, (member, rows), below)
            feed = sign * mul(mm(vt_refs[other][leaf], bases_ref[member, leaf, 0]), below)
            put(feed_ref, (member, rows), feed)
            table = tuple(
                up_refs[other][piece, :, pl.ds(leaf * rank, rank)] for piece in range(2)
            )
            term = left_mul(table, feed)
            total = term if total is None else total + term
        chip_ref[2 * member] = total[:rank]
        chip_ref[2 * member + 1] = total[rank:].T


def far_table_kernel(plan, half, upper_ref, top_ref, chip_ref, got_ref, *refs):
    lower_refs, (far_ref, sibling_ref) = refs[:-2], refs[-2:]
    rank = top_ref.shape[-1]
    for member in range(2):
        put(sibling_ref, (member,), got_ref[2 * member])
        loop = pieces(chip_ref[2 * member + 1] + got_ref[2 * member + 1])
        trail = None
        couplings = []
        levels = upper_ref.shape[1] + 1
        for level in range(levels):
            coupling = top_ref[member] if level == levels - 1 else upper_ref[member, level, 2]
            coupling = coupling.T
            couplings.append(
                coupling.astype(F32) if trail is None else exact_left(coupling, trail)
            )
            if level < levels - 1:
                step = upper_ref[member, level, 1].T
                trail = step.astype(F32) if trail is None else exact_left(step, trail)
        for index, (level, lower) in enumerate(plan):
            weight = couplings[level]
            if lower is not None:
                transfer = lower_refs[lower][pl.ds(half + member * rank, rank)]
                weight = exact_left(transfer.astype(BF16), weight)
            rows = pl.ds(index * rank, rank)
            put(far_ref, (member, rows, slice(0, rank)), right_mul(weight, loop))
            put(far_ref, (member, rows, slice(rank, 2 * rank)), weight)


def stage_kernel(member, half, table_ref, *refs):
    rank = table_ref.shape[-1]
    total = None
    for index in range(4):
        rows = pl.ds(index * rank, rank)
        table = (table_ref[0, member, rows], table_ref[1, member, rows])
        term = right_mul(refs[index][:half], table)
        total = term if total is None else total + term
    refs[-1][:half] = total
    if len(refs) > 5:
        refs[-1][half:] = refs[4][...] + refs[5][...]


def far_kernel(member, last, table_ref, keep_ref, got_ref, *refs):
    rank = table_ref.shape[-1] // 2
    half = refs[-1].shape[0]
    count = len(refs) - 2
    total = None
    for index in range(count):
        rows = pl.ds(index * rank, rank)
        table = (table_ref[0, member, rows], table_ref[1, member, rows])
        term = right_mul(refs[index][:half], table)
        total = term if total is None else total + term
    if not last:
        refs[count][...] = keep_ref[...] + got_ref[rank:] + total[:, :rank]
    else:
        sums = None
        for ref in refs[:count]:
            if ref.shape[0] == half + 8:
                sums = ref[half:] if sums is None else sums + ref[half:]
        refs[count][...] = sums
    refs[-1][...] = total[:, rank:]


def far_rows(mine_ref, theirs_ref):
    mine, theirs = mine_ref[...], theirs_ref[...]
    first = lax.axis_index("leaf") % 2 == 0
    return jnp.concatenate(
        [jnp.where(first, mine, theirs), jnp.where(first, theirs, mine)], axis=0
    ).T


def expand(member, base, far):
    if member == 0:
        return exact_left(base, far)
    return mm(base, far.astype(BF16))


def local_kernel(member, leaves, first, *refs):
    refs = list(refs)
    near_ref, bases_ref, vt_ref, up_ref, wide_ref = (refs.pop(0) for _ in range(5))
    base_ref, other_ref, coef_ref, got_ref = (refs.pop(0) for _ in range(4))
    other = 1 - member
    rank = up_ref.shape[-1] // leaves
    rows = base_ref.shape[0] // leaves
    if first:
        coef = coef_ref[...]
        sibling = got_ref[:rank]
    else:
        down_ref, feed_ref, sibling_ref, mine_ref, theirs_ref = (refs.pop(0) for _ in range(5))
        far = far_rows(mine_ref, theirs_ref)
        coef = coef_ref[...] + left_mul((feed_ref[0, other], feed_ref[1, other]), far)
        sibling = got_ref[:rank] + left_mul((sibling_ref[0, other], sibling_ref[1, other]), far)
        leaf_far = left_mul((down_ref[0, other], down_ref[1, other]), far)
    out_ref, next_ref, send_ref, keep_ref = refs[:4]
    table = (wide_ref[0, member], wide_ref[1, member])
    inner = left_mul(table, jnp.concatenate([sibling, coef], axis=0))
    norm = None
    for leaf in range(leaves):
        part = slice(leaf * rows, (leaf + 1) * rows)
        small = slice(leaf * rank, (leaf + 1) * rank)
        value = base_ref[part]
        if not first:
            moved = expand(other, bases_ref[other, leaf, 0], leaf_far[small])
            value = value + moved if other == 1 else value - moved
            if other == 1:
                refs[4][part] = value
            else:
                term = jnp.sum(value * value, axis=0, keepdims=True)
                norm = term if norm is None else norm + term
        near = near_ref[member, leaf]
        if member == 0:
            result = exact_left(near, value)
        else:
            result = mm(near, value.astype(BF16))
        result = result + expand(member, bases_ref[member, leaf, 0], inner[small])
        if member == 0:
            result = other_ref[part] - result
        elif not first:
            result = other_ref[part] + result
        out_ref[part] = result
        if other == 0:
            next_ref[small] = exact_left(vt_ref[leaf], result)
        else:
            next_ref[small] = mm(vt_ref[leaf], result.astype(BF16))
    if norm is not None:
        refs[4][...] = norm
    lifted = left_mul((up_ref[0], up_ref[1]), next_ref[...])
    send_parts(lifted[:rank], lifted[rank:], send_ref, keep_ref)


def last_local_kernel(leaves, near_ref, bases_ref, vt_ref, up_ref, wide_ref, *refs):
    member, other = 1, 0
    base_ref, other_ref, coef_ref, got_ref = refs[:4]
    down_ref, feed_ref, sibling_ref, mine_ref, theirs_ref = refs[4:9]
    *old_refs, out_ref, norm_ref = refs[9:]
    rank = up_ref.shape[-1] // leaves
    rows = base_ref.shape[0] // leaves
    far = far_rows(mine_ref, theirs_ref)
    coef = coef_ref[...] + left_mul((feed_ref[0, other], feed_ref[1, other]), far)
    sibling = got_ref[:rank] + left_mul((sibling_ref[0, other], sibling_ref[1, other]), far)
    leaf_far = left_mul((down_ref[0, other], down_ref[1, other]), far)
    table = (wide_ref[0, member], wide_ref[1, member])
    inner = left_mul(table, jnp.concatenate([sibling, coef], axis=0))
    norm = None
    for leaf in range(leaves):
        part = slice(leaf * rows, (leaf + 1) * rows)
        small = slice(leaf * rank, (leaf + 1) * rank)
        value = base_ref[part] - expand(other, bases_ref[other, leaf, 0], leaf_far[small])
        term = jnp.sum(value * value, axis=0, keepdims=True)
        norm = term if norm is None else norm + term
        result = mm(near_ref[member, leaf], value.astype(BF16))
        result = result + expand(member, bases_ref[member, leaf, 0], inner[small])
        out_ref[part] = other_ref[part] + result
    norm_ref[...] = jnp.zeros_like(norm_ref)
    for index, ref in enumerate(old_refs):
        norm_ref[index : index + 1] = ref[...]
    norm_ref[len(old_refs) : len(old_refs) + 1] = norm


def finish_kernel(leaves, bases_ref, down_ref, base_ref, mine_ref, theirs_ref, out_ref):
    rank = down_ref.shape[-1]
    rows = base_ref.shape[0] // leaves
    far = far_rows(mine_ref, theirs_ref)
    leaf_far = left_mul((down_ref[0, 1], down_ref[1, 1]), far)
    for leaf in range(leaves):
        part = slice(leaf * rows, (leaf + 1) * rows)
        small = slice(leaf * rank, (leaf + 1) * rank)
        out_ref[part] = base_ref[part] + expand(1, bases_ref[1, leaf, 0], leaf_far[small])


def body(right_sides, near_blocks, leaf_bases, local_factors, upper_factors, top_couplings):
    bits_leaf = lax.axis_size("leaf").bit_length() - 1
    bits_rows = lax.axis_size("rows").bit_length() - 1
    devices = lax.axis_size("rows") * lax.axis_size("leaf")
    leaves = near_blocks.shape[1]
    columns = right_sides.shape[1]
    rank = leaf_bases.shape[-1]
    half = columns // 2
    stages = stages_of(bits_leaf + bits_rows)

    def swap(value, mask):
        pairs = [(source, source ^ mask) for source in range(devices)]
        return lax.ppermute(value, ("rows", "leaf"), pairs)

    unit = 2 * rank * rank * columns
    message = ((half, rank), F32)
    lifted = ((rank + half, rank), F32)
    coefs = ((leaves * rank, columns), F32)
    size = (right_sides.shape, F32)
    uppers = (2,) + upper_factors.shape[2:]
    loaded = call(
        functools.partial(start_kernel, leaves),
        [
            size,
            (near_blocks.shape, BF16),
            (leaf_bases.shape, BF16),
            (local_factors.shape, BF16),
            (uppers, BF16),
            ((2, rank, rank), BF16),
            ((leaves, rank, leaf_bases.shape[3]), BF16),
            ((2, 2 * rank, leaves * rank), BF16),
            coefs,
            lifted,
            message,
        ],
        [right_sides, near_blocks, leaf_bases, local_factors, upper_factors, top_couplings],
        150 * unit,
        hbm=True,
        scratch=[pltpu.SemaphoreType.DMA((6,))],
    )
    right, near, bases, local, upper, top, vt_inverse, up_inverse, coef, send, keep = loaded
    got = swap(send, 1)

    vt = [None, vt_inverse]
    up = [None, up_inverse]
    stage_tables, lower_refs, plan = [], [], []
    member = 1
    base = current = right
    chip = None
    norms = []
    mine = theirs = None
    applies = 2 * STEPS + 1
    for index in range(applies):
        last = index == applies - 1
        arrived = []
        value = chip
        norm = None
        for number, stage in enumerate(stages):
            low = 2 ** stage[0]
            lower_level = stage[0] - 1
            top_stage = number == len(stages) - 1
            masks = (low,) if len(stage) == 1 else (low, 2 * low, 3 * low)
            sent = [value] * len(masks)
            if index == 0 and len(stage) > 1:
                tall = (half + 2 * rank, rank)
                sent = call(
                    functools.partial(pack_kernel, lower_level, top_stage),
                    [
                        message if top_stage else (tall, F32),
                        (tall if top_stage else (half + 4 * rank, rank), F32),
                        (tall, F32),
                    ],
                    [upper] + ([value] if number else [keep, got]),
                    unit,
                )
                value = sent[0]
            elif index == 0 and value is None:
                value = keep + got[rank:]
                sent = [value] * len(masks)
            batch = [swap(data, mask) for data, mask in zip(sent, masks)]
            arrived += batch
            if index == 0:
                plan.append((lower_level, None))
                if len(stage) > 1:
                    plan.append((lower_level + 1, len(lower_refs)))
                    plan.append((lower_level + 1, len(lower_refs) + 1))
                    lower_refs += batch[1:]
                if not top_stage:
                    stage_tables += call(
                        functools.partial(stage_table_kernel, lower_level),
                        [((2, 2, 4 * rank, rank), BF16)],
                        [upper] + batch,
                        16 * unit,
                    )
            if number == 0:
                if index == 0:
                    tables = call(
                        functools.partial(local_table_kernel, leaves),
                        [
                            ((leaves, rank, leaf_bases.shape[3]), BF16),
                            ((2, 2 * rank, leaves * rank), BF16),
                            ((2, 2, leaves * rank, (leaves + 1) * rank), BF16),
                            ((2, 2, leaves * rank, rank), BF16),
                            ((2, 2, leaves * rank, rank), BF16),
                            ((4, rank, rank), F32),
                        ],
                        [local, bases, vt_inverse, up_inverse],
                        300 * unit,
                    )
                    vt[0], up[0], wide, down, feed, chip_feed = tables
                    chip_got = swap(chip_feed, 1)
                other = 1 - member
                shared = [near, bases, vt[other], up[other], wide, base, current, coef, got]
                if index:
                    shared += [down, feed, sibling_table, mine, theirs]
                if last:
                    base, norm = call(
                        functools.partial(last_local_kernel, leaves),
                        [size, ((8, columns), F32)],
                        shared + norms,
                        200 * unit,
                    )
                    norm_got = swap(norm, 1)
                else:
                    outs = [size, coefs, lifted, message]
                    if index:
                        outs.append(size if member == 0 else ((1, columns), F32))
                    results = call(
                        functools.partial(local_kernel, member, leaves, index == 0),
                        outs,
                        shared,
                        300 * unit,
                    )
                    base, coef, send, next_keep = results[:4]
                    next_got = swap(send, 1)
                    if index and member == 0:
                        iterate = results[4]
                    elif index:
                        norms.append(results[4])
            if not top_stage:
                extra = [norm, norm_got] if last and number == len(stages) - 2 else []
                args = [value] + batch + extra
                shape = (half + (8 if extra else 0), rank)
                value = call(
                    functools.partial(stage_kernel, member, half),
                    [(shape, F32)],
                    [stage_tables[number]] + args,
                    8 * unit,
                )[0]
        if index == 0:
            far_table, sibling_table = call(
                functools.partial(far_table_kernel, plan, half),
                [((2, 2, len(plan) * rank, 2 * rank), BF16), ((2, 2, rank, rank), BF16)],
                [upper, top, chip_feed, chip_got] + lower_refs,
                100 * unit,
            )
        results = call(
            functools.partial(far_kernel, member, last),
            [((8, columns), F32) if last else message, message],
            [far_table] + ([keep, got] if last else [next_keep, next_got]) + arrived,
            20 * unit,
        )
        chip, mine = results
        theirs = swap(mine, 1)
        if last:
            sums = chip + value[half:]
        else:
            keep, got = next_keep, next_got
        member = 1 - member
        if not last:
            current = right if member == 0 else iterate
    solution = call(
        functools.partial(finish_kernel, leaves),
        [size],
        [bases, down, base, mine, theirs],
        30 * unit,
    )[0]
    for stage in stages[:-1]:
        low = 2 ** stage[0]
        masks = (low,) if len(stage) == 1 else (low, 2 * low, 3 * low)
        sums = sum([swap(sums, mask) for mask in masks], sums)
    return solution, sums[:STEPS]


def stages_of(levels_up):
    return [tuple(range(level, min(level + 2, levels_up))) for level in range(1, levels_up, 2)]


def solution(mesh):
    placed = (
        P(("rows", "leaf"), None),
        P(None, ("rows", "leaf"), None, None),
        P(None, ("rows", "leaf"), None, None, None),
        P(None, ("rows", "leaf"), None, None, None),
        P(None, ("rows", "leaf"), None, None, None, None),
        P(),
    )

    return jax.shard_map(
        body,
        mesh=mesh,
        in_specs=placed,
        out_specs=(P(("rows", "leaf"), None), P()),
        check_vma=False,
    )
```

time: 209 us -> 172 us (0.82)
  local copies, waits for them, and re-layouts: 42.1 us -> 5.48 us
  waiting for transfers between devices: 46.1 us -> 60 us
  starting transfers between devices: 75.2 us -> 64.7 us
  other arithmetic: 2.79 us -> 0.01 us
    unnamed x105 -> x12, local copies, waits for them, and re-layouts: 32.4 us -> 4.9 us
    ppermute x69 -> x61, waiting for transfers between devices: 46.1 us -> 60 us  [swap(): return lax.ppermute(value, ('rows', 'leaf'), pairs)]
    ppermute x69 -> x61, starting transfers between devices: 75.2 us -> 64.7 us  [swap(): return lax.ppermute(value, ('rows', 'leaf'), pairs)]
    slice x5 -> x1, local copies, waits for them, and re-layouts: 4.78 us -> 0.58 us  [body(): return (solution, sums[:STEPS])]
    transpose x2 -> x0, local copies, waits for them, and re-layouts: 2.72 us -> none  [body(): qct = jnp.swapaxes(upper[:, :, 1:], -1, -2)]
    dynamic_slice x2 -> x0, local copies, waits for them, and re-layouts: 2.2 us -> none  [body(): lax.dynamic_index_in_dim(top_couplings, top_position, 1, keepdims=False)]
    pallas_call x26 -> x28, Pallas kernels: 40.2 us -> 40.3 us  [call(): pl.pallas_call(kernel, out_shape=[jax.ShapeDtypeStruct(shape, dtype) for...]
  transfers between devices with their start and end apart: 69 -> 61, of which waited for: 35 -> 40; matrix products, arithmetic and copies ran while one was open for 7% -> 0% of each run, Pallas kernels for 8% -> 8%
where the time goes in v2:
time: 172 us
  starting transfers between devices  64.7 us (38%)
  waiting for transfers between devices  60 us (35%)
  Pallas kernels  40.3 us (23%)
  local copies, waits for them, and re-layouts  5.48 us (3%)
    ppermute x61, starting transfers between devices, swap(): return lax.ppermute(value, ('rows', 'leaf'), pairs)  64.7 us
    ppermute x61, waiting for transfers between devices, swap(): return lax.ppermute(value, ('rows', 'leaf'), pairs)  60 us
    pallas_call x28, Pallas kernels, call(): pl.pallas_call(kernel, out_shape=[jax.ShapeDtypeStruct(shape, dtype) for...  40.3 us
    unnamed x12, local copies, waits for them, and re-layouts  4.9 us
  transfers between devices with their start and end apart: 61, of which 40 were waited for; matrix products, arithmetic and copies ran while one was open for 0% of the time, Pallas kernels for 8%

profile of v2, /device:TPU:0, one launch (start us, length us, event | category | flops | bytes accessed | tf_op | source)
XLA Modules:
  0.0 171.5 jit_solution(16725688780000337729)
XLA Ops:
  2.6 6.8 %shard_map.77 = (f32[2048,128]{1,0:T(8,128)S(1)}, bf16[2,4,512,512]{3,2,1,0:T(8,128)(2,1)}, bf16[2,4,2,512,128]{4,3,2,1,0:T(8,128)(2,1)}, bf16[2,7,3,128,128]{4,...) custom-call(f32[2048,128]{1,0:T(8,128)} %refs_0_.1, ...), custom_call_target="tpu_custom_call" | custom-call | flops 629145600 | tf_op jit(solution)/shard_map/pallas_call | solution.py:67
  11.0 2.9 %collective-permute-start.3 = (f32[576,128]{1,0:T(8,128)S(1)}, f32[576,128]{1,0:T(8,128)S(1)}, u32[]{:S(2)}, u32[]{:S(2)}) collective-permute-start(f32[576,128]{1,0:T(8,128)S(1)} %get-tuple-element.92), channel_id=1, source_target_pairs={{0,4},{1,5},{2,6},{3,7},{4,0},{5,1},{6,2},{7,3},{8,12},{9,13},{10,... | collective-permute-start | bytes 884744 | tf_op jit(solution)/shard_map/ppermute | solution.py:427
  18.4 5.8 %shard_map.78 = (bf16[4,128,512]{2,1,0:T(8,128)(2,1)S(1)}, bf16[2,256,512]{2,1,0:T(8,128)(2,1)S(1)}, bf16[2,2,512,640]{3,2,1,0:T(8,128)(2,1)S(1)}, bf16[2,2,512,...) custom-call(bf16[2,7,3,128,128]{4,3,2,1,0:T(8,128)(2,1)S(1)} %copy-done.5, ...), custom_call_target="tpu_custom_call" | custom-call | flops 1258291200 | tf_op jit(solution)/shard_map/pallas_call | solution.py:67
  26.4 2.7 %collective-permute-start.6 = (f32[320,128]{1,0:T(8,128)S(1)}, f32[320,128]{1,0:T(8,128)S(1)}, u32[]{:S(2)}, u32[]{:S(2)}) collective-permute-start(f32[320,128]{1,0:T(8,128)S(1)} %get-tuple-element.95), channel_id=1, source_target_pairs={{0,16},{1,17},{2,18},{3,19},{4,20},{5,21},{6,22},{7,23},{8,24},{9,... | collective-permute-start | bytes 491528 | tf_op jit(solution)/shard_map/ppermute | solution.py:427
  30.4 2.1 %shard_map.79 = (f32[2048,128]{1,0:T(8,128)S(1)}, f32[512,128]{1,0:T(8,128)S(1)}, f32[192,128]{1,0:T(8,128)S(1)}, f32[64,128]{1,0:T(8,128)S(1)}) custom-call(bf16[2,4,512,512]{3,2,1,0:T(8,128)(2,1)S(1)} %copy-done, bf16[2,4,2,512,128]{4,3,2,1,0:T(8,128)(2,1)S(1)} %copy-done.2, bf16[4,128,512]{2,1,0:T(8,128)(2,1)S(1)} %get-tuple-element.78.refs_2_.vt_ref, ...), custom_call_target="tpu_custom_call" | custom-call | flops 1258291200 | tf_op jit(solution)/shard_map/pallas_call | solution.py:67
  32.9 8.0 %collective-permute-done.6.refs_2_.refs_4_ = f32[320,128]{1,0:T(8,128)S(1)} collective-permute-done((f32[320,128]{1,0:T(8,128)S(1)}, f32[320,128]{1,0:T(8,128)S(1)}, u32[]{:S(2)}, u32[]{:S(2)}) %collective-permute-start.6) | collective-permute-done | bytes 163872 | tf_op jit(solution)/shard_map/ppermute | solution.py:427
  44.2 3.5 %shard_map.86 = (f32[2048,128]{1,0:T(8,128)S(1)}, f32[512,128]{1,0:T(8,128)S(1)}, f32[192,128]{1,0:T(8,128)S(1)}, f32[64,128]{1,0:T(8,128)S(1)}, f32[2048,128]{1,0:T(8,128)S(1)}) custom-call(bf16[2,4,512,512]{3,2,1,0:T(8,128)(2,1)S(1)} %copy-done, bf16[2,4,2,512,128]{4,3,2,1,0:T(8,128)(2,1)S(1)} %copy-done.2, ...), custom_call_target="tpu_custom_call" | custom-call | flops 1258291200 | tf_op jit(solution)/shard_map/pallas_call | solution.py:67
  52.7 2.6 %collective-permute-done.13.refs_3_.refs_2_ = f32[64,128]{1,0:T(8,128)S(1)} collective-permute-done((f32[64,128]{1,0:T(8,128)S(1)}, f32[64,128]{1,0:T(8,128)S(1)}, u32[]{:S(2)}, u32[]{:S(2)}) %collective-permute-start.13) | collective-permute-done | bytes 32800 | tf_op jit(solution)/shard_map/ppermute | solution.py:427
  55.5 3.6 %collective-permute-start.14 = (f32[64,128]{1,0:T(8,128)S(1)}, f32[64,128]{1,0:T(8,128)S(1)}, u32[]{:S(2)}, u32[]{:S(2)}) collective-permute-start(f32[64,128]{1,0:T(8,128)S(1)} %shard_map.87), channel_id=1, source_target_pairs={{0,8},{1,9},{2,10},{3,11},{4,12},{5,13},{6,14},{7,15},{8,0},{9,1},... | collective-permute-start | bytes 98312 | tf_op jit(solution)/shard_map/ppermute | solution.py:427
  59.1 2.0 %collective-permute-start.15 = (f32[64,128]{1,0:T(8,128)S(1)}, f32[64,128]{1,0:T(8,128)S(1)}, u32[]{:S(2)}, u32[]{:S(2)}) collective-permute-start(f32[64,128]{1,0:T(8,128)S(1)} %shard_map.87), channel_id=1, source_target_pairs={{0,16},{1,17},{2,18},{3,19},{4,20},{5,21},{6,22},{7,23},{8,24},{9,... | collective-permute-start | bytes 98312 | tf_op jit(solution)/shard_map/ppermute | solution.py:427
  63.9 2.9 %collective-permute-done.16.refs_5_ = f32[64,128]{1,0:T(8,128)S(1)} collective-permute-done((f32[64,128]{1,0:T(8,128)S(1)}, f32[64,128]{1,0:T(8,128)S(1)}, u32[]{:S(2)}, u32[]{:S(2)}) %collective-permute-start.16) | collective-permute-done | bytes 32800 | tf_op jit(solution)/shard_map/ppermute | solution.py:427
  68.3 3.1 %shard_map.89 = (f32[2048,128]{1,0:T(8,128)S(1)}, f32[512,128]{1,0:T(8,128)S(1)}, f32[192,128]{1,0:T(8,128)S(1)}, f32[64,128]{1,0:T(8,128)S(1)}, f32[1,128]{1,0:T(1,128)S(1)}) custom-call(bf16[2,4,512,512]{3,2,1,0:T(8,128)(2,1)S(1)} %copy-done, bf16[2,4,2,512,128]{4,3,2,1,0:T(8,128)(2,1)S(1)} %copy-done.2, ...), custom_call_target="tpu_custom_call" | custom-call | flops 1258291200 | tf_op jit(solution)/shard_map/pallas_call | solution.py:67
  72.7 2.4 %collective-permute-start.21 = (f32[64,128]{1,0:T(8,128)S(1)}, f32[64,128]{1,0:T(8,128)S(1)}, u32[]{:S(2)}, u32[]{:S(2)}) collective-permute-start(f32[64,128]{1,0:T(8,128)S(1)} %get-tuple-element.113.refs_0_), channel_id=1, source_target_pairs={{0,6},{1,7},{2,4},{3,5},{4,2},{5,3},{6,0},{7,1},{8,14},{9,15},{10,... | collective-permute-start | bytes 98312 | tf_op jit(solution)/shard_map/ppermute | solution.py:427
  79.6 2.4 %collective-permute-start.24 = (f32[64,128]{1,0:T(8,128)S(1)}, f32[64,128]{1,0:T(8,128)S(1)}, u32[]{:S(2)}, u32[]{:S(2)}) collective-permute-start(f32[64,128]{1,0:T(8,128)S(1)} %shard_map.90), channel_id=1, source_target_pairs={{0,24},{1,25},{2,26},{3,27},{4,28},{5,29},{6,30},{7,31},{8,16},{9,... | collective-permute-start | bytes 98312 | tf_op jit(solution)/shard_map/ppermute | solution.py:427
  83.0 2.4 %collective-permute-done.24.refs_5_ = f32[64,128]{1,0:T(8,128)S(1)} collective-permute-done((f32[64,128]{1,0:T(8,128)S(1)}, f32[64,128]{1,0:T(8,128)S(1)}, u32[]{:S(2)}, u32[]{:S(2)}) %collective-permute-start.24) | collective-permute-done | bytes 32800 | tf_op jit(solution)/shard_map/ppermute | solution.py:427
  87.0 3.5 %shard_map.92 = (f32[2048,128]{1,0:T(8,128)S(1)}, f32[512,128]{1,0:T(8,128)S(1)}, f32[192,128]{1,0:T(8,128)S(1)}, f32[64,128]{1,0:T(8,128)S(1)}, f32[2048,128]{1,0:T(8,128)S(1)}) custom-call(bf16[2,4,512,512]{3,2,1,0:T(8,128)(2,1)S(1)} %copy-done, bf16[2,4,2,512,128]{4,3,2,1,0:T(8,128)(2,1)S(1)} %copy-done.2, ...), custom_call_target="tpu_custom_call" | custom-call | flops 1258291200 | tf_op jit(solution)/shard_map/pallas_call | solution.py:67
  96.2 2.3 %collective-permute-done.29.refs_3_.refs_2_ = f32[64,128]{1,0:T(8,128)S(1)} collective-permute-done((f32[64,128]{1,0:T(8,128)S(1)}, f32[64,128]{1,0:T(8,128)S(1)}, u32[]{:S(2)}, u32[]{:S(2)}) %collective-permute-start.29) | collective-permute-done | bytes 32800 | tf_op jit(solution)/shard_map/ppermute | solution.py:427
  98.7 3.0 %collective-permute-start.31 = (f32[64,128]{1,0:T(8,128)S(1)}, f32[64,128]{1,0:T(8,128)S(1)}, u32[]{:S(2)}, u32[]{:S(2)}) collective-permute-start(f32[64,128]{1,0:T(8,128)S(1)} %shard_map.93), channel_id=1, source_target_pairs={{0,16},{1,17},{2,18},{3,19},{4,20},{5,21},{6,22},{7,23},{8,24},{9,... | collective-permute-start | bytes 98312 | tf_op jit(solution)/shard_map/ppermute | solution.py:427
  103.6 3.8 %collective-permute-done.32.refs_5_ = f32[64,128]{1,0:T(8,128)S(1)} collective-permute-done((f32[64,128]{1,0:T(8,128)S(1)}, f32[64,128]{1,0:T(8,128)S(1)}, u32[]{:S(2)}, u32[]{:S(2)}) %collective-permute-start.32) | collective-permute-done | bytes 32800 | tf_op jit(solution)/shard_map/ppermute | solution.py:427
  109.0 2.9 %shard_map.95 = (f32[2048,128]{1,0:T(8,128)S(1)}, f32[512,128]{1,0:T(8,128)S(1)}, f32[192,128]{1,0:T(8,128)S(1)}, f32[64,128]{1,0:T(8,128)S(1)}, f32[1,128]{1,0:T(1,128)S(1)}) custom-call(bf16[2,4,512,512]{3,2,1,0:T(8,128)(2,1)S(1)} %copy-done, bf16[2,4,2,512,128]{4,3,2,1,0:T(8,128)(2,1)S(1)} %copy-done.2, ...), custom_call_target="tpu_custom_call" | custom-call | flops 1258291200 | tf_op jit(solution)/shard_map/pallas_call | solution.py:67
  113.2 2.4 %collective-permute-start.37 = (f32[64,128]{1,0:T(8,128)S(1)}, f32[64,128]{1,0:T(8,128)S(1)}, u32[]{:S(2)}, u32[]{:S(2)}) collective-permute-start(f32[64,128]{1,0:T(8,128)S(1)} %get-tuple-element.126.refs_0_), channel_id=1, source_target_pairs={{0,6},{1,7},{2,4},{3,5},{4,2},{5,3},{6,0},{7,1},{8,14},{9,15},{10,... | collective-permute-start | bytes 98312 | tf_op jit(solution)/shard_map/ppermute | solution.py:427
  118.2 1.9 %collective-permute-start.39 = (f32[64,128]{1,0:T(8,128)S(1)}, f32[64,128]{1,0:T(8,128)S(1)}, u32[]{:S(2)}, u32[]{:S(2)}) collective-permute-start(f32[64,128]{1,0:T(8,128)S(1)} %shard_map.96), channel_id=1, source_target_pairs={{0,16},{1,17},{2,18},{3,19},{4,20},{5,21},{6,22},{7,23},{8,24},{9,... | collective-permute-start | bytes 98312 | tf_op jit(solution)/shard_map/ppermute | solution.py:427
  120.1 2.4 %collective-permute-start.40 = (f32[64,128]{1,0:T(8,128)S(1)}, f32[64,128]{1,0:T(8,128)S(1)}, u32[]{:S(2)}, u32[]{:S(2)}) collective-permute-start(f32[64,128]{1,0:T(8,128)S(1)} %shard_map.96), channel_id=1, source_target_pairs={{0,24},{1,25},{2,26},{3,27},{4,28},{5,29},{6,30},{7,31},{8,16},{9,... | collective-permute-start | bytes 98312 | tf_op jit(solution)/shard_map/ppermute | solution.py:427
  123.4 2.4 %collective-permute-done.40.refs_5_ = f32[64,128]{1,0:T(8,128)S(1)} collective-permute-done((f32[64,128]{1,0:T(8,128)S(1)}, f32[64,128]{1,0:T(8,128)S(1)}, u32[]{:S(2)}, u32[]{:S(2)}) %collective-permute-start.40) | collective-permute-done | bytes 32800 | tf_op jit(solution)/shard_map/ppermute | solution.py:427
  127.4 3.5 %shard_map.98 = (f32[2048,128]{1,0:T(8,128)S(1)}, f32[512,128]{1,0:T(8,128)S(1)}, f32[192,128]{1,0:T(8,128)S(1)}, f32[64,128]{1,0:T(8,128)S(1)}, f32[2048,128]{1,0:T(8,128)S(1)}) custom-call(bf16[2,4,512,512]{3,2,1,0:T(8,128)(2,1)S(1)} %copy-done, bf16[2,4,2,512,128]{4,3,2,1,0:T(8,128)(2,1)S(1)} %copy-done.2, ...), custom_call_target="tpu_custom_call" | custom-call | flops 1258291200 | tf_op jit(solution)/shard_map/pallas_call | solution.py:67
  136.9 2.3 %collective-permute-done.45.refs_3_.refs_2_ = f32[64,128]{1,0:T(8,128)S(1)} collective-permute-done((f32[64,128]{1,0:T(8,128)S(1)}, f32[64,128]{1,0:T(8,128)S(1)}, u32[]{:S(2)}, u32[]{:S(2)}) %collective-permute-start.45) | collective-permute-done | bytes 32800 | tf_op jit(solution)/shard_map/ppermute | solution.py:427
  139.4 3.0 %collective-permute-start.47 = (f32[64,128]{1,0:T(8,128)S(1)}, f32[64,128]{1,0:T(8,128)S(1)}, u32[]{:S(2)}, u32[]{:S(2)}) collective-permute-start(f32[64,128]{1,0:T(8,128)S(1)} %shard_map.99), channel_id=1, source_target_pairs={{0,16},{1,17},{2,18},{3,19},{4,20},{5,21},{6,22},{7,23},{8,24},{9,... | collective-permute-start | bytes 98312 | tf_op jit(solution)/shard_map/ppermute | solution.py:427
  144.3 3.8 %collective-permute-done.48.refs_5_ = f32[64,128]{1,0:T(8,128)S(1)} collective-permute-done((f32[64,128]{1,0:T(8,128)S(1)}, f32[64,128]{1,0:T(8,128)S(1)}, u32[]{:S(2)}, u32[]{:S(2)}) %collective-permute-start.48) | collective-permute-done | bytes 32800 | tf_op jit(solution)/shard_map/ppermute | solution.py:427
  149.7 2.4 %collective-permute-start.52 = (f32[64,128]{1,0:T(8,128)S(1)}, f32[64,128]{1,0:T(8,128)S(1)}, u32[]{:S(2)}, u32[]{:S(2)}) collective-permute-start(f32[64,128]{1,0:T(8,128)S(1)} %get-tuple-element.138.refs_0_), channel_id=1, source_target_pairs={{0,6},{1,7},{2,4},{3,5},{4,2},{5,3},{6,0},{7,1},{8,14},{9,15},{10,... | collective-permute-start | bytes 98312 | tf_op jit(solution)/shard_map/ppermute | solution.py:427
  152.1 2.2 %shard_map.101 = (f32[2048,128]{1,0:T(8,128)S(1)}, f32[8,128]{1,0:T(8,128)S(1)}) custom-call(bf16[2,4,512,512]{3,2,1,0:T(8,128)(2,1)S(1)} %copy-done, bf16[2,4,2,512,128]{4,3,2,1,0:T(8,128)(2,1)S(1)} %copy-done.2, bf16[4,128,512]{2,1,0:T(8,128)(2,1)S(1)} %get-tuple-element.78.refs_2_.vt_ref, bf16[2,256,512]{2,1,0:T(8,128)(2,1)S(1)} %get-tuple-element.79.refs_3_.up_ref, ...), custom_call_target="tpu_custom_call" | custom-call | flops 838860800 | tf_op jit(solution)/shard_map/pallas_call | solution.py:67
  157.7 2.5 %collective-permute-start.56 = (f32[72,128]{1,0:T(8,128)S(1)}, f32[72,128]{1,0:T(8,128)S(1)}, u32[]{:S(2)}, u32[]{:S(2)}) collective-permute-start(f32[72,128]{1,0:T(8,128)S(1)} %shard_map.102), channel_id=1, source_target_pairs={{0,24},{1,25},{2,26},{3,27},{4,28},{5,29},{6,30},{7,31},{8,16},{9,... | collective-permute-start | bytes 110600 | tf_op jit(solution)/shard_map/ppermute | solution.py:427
  160.7 2.7 %collective-permute-done.56.refs_5_ = f32[72,128]{1,0:T(8,128)S(1)} collective-permute-done((f32[72,128]{1,0:T(8,128)S(1)}, f32[72,128]{1,0:T(8,128)S(1)}, u32[]{:S(2)}, u32[]{:S(2)}) %collective-permute-start.56) | collective-permute-done | bytes 36896 | tf_op jit(solution)/shard_map/ppermute | solution.py:427
  (133 shorter events, 70.3 us)
Async XLA Ops:
  11.0 14.9 %collective-permute-start.3 = (f32[576,128]{1,0:T(8,128)S(1)}, f32[576,128]{1,0:T(8,128)S(1)}, u32[]{:S(2)}, u32[]{:S(2)}) collective-permute-start(f32[576,128]{1,0:T(8,128)S(1)} %get-tuple-element.92), channel_id=1, source_target_pairs={{0,4},{1,5},{2,6},{3,7},{4,0},{5,1},{6,2},{7,3},{8,12},{9,13},{10,... | collective-permute-start | bytes 884744 | tf_op jit(solution)/shard_map/ppermute | solution.py:427
  13.9 12.0 %collective-permute-start.4 = (f32[320,128]{1,0:T(8,128)S(1)}, f32[320,128]{1,0:T(8,128)S(1)}, u32[]{:S(2)}, u32[]{:S(2)}) collective-permute-start(f32[320,128]{1,0:T(8,128)S(1)} %get-tuple-element.93), channel_id=1, source_target_pairs={{0,6},{1,7},{2,4},{3,5},{4,2},{5,3},{6,0},{7,1},{8,14},{9,15},{10,... | collective-permute-start | bytes 491528 | tf_op jit(solution)/shard_map/ppermute | solution.py:427
  15.4 10.6 %collective-permute-start.5 = (f32[320,128]{1,0:T(8,128)S(1)}, f32[320,128]{1,0:T(8,128)S(1)}, u32[]{:S(2)}, u32[]{:S(2)}) collective-permute-start(f32[320,128]{1,0:T(8,128)S(1)} %get-tuple-element.94.refs_0_), channel_id=1, source_target_pairs={{0,2},{1,3},{2,0},{3,1},{4,6},{5,7},{6,4},{7,5},{8,10},{9,11},{10,... | collective-permute-start | bytes 491528 | tf_op jit(solution)/shard_map/ppermute | solution.py:427
  24.2 8.7 %collective-permute-start.2 = (f32[4,128,128]{2,1,0:T(8,128)S(1)}, f32[4,128,128]{2,1,0:T(8,128)S(1)}, u32[]{:S(2)}, u32[]{:S(2)}) collective-permute-start(f32[4,128,128]{2,1,0:T(8,128)S(1)} %get-tuple-element.90.chip_ref), channel_id=1, source_target_pairs={{0,1},{1,0},{2,3},{3,2},{4,5},{5,4},{6,7},{7,6},{8,9},{9,8},{10,11... | collective-permute-start | bytes 786440 | tf_op jit(solution)/shard_map/ppermute | solution.py:427
  26.4 14.5 %collective-permute-start.6 = (f32[320,128]{1,0:T(8,128)S(1)}, f32[320,128]{1,0:T(8,128)S(1)}, u32[]{:S(2)}, u32[]{:S(2)}) collective-permute-start(f32[320,128]{1,0:T(8,128)S(1)} %get-tuple-element.95), channel_id=1, source_target_pairs={{0,16},{1,17},{2,18},{3,19},{4,20},{5,21},{6,22},{7,23},{8,24},{9,... | collective-permute-start | bytes 491528 | tf_op jit(solution)/shard_map/ppermute | solution.py:427
  29.1 11.9 %collective-permute-start.7 = (f32[320,128]{1,0:T(8,128)S(1)}, f32[320,128]{1,0:T(8,128)S(1)}, u32[]{:S(2)}, u32[]{:S(2)}) collective-permute-start(f32[320,128]{1,0:T(8,128)S(1)} %get-tuple-element.96), channel_id=1, source_target_pairs={{0,24},{1,25},{2,26},{3,27},{4,28},{5,29},{6,30},{7,31},{8,16},{9,... | collective-permute-start | bytes 491528 | tf_op jit(solution)/shard_map/ppermute | solution.py:427
  32.5 10.0 %collective-permute-start.1 = (f32[192,128]{1,0:T(8,128)S(1)}, f32[192,128]{1,0:T(8,128)S(1)}, u32[]{:S(2)}, u32[]{:S(2)}) collective-permute-start(f32[192,128]{1,0:T(8,128)S(1)} %get-tuple-element.86), channel_id=1, source_target_pairs={{0,1},{1,0},{2,3},{3,2},{4,5},{5,4},{6,7},{7,6},{8,9},{9,8},{10,11... | collective-permute-start | bytes 294920 | tf_op jit(solution)/shard_map/ppermute | solution.py:427
  32.6 10.0 %collective-permute-start.8 = (f32[64,128]{1,0:T(8,128)S(1)}, f32[64,128]{1,0:T(8,128)S(1)}, u32[]{:S(2)}, u32[]{:S(2)}) collective-permute-start(f32[64,128]{1,0:T(8,128)S(1)} %get-tuple-element.100), channel_id=1, source_target_pairs={{0,8},{1,9},{2,10},{3,11},{4,12},{5,13},{6,14},{7,15},{8,0},{9,1},... | collective-permute-start | bytes 98312 | tf_op jit(solution)/shard_map/ppermute | solution.py:427
  47.7 19.0 %collective-permute-start.10 = (f32[192,128]{1,0:T(8,128)S(1)}, f32[192,128]{1,0:T(8,128)S(1)}, u32[]{:S(2)}, u32[]{:S(2)}) collective-permute-start(f32[192,128]{1,0:T(8,128)S(1)} %get-tuple-element.105), channel_id=1, source_target_pairs={{0,1},{1,0},{2,3},{3,2},{4,5},{5,4},{6,7},{7,6},{8,9},{9,8},{10,11... | collective-permute-start | bytes 294920 | tf_op jit(solution)/shard_map/ppermute | solution.py:427
  50.5 4.8 %collective-permute-start.13 = (f32[64,128]{1,0:T(8,128)S(1)}, f32[64,128]{1,0:T(8,128)S(1)}, u32[]{:S(2)}, u32[]{:S(2)}) collective-permute-start(f32[64,128]{1,0:T(8,128)S(1)} %get-tuple-element.107.refs_0_), channel_id=1, source_target_pairs={{0,6},{1,7},{2,4},{3,5},{4,2},{5,3},{6,0},{7,1},{8,14},{9,15},{10,... | collective-permute-start | bytes 98312 | tf_op jit(solution)/shard_map/ppermute | solution.py:427
  55.5 6.9 %collective-permute-start.14 = (f32[64,128]{1,0:T(8,128)S(1)}, f32[64,128]{1,0:T(8,128)S(1)}, u32[]{:S(2)}, u32[]{:S(2)}) collective-permute-start(f32[64,128]{1,0:T(8,128)S(1)} %shard_map.87), channel_id=1, source_target_pairs={{0,8},{1,9},{2,10},{3,11},{4,12},{5,13},{6,14},{7,15},{8,0},{9,1},... | collective-permute-start | bytes 98312 | tf_op jit(solution)/shard_map/ppermute | solution.py:427
  59.1 4.8 %collective-permute-start.15 = (f32[64,128]{1,0:T(8,128)S(1)}, f32[64,128]{1,0:T(8,128)S(1)}, u32[]{:S(2)}, u32[]{:S(2)}) collective-permute-start(f32[64,128]{1,0:T(8,128)S(1)} %shard_map.87), channel_id=1, source_target_pairs={{0,16},{1,17},{2,18},{3,19},{4,20},{5,21},{6,22},{7,23},{8,24},{9,... | collective-permute-start | bytes 98312 | tf_op jit(solution)/shard_map/ppermute | solution.py:427
  61.0 5.7 %collective-permute-start.16 = (f32[64,128]{1,0:T(8,128)S(1)}, f32[64,128]{1,0:T(8,128)S(1)}, u32[]{:S(2)}, u32[]{:S(2)}) collective-permute-start(f32[64,128]{1,0:T(8,128)S(1)} %shard_map.87), channel_id=1, source_target_pairs={{0,24},{1,25},{2,26},{3,27},{4,28},{5,29},{6,30},{7,31},{8,16},{9,... | collective-permute-start | bytes 98312 | tf_op jit(solution)/shard_map/ppermute | solution.py:427
  71.4 14.0 %collective-permute-start.18 = (f32[192,128]{1,0:T(8,128)S(1)}, f32[192,128]{1,0:T(8,128)S(1)}, u32[]{:S(2)}, u32[]{:S(2)}) collective-permute-start(f32[192,128]{1,0:T(8,128)S(1)} %get-tuple-element.111), channel_id=1, source_target_pairs={{0,1},{1,0},{2,3},{3,2},{4,5},{5,4},{6,7},{7,6},{8,9},{9,8},{10,11... | collective-permute-start | bytes 294920 | tf_op jit(solution)/shard_map/ppermute | solution.py:427
  72.7 4.8 %collective-permute-start.21 = (f32[64,128]{1,0:T(8,128)S(1)}, f32[64,128]{1,0:T(8,128)S(1)}, u32[]{:S(2)}, u32[]{:S(2)}) collective-permute-start(f32[64,128]{1,0:T(8,128)S(1)} %get-tuple-element.113.refs_0_), channel_id=1, source_target_pairs={{0,6},{1,7},{2,4},{3,5},{4,2},{5,3},{6,0},{7,1},{8,14},{9,15},{10,... | collective-permute-start | bytes 98312 | tf_op jit(solution)/shard_map/ppermute | solution.py:427
  77.8 5.1 %collective-permute-start.23 = (f32[64,128]{1,0:T(8,128)S(1)}, f32[64,128]{1,0:T(8,128)S(1)}, u32[]{:S(2)}, u32[]{:S(2)}) collective-permute-start(f32[64,128]{1,0:T(8,128)S(1)} %shard_map.90), channel_id=1, source_target_pairs={{0,16},{1,17},{2,18},{3,19},{4,20},{5,21},{6,22},{7,23},{8,24},{9,... | collective-permute-start | bytes 98312 | tf_op jit(solution)/shard_map/ppermute | solution.py:427
  79.6 5.7 %collective-permute-start.24 = (f32[64,128]{1,0:T(8,128)S(1)}, f32[64,128]{1,0:T(8,128)S(1)}, u32[]{:S(2)}, u32[]{:S(2)}) collective-permute-start(f32[64,128]{1,0:T(8,128)S(1)} %shard_map.90), channel_id=1, source_target_pairs={{0,24},{1,25},{2,26},{3,27},{4,28},{5,29},{6,30},{7,31},{8,16},{9,... | collective-permute-start | bytes 98312 | tf_op jit(solution)/shard_map/ppermute | solution.py:427
  90.5 17.0 %collective-permute-start.26 = (f32[192,128]{1,0:T(8,128)S(1)}, f32[192,128]{1,0:T(8,128)S(1)}, u32[]{:S(2)}, u32[]{:S(2)}) collective-permute-start(f32[192,128]{1,0:T(8,128)S(1)} %get-tuple-element.118), channel_id=1, source_target_pairs={{0,1},{1,0},{2,3},{3,2},{4,5},{5,4},{6,7},{7,6},{8,9},{9,8},{10,11... | collective-permute-start | bytes 294920 | tf_op jit(solution)/shard_map/ppermute | solution.py:427
  93.7 4.8 %collective-permute-start.29 = (f32[64,128]{1,0:T(8,128)S(1)}, f32[64,128]{1,0:T(8,128)S(1)}, u32[]{:S(2)}, u32[]{:S(2)}) collective-permute-start(f32[64,128]{1,0:T(8,128)S(1)} %get-tuple-element.120.refs_0_), channel_id=1, source_target_pairs={{0,6},{1,7},{2,4},{3,5},{4,2},{5,3},{6,0},{7,1},{8,14},{9,15},{10,... | collective-permute-start | bytes 98312 | tf_op jit(solution)/shard_map/ppermute | solution.py:427
  98.7 4.9 %collective-permute-start.31 = (f32[64,128]{1,0:T(8,128)S(1)}, f32[64,128]{1,0:T(8,128)S(1)}, u32[]{:S(2)}, u32[]{:S(2)}) collective-permute-start(f32[64,128]{1,0:T(8,128)S(1)} %shard_map.93), channel_id=1, source_target_pairs={{0,16},{1,17},{2,18},{3,19},{4,20},{5,21},{6,22},{7,23},{8,24},{9,... | collective-permute-start | bytes 98312 | tf_op jit(solution)/shard_map/ppermute | solution.py:427
  101.7 5.7 %collective-permute-start.32 = (f32[64,128]{1,0:T(8,128)S(1)}, f32[64,128]{1,0:T(8,128)S(1)}, u32[]{:S(2)}, u32[]{:S(2)}) collective-permute-start(f32[64,128]{1,0:T(8,128)S(1)} %shard_map.93), channel_id=1, source_target_pairs={{0,24},{1,25},{2,26},{3,27},{4,28},{5,29},{6,30},{7,31},{8,16},{9,... | collective-permute-start | bytes 98312 | tf_op jit(solution)/shard_map/ppermute | solution.py:427
  111.9 14.0 %collective-permute-start.34 = (f32[192,128]{1,0:T(8,128)S(1)}, f32[192,128]{1,0:T(8,128)S(1)}, u32[]{:S(2)}, u32[]{:S(2)}) collective-permute-start(f32[192,128]{1,0:T(8,128)S(1)} %get-tuple-element.124), channel_id=1, source_target_pairs={{0,1},{1,0},{2,3},{3,2},{4,5},{5,4},{6,7},{7,6},{8,9},{9,8},{10,11... | collective-permute-start | bytes 294920 | tf_op jit(solution)/shard_map/ppermute | solution.py:427
  118.2 5.2 %collective-permute-start.39 = (f32[64,128]{1,0:T(8,128)S(1)}, f32[64,128]{1,0:T(8,128)S(1)}, u32[]{:S(2)}, u32[]{:S(2)}) collective-permute-start(f32[64,128]{1,0:T(8,128)S(1)} %shard_map.96), channel_id=1, source_target_pairs={{0,16},{1,17},{2,18},{3,19},{4,20},{5,21},{6,22},{7,23},{8,24},{9,... | collective-permute-start | bytes 98312 | tf_op jit(solution)/shard_map/ppermute | solution.py:427
  120.1 5.7 %collective-permute-start.40 = (f32[64,128]{1,0:T(8,128)S(1)}, f32[64,128]{1,0:T(8,128)S(1)}, u32[]{:S(2)}, u32[]{:S(2)}) collective-permute-start(f32[64,128]{1,0:T(8,128)S(1)} %shard_map.96), channel_id=1, source_target_pairs={{0,24},{1,25},{2,26},{3,27},{4,28},{5,29},{6,30},{7,31},{8,16},{9,... | collective-permute-start | bytes 98312 | tf_op jit(solution)/shard_map/ppermute | solution.py:427
  130.9 17.2 %collective-permute-start.42 = (f32[192,128]{1,0:T(8,128)S(1)}, f32[192,128]{1,0:T(8,128)S(1)}, u32[]{:S(2)}, u32[]{:S(2)}) collective-permute-start(f32[192,128]{1,0:T(8,128)S(1)} %get-tuple-element.131), channel_id=1, source_target_pairs={{0,1},{1,0},{2,3},{3,2},{4,5},{5,4},{6,7},{7,6},{8,9},{9,8},{10,11... | collective-permute-start | bytes 294920 | tf_op jit(solution)/shard_map/ppermute | solution.py:427
  139.4 4.9 %collective-permute-start.47 = (f32[64,128]{1,0:T(8,128)S(1)}, f32[64,128]{1,0:T(8,128)S(1)}, u32[]{:S(2)}, u32[]{:S(2)}) collective-permute-start(f32[64,128]{1,0:T(8,128)S(1)} %shard_map.99), channel_id=1, source_target_pairs={{0,16},{1,17},{2,18},{3,19},{4,20},{5,21},{6,22},{7,23},{8,24},{9,... | collective-permute-start | bytes 98312 | tf_op jit(solution)/shard_map/ppermute | solution.py:427
  142.4 5.7 %collective-permute-start.48 = (f32[64,128]{1,0:T(8,128)S(1)}, f32[64,128]{1,0:T(8,128)S(1)}, u32[]{:S(2)}, u32[]{:S(2)}) collective-permute-start(f32[64,128]{1,0:T(8,128)S(1)} %shard_map.99), channel_id=1, source_target_pairs={{0,24},{1,25},{2,26},{3,27},{4,28},{5,29},{6,30},{7,31},{8,16},{9,... | collective-permute-start | bytes 98312 | tf_op jit(solution)/shard_map/ppermute | solution.py:427
  148.5 5.8 %collective-permute-start.50 = (f32[64,128]{1,0:T(8,128)S(1)}, f32[64,128]{1,0:T(8,128)S(1)}, u32[]{:S(2)}, u32[]{:S(2)}) collective-permute-start(f32[64,128]{1,0:T(8,128)S(1)} %get-tuple-element.138.refs_0_), channel_id=1, source_target_pairs={{0,2},{1,3},{2,0},{3,1},{4,6},{5,7},{6,4},{7,5},{8,10},{9,11},{10,... | collective-permute-start | bytes 98312 | tf_op jit(solution)/shard_map/ppermute | solution.py:427
  149.1 5.3 %collective-permute-start.51 = (f32[64,128]{1,0:T(8,128)S(1)}, f32[64,128]{1,0:T(8,128)S(1)}, u32[]{:S(2)}, u32[]{:S(2)}) collective-permute-start(f32[64,128]{1,0:T(8,128)S(1)} %get-tuple-element.138.refs_0_), channel_id=1, source_target_pairs={{0,4},{1,5},{2,6},{3,7},{4,0},{5,1},{6,2},{7,3},{8,12},{9,13},{10,... | collective-permute-start | bytes 98312 | tf_op jit(solution)/shard_map/ppermute | solution.py:427
  149.7 4.8 %collective-permute-start.52 = (f32[64,128]{1,0:T(8,128)S(1)}, f32[64,128]{1,0:T(8,128)S(1)}, u32[]{:S(2)}, u32[]{:S(2)}) collective-permute-start(f32[64,128]{1,0:T(8,128)S(1)} %get-tuple-element.138.refs_0_), channel_id=1, source_target_pairs={{0,6},{1,7},{2,4},{3,5},{4,2},{5,3},{6,0},{7,1},{8,14},{9,15},{10,... | collective-permute-start | bytes 98312 | tf_op jit(solution)/shard_map/ppermute | solution.py:427
  155.8 4.9 %collective-permute-start.55 = (f32[72,128]{1,0:T(8,128)S(1)}, f32[72,128]{1,0:T(8,128)S(1)}, u32[]{:S(2)}, u32[]{:S(2)}) collective-permute-start(f32[72,128]{1,0:T(8,128)S(1)} %shard_map.102), channel_id=1, source_target_pairs={{0,16},{1,17},{2,18},{3,19},{4,20},{5,21},{6,22},{7,23},{8,24},{9,... | collective-permute-start | bytes 110600 | tf_op jit(solution)/shard_map/ppermute | solution.py:427
  157.7 5.8 %collective-permute-start.56 = (f32[72,128]{1,0:T(8,128)S(1)}, f32[72,128]{1,0:T(8,128)S(1)}, u32[]{:S(2)}, u32[]{:S(2)}) collective-permute-start(f32[72,128]{1,0:T(8,128)S(1)} %shard_map.102), channel_id=1, source_target_pairs={{0,24},{1,25},{2,26},{3,27},{4,28},{5,29},{6,30},{7,31},{8,16},{9,... | collective-permute-start | bytes 110600 | tf_op jit(solution)/shard_map/ppermute | solution.py:427
  (35 other events, 121.5 us)

commit v3 on v2

v3 whole, which is shorter than its diff:
```python
import functools

import jax
import jax.numpy as jnp
from jax import lax
from jax.experimental import pallas as pl
from jax.experimental.pallas import tpu as pltpu
from jax.sharding import PartitionSpec as P


STEPS = 3
BF16 = jnp.bfloat16
F32 = jnp.float32
VMEM_LIMIT = 16 * 2**20
START_LIMIT = 48 * 2**20


def mm(left, right):
    return jnp.dot(left, right, preferred_element_type=F32)


def pieces(value):
    high = value.astype(BF16)
    return high, (value - high.astype(F32)).astype(BF16)


def left_mul(table, value):
    high, low = pieces(value)
    width = value.shape[1]
    both = mm(table[0], jnp.concatenate([high, low], axis=1))
    return both[:, :width] + both[:, width:] + mm(table[1], high)


def right_mul(value, table):
    high, low = pieces(value)
    rows = value.shape[0]
    both = mm(jnp.concatenate([high, low], axis=0), table[0])
    return both[:rows] + both[rows:] + mm(high, table[1])


def mul(left, right):
    return left_mul(pieces(left), right)


def exact_left(table, value):
    high, low = pieces(value)
    width = value.shape[1]
    both = mm(table, jnp.concatenate([high, low], axis=1))
    return both[:, :width] + both[:, width:]


def exact_right(value, table):
    high, low = pieces(value)
    rows = value.shape[0]
    both = mm(jnp.concatenate([high, low], axis=0), table)
    return both[:rows] + both[rows:]


def put(ref, index, value):
    high, low = pieces(value)
    ref[(0,) + index] = high
    ref[(1,) + index] = low


def call(kernel, outs, args, flops, hbm=False, scratch=()):
    specs = [pl.BlockSpec(memory_space=pltpu.HBM if hbm else pltpu.VMEM)] * len(args)
    return pl.pallas_call(
        kernel,
        out_shape=[jax.ShapeDtypeStruct(shape, dtype) for shape, dtype in outs],
        in_specs=specs,
        out_specs=[pl.BlockSpec(memory_space=pltpu.VMEM)] * len(outs),
        scratch_shapes=list(scratch),
        compiler_params=pltpu.CompilerParams(vmem_limit_bytes=START_LIMIT if hbm else VMEM_LIMIT),
        cost_estimate=pl.CostEstimate(flops=flops, bytes_accessed=0, transcendentals=0),
    )(*args)


def level_offsets(leaf_count):
    offsets, count, offset = [], leaf_count, 0
    while count >= 1:
        offsets.append(offset)
        offset += count
        count //= 2
    return offsets


def send_parts(device, lifted, send_ref, keep_ref):
    columns = lifted.shape[1]
    half = columns // 2
    turned = lifted.T
    first = lax.axis_index("leaf") % 2 == 0
    keep_ref[...] = jnp.where(first, turned[:half], turned[half:])
    send_ref[: device.shape[0]] = device
    send_ref[device.shape[0] :] = jnp.where(first, turned[half:], turned[:half])


def start_kernel(leaves, *refs):
    right_hbm, bases_hbm, local_hbm = refs[:3]
    upper_rows_ref, lower_rows_ref, u0_ref, u1_ref, v0_ref, local0_ref, local1_ref = refs[3:10]
    vt_ref, up_ref, coef_ref, send_ref, keep_ref, v1_ref, semaphores = refs[10:]
    rows = right_hbm.shape[0] // leaves
    middle = right_hbm.shape[0] // 2
    copies = [
        pltpu.make_async_copy(source, target, semaphores.at[index])
        for index, (source, target) in enumerate(
            [
                (local_hbm.at[1], local1_ref),
                (bases_hbm.at[1, :, 1], v1_ref),
                (right_hbm.at[:middle], upper_rows_ref),
                (right_hbm.at[middle:], lower_rows_ref),
                (local_hbm.at[0], local0_ref),
                (bases_hbm.at[0, :, 1], v0_ref),
                (bases_hbm.at[1, :, 0], u1_ref),
                (bases_hbm.at[0, :, 0], u0_ref),
            ]
        )
    ]
    for copy in copies:
        copy.start()
    copies[0].wait()
    rank = local1_ref.shape[-1]
    up_table(leaves, local1_ref, up_ref)
    copies[1].wait()
    for leaf in range(leaves):
        vt_ref[leaf] = v1_ref[leaf].T
    copies[2].wait()
    copies[3].wait()
    for leaf in range(leaves):
        value = rows_of((upper_rows_ref, lower_rows_ref), leaf, rows).astype(BF16)
        coef_ref[leaf * rank : (leaf + 1) * rank] = mm(vt_ref[leaf], value)
    lifted = left_mul((up_ref[0], up_ref[1]), coef_ref[...])
    send_parts(lifted[:rank], lifted[rank:], send_ref, keep_ref)
    for copy in copies[4:]:
        copy.wait()


def rows_of(refs, leaf, rows):
    held = refs[0].shape[0] // rows
    place = (leaf % held) * rows
    return refs[leaf // held][place : place + rows]


def up_table(leaves, local_ref, up_ref):
    rank = local_ref.shape[-1]
    offsets = level_offsets(leaves)
    turned = {}

    def transfer(node):
        if node not in turned:
            turned[node] = local_ref[node, 0].T
        return turned[node]

    for leaf in range(leaves):
        trail = transfer(leaf).astype(F32)
        for depth in range(1, len(offsets)):
            if depth == len(offsets) - 1:
                put(up_ref, (slice(0, rank), pl.ds(leaf * rank, rank)), trail)
            trail = exact_left(transfer(offsets[depth] + (leaf >> depth)), trail)
        put(up_ref, (slice(rank, 2 * rank), pl.ds(leaf * rank, rank)), trail)


def pack_kernel(base, last, upper_ref, *refs):
    near_ref, far_ref, cross_ref = refs[-3:]
    half = cross_ref.shape[0]
    rank = upper_ref.shape[-1]
    value = refs[0][...]
    if len(refs) == 5:
        value = value + refs[1][rank:]
    risen = exact_right(value, upper_ref[1, base, 0])
    near_ref[:half] = value
    far_ref[:half] = risen
    cross_ref[...] = risen
    if not last:
        for member in range(2):
            rows = pl.ds(half + member * rank, rank)
            near_ref[rows] = upper_ref[member, base, 0].astype(F32)
            far_ref[rows] = upper_ref[member, base + 1, 0].astype(F32)


def stage_table_kernel(base, half, upper_ref, near_ref, far_ref, out_ref):
    rank = upper_ref.shape[-1]
    for member in range(2):
        rows = pl.ds(half + member * rank, rank)
        here = upper_ref[member, base + 1, 0]
        put(out_ref, (member, pl.ds(0, rank)), mm(upper_ref[member, base, 0], here))
        put(out_ref, (member, pl.ds(rank, rank)), mm(near_ref[rows].astype(BF16), here))
        put(out_ref, (member, pl.ds(2 * rank, rank)), far_ref[rows])


def local_table_kernel(leaves, *refs):
    local_refs, u_refs = refs[0:2], refs[2:4]
    v0_ref, vt1_ref, up1_ref, vt0_ref, up0_ref, wide_ref, down_ref, feed_ref, chip_ref = refs[4:]
    vt_refs, up_refs = (vt0_ref, vt1_ref), (up0_ref, up1_ref)
    rank = up1_ref.shape[-1] // leaves
    offsets = level_offsets(leaves)
    own = offsets[-1]
    up_table(leaves, local_refs[0], up0_ref)
    for leaf in range(leaves):
        vt0_ref[leaf] = v0_ref[leaf].T
    for member in (1, 0):
        other = 1 - member
        local_ref = local_refs[member]
        sign = 1.0 if member == 1 else -1.0
        total = None
        turned = {}

        def transfer(node):
            if node not in turned:
                turned[node] = local_ref[node, 0].T
            return turned[node]

        for leaf in range(leaves):
            rows = pl.ds(leaf * rank, rank)
            trail = None
            for depth in range(len(offsets) - 1):
                node = leaf >> depth
                step = local_ref[offsets[depth] + node, 1]
                coupling = local_ref[offsets[depth] + node, 2]
                coupled = coupling.astype(F32) if trail is None else exact_right(trail, coupling)
                for peer in range(leaves):
                    if peer >> depth != node ^ 1:
                        continue
                    entry = coupled
                    for lower in range(depth - 1, -1, -1):
                        entry = exact_right(entry, transfer(offsets[lower] + (peer >> lower)))
                    put(wide_ref, (member, rows, pl.ds((1 + peer) * rank, rank)), entry)
                trail = step.astype(F32) if trail is None else exact_right(trail, step)
            put(
                wide_ref,
                (member, rows, pl.ds((1 + leaf) * rank, rank)),
                jnp.zeros((rank, rank), F32),
            )
            put(
                wide_ref,
                (member, rows, pl.ds(0, rank)),
                exact_right(trail, local_ref[own, 2]),
            )
            below = exact_right(trail, local_ref[own, 1])
            put(down_ref, (member, rows), below)
            feed = sign * mul(mm(vt_refs[other][leaf], u_refs[member][leaf]), below)
            put(feed_ref, (member, rows), feed)
            table = tuple(
                up_refs[other][piece, :, pl.ds(leaf * rank, rank)] for piece in range(2)
            )
            term = left_mul(table, feed)
            total = term if total is None else total + term
        chip_ref[2 * member] = total[:rank]
        chip_ref[2 * member + 1] = total[rank:].T


def far_table_kernel(upper_ref, top_ref, chip_ref, got_ref, far_ref, sibling_ref):
    position = lax.axis_index("rows") // (lax.axis_size("rows") // 2)
    rank = top_ref.shape[-1]
    for member in range(2):
        put(sibling_ref, (member,), got_ref[2 * member])
        loop = pieces(chip_ref[2 * member + 1] + got_ref[2 * member + 1])
        trail = None
        levels = upper_ref.shape[1] + 1
        for level in range(levels):
            if level == levels - 1:
                coupling = jnp.where(position == 0, top_ref[member, 0], top_ref[member, 1])
            else:
                coupling = upper_ref[member, level, 2]
            coupling = coupling.T
            weight = coupling.astype(F32) if trail is None else exact_left(coupling, trail)
            if level < levels - 1:
                step = upper_ref[member, level, 1].T
                trail = step.astype(F32) if trail is None else exact_left(step, trail)
            rows = pl.ds(level * rank, rank)
            put(far_ref, (member, rows, slice(0, rank)), right_mul(weight, loop))
            put(far_ref, (member, rows, slice(rank, 2 * rank)), weight)


def rows_table(table_ref, member, index, rank):
    rows = pl.ds(index * rank, rank)
    return (table_ref[0, member, rows], table_ref[1, member, rows])


def stage_kernel(member, half, lift, upper_ref, table_ref, own_ref, *refs):
    near_ref, far_ref, cross_ref = refs[:3]
    rank = table_ref.shape[-1]
    total = right_mul(own_ref[:half], rows_table(table_ref, member, 0, rank))
    total = total + right_mul(near_ref[:half], rows_table(table_ref, member, 1, rank))
    both = far_ref[:half] + cross_ref[:half]
    total = total + exact_right(both, table_ref[0, member, pl.ds(2 * rank, rank)])
    outs = refs[3:]
    if lift is None:
        outs = outs[-1:]
    elif len(outs) > 2:
        outs = outs[-2:]
    outs[0][:half] = total
    if lift is not None:
        outs[1][:half] = exact_right(total, upper_ref[member, lift, 0])
    if outs[0].shape[0] > half:
        for ref in outs:
            ref[half:] = refs[3][...] + refs[4][...]


def far_kernel(member, last, plan, half, upper_ref, table_ref, keep_ref, got_ref, *refs):
    rank = table_ref.shape[-1] // 2
    total = None
    count = sum(plan)
    place = level = 0
    for size in plan:
        parts = [refs[place][:half]]
        if size == 3:
            parts.append(refs[place + 1][:half] + refs[place + 2][:half])
        for part in parts:
            term = right_mul(part, rows_table(table_ref, member, level, rank))
            total = term if total is None else total + term
            level += 1
        place += size
    refs[-1][...] = total[:, rank:]
    if last:
        sums = None
        for ref in refs[:count]:
            if ref.shape[0] == half + 8:
                sums = ref[half:] if sums is None else sums + ref[half:]
        refs[count][...] = sums
    else:
        value = keep_ref[...] + got_ref[rank:] + total[:, :rank]
        refs[count][...] = value
        if len(refs) == count + 3:
            refs[count + 1][...] = exact_right(value, upper_ref[1 - member, 0, 0])


def far_rows(mine_ref, theirs_ref):
    mine, theirs = mine_ref[...], theirs_ref[...]
    first = lax.axis_index("leaf") % 2 == 0
    return jnp.concatenate(
        [jnp.where(first, mine, theirs), jnp.where(first, theirs, mine)], axis=0
    ).T


def expand(member, base, far):
    if member == 0:
        return exact_left(base, far)
    return mm(base, far.astype(BF16))


def finish_value(other, rows, leaf, base_refs, u_ref, leaf_far):
    rank = u_ref.shape[-1]
    value = rows_of(base_refs, leaf, rows)
    moved = expand(other, u_ref[leaf], leaf_far[leaf * rank : (leaf + 1) * rank])
    return value + moved if other == 1 else value - moved


def local_kernel(member, first, counts, *refs):
    refs = list(refs)
    near_ref, u_ref, wide_ref, coef_ref, got_ref = (refs.pop(0) for _ in range(5))
    base_refs = tuple(refs.pop(0) for _ in range(counts[0]))
    other_refs = tuple(refs.pop(0) for _ in range(counts[1]))
    other = 1 - member
    leaves, rows, rank = u_ref.shape
    if first:
        coef = coef_ref[...]
        sibling = got_ref[:rank]
    else:
        before_ref, down_ref, feed_ref, sibling_ref, mine_ref, theirs_ref = (
            refs.pop(0) for _ in range(6)
        )
        far = far_rows(mine_ref, theirs_ref)
        coef = coef_ref[...] + left_mul((feed_ref[0, other], feed_ref[1, other]), far)
        sibling = got_ref[:rank] + left_mul((sibling_ref[0, other], sibling_ref[1, other]), far)
        leaf_far = left_mul((down_ref[0, other], down_ref[1, other]), far)
    table = (wide_ref[0, member], wide_ref[1, member])
    inner = left_mul(table, jnp.concatenate([sibling, coef], axis=0))
    norm = None
    for leaf in range(leaves):
        part = slice(leaf * rows, (leaf + 1) * rows)
        small = slice(leaf * rank, (leaf + 1) * rank)
        if first:
            value = rows_of(base_refs, leaf, rows)
        else:
            value = finish_value(other, rows, leaf, base_refs, before_ref, leaf_far)
            if other == 1:
                refs[1][part] = value
            else:
                term = jnp.sum(value * value, axis=0, keepdims=True)
                norm = term if norm is None else norm + term
        near = near_ref[member, leaf]
        if member == 0:
            result = exact_left(near, value)
        else:
            result = mm(near, value.astype(BF16))
        result = result + expand(member, u_ref[leaf], inner[small])
        if member == 0:
            result = rows_of(other_refs, leaf, rows) - result
        elif not first:
            result = rows_of(other_refs, leaf, rows) + result
        refs[0][part] = result
    if norm is not None:
        refs[1][...] = norm


def lift_kernel(other, value_ref, vt_ref, up_ref, next_ref, send_ref, keep_ref):
    leaves, rank, rows = vt_ref.shape
    for leaf in range(leaves):
        value = value_ref[leaf * rows : (leaf + 1) * rows]
        small = slice(leaf * rank, (leaf + 1) * rank)
        if other == 0:
            next_ref[small] = exact_left(vt_ref[leaf], value)
        else:
            next_ref[small] = mm(vt_ref[leaf], value.astype(BF16))
    lifted = left_mul((up_ref[0], up_ref[1]), next_ref[...])
    send_parts(lifted[:rank], lifted[rank:], send_ref, keep_ref)


def last_value_kernel(base_ref, u_ref, down_ref, mine_ref, theirs_ref, *refs):
    *old_refs, value_ref, norm_ref = refs
    leaves, rows, _ = u_ref.shape
    far = far_rows(mine_ref, theirs_ref)
    leaf_far = left_mul((down_ref[0, 0], down_ref[1, 0]), far)
    norm = None
    for leaf in range(leaves):
        value = finish_value(0, rows, leaf, (base_ref,), u_ref, leaf_far)
        value_ref[leaf * rows : (leaf + 1) * rows] = value.astype(BF16)
        term = jnp.sum(value * value, axis=0, keepdims=True)
        norm = term if norm is None else norm + term
    norm_ref[...] = jnp.zeros_like(norm_ref)
    for index, ref in enumerate(old_refs):
        norm_ref[index : index + 1] = ref[...]
    norm_ref[len(old_refs) : len(old_refs) + 1] = norm


def last_local_kernel(near_ref, u_ref, wide_ref, coef_ref, got_ref, *refs):
    value_ref, other_ref, feed_ref, sibling_ref, mine_ref, theirs_ref, out_ref = refs
    leaves, rows, rank = u_ref.shape
    far = far_rows(mine_ref, theirs_ref)
    coef = coef_ref[...] + left_mul((feed_ref[0, 0], feed_ref[1, 0]), far)
    sibling = got_ref[:rank] + left_mul((sibling_ref[0, 0], sibling_ref[1, 0]), far)
    table = (wide_ref[0, 1], wide_ref[1, 1])
    inner = left_mul(table, jnp.concatenate([sibling, coef], axis=0))
    for leaf in range(leaves):
        part = slice(leaf * rows, (leaf + 1) * rows)
        result = mm(near_ref[1, leaf], value_ref[part])
        result = result + expand(1, u_ref[leaf], inner[leaf * rank : (leaf + 1) * rank])
        out_ref[part] = other_ref[part] + result


def finish_kernel(u_ref, down_ref, base_ref, mine_ref, theirs_ref, out_ref):
    leaves, rows, _ = u_ref.shape
    far = far_rows(mine_ref, theirs_ref)
    leaf_far = left_mul((down_ref[0, 1], down_ref[1, 1]), far)
    for leaf in range(leaves):
        value = finish_value(1, rows, leaf, (base_ref,), u_ref, leaf_far)
        out_ref[leaf * rows : (leaf + 1) * rows] = value


def body(right_sides, near_blocks, leaf_bases, local_factors, upper_factors, top_couplings):
    bits_leaf = lax.axis_size("leaf").bit_length() - 1
    bits_rows = lax.axis_size("rows").bit_length() - 1
    devices = lax.axis_size("rows") * lax.axis_size("leaf")
    leaves = near_blocks.shape[1]
    columns = right_sides.shape[1]
    rank = leaf_bases.shape[-1]
    half = columns // 2
    stages = stages_of(bits_leaf + bits_rows)

    def swap(value, mask):
        pairs = [(source, source ^ mask) for source in range(devices)]
        return lax.ppermute(value, ("rows", "leaf"), pairs)

    unit = 2 * rank * rank * columns
    message = ((half, rank), F32)
    lifted = ((rank + half, rank), F32)
    coefs = ((leaves * rank, columns), F32)
    size = (right_sides.shape, F32)
    wide_half = ((right_sides.shape[0] // 2, columns), F32)
    basis = ((leaves, leaf_bases.shape[3], rank), BF16)
    turned = ((leaves, rank, leaf_bases.shape[3]), BF16)
    node = (local_factors.shape[1:], BF16)
    rises = ((2, 2 * rank, leaves * rank), BF16)
    loaded = call(
        functools.partial(start_kernel, leaves),
        [wide_half, wide_half, basis, basis, basis, node, node, turned, rises, coefs, lifted, message],
        [right_sides, leaf_bases, local_factors],
        150 * unit,
        hbm=True,
        scratch=[pltpu.VMEM(*basis), pltpu.SemaphoreType.DMA((8,))],
    )
    right = loaded[:2]
    u = loaded[2:4]
    v_operator, local_operator, local_inverse, vt_inverse, up_inverse = loaded[4:9]
    coef, send, keep = loaded[9:]
    got = swap(send, 1)
    near = near_blocks
    upper = upper_factors[:, 0]

    vt = [None, vt_inverse]
    up = [None, up_inverse]
    stage_tables, plan = [], []
    member = 1
    base = current = right
    chip = chip_risen = None
    norms = []
    mine = theirs = None
    applies = 2 * STEPS + 1
    plan = [1 if len(stage) == 1 else 3 for stage in stages]
    for index in range(applies):
        last = index == applies - 1
        other = 1 - member
        arrived = []
        value, risen = chip, chip_risen
        norm = None
        for number, stage in enumerate(stages):
            low = 2 ** stage[0]
            lower_level = stage[0] - 1
            top_stage = number == len(stages) - 1
            masks = (low,) if len(stage) == 1 else (low, 2 * low, 3 * low)
            sent = [value, risen, risen][: len(masks)]
            if index == 0 and len(stage) > 1:
                tall = message if top_stage else ((half + 2 * rank, rank), F32)
                if number == 0 or not top_stage:
                    sent = call(
                        functools.partial(pack_kernel, lower_level, top_stage),
                        [tall, tall, message],
                        [upper] + ([value] if number else [keep, got]),
                        unit,
                    )
                value = sent[0]
            elif index == 0 and value is None:
                value = keep + got[rank:]
                sent = [value] * len(masks)
            batch = [swap(data, mask) for data, mask in zip(sent, masks)]
            arrived += batch
            if index == 0 and not top_stage:
                stage_tables += call(
                    functools.partial(stage_table_kernel, lower_level, half),
                    [((2, 2, 3 * rank, rank), BF16)],
                    [upper] + batch[:2],
                    16 * unit,
                )
            if number == 0:
                if index == 0:
                    tables = call(
                        functools.partial(local_table_kernel, leaves),
                        [
                            turned,
                            rises,
                            ((2, 2, leaves * rank, (leaves + 1) * rank), BF16),
                            ((2, 2, leaves * rank, rank), BF16),
                            ((2, 2, leaves * rank, rank), BF16),
                            ((4, rank, rank), F32),
                        ],
                        [local_operator, local_inverse] + list(u) + [v_operator, vt_inverse, up_inverse],
                        300 * unit,
                    )
                    vt[0], up[0], wide, down, feed, chip_feed = tables
                    chip_got = swap(chip_feed, 1)
                if last:
                    finished, norm = call(
                        last_value_kernel,
                        [(right_sides.shape, BF16), ((8, columns), F32)],
                        [base, u[0], down, mine, theirs] + norms,
                        100 * unit,
                    )
                    norm_got = swap(norm, 1)
                    base = call(
                        last_local_kernel,
                        [size],
                        [near, u[1], wide, coef, got, finished, current, feed, sibling_table]
                        + [mine, theirs],
                        100 * unit,
                    )[0]
                else:
                    args = [near, u[member], wide, coef, got]
                    base_list = list(base) if isinstance(base, (list, tuple)) else [base]
                    other_list = list(right) if member == 0 else [] if index == 0 else [current]
                    args += base_list + other_list
                    if index:
                        args += [u[other], down, feed, sibling_table, mine, theirs]
                    outs = [size]
                    if index:
                        outs.append(size if member == 0 else ((1, columns), F32))
                    counts = (len(base_list), len(other_list))
                    results = call(
                        functools.partial(local_kernel, member, index == 0, counts),
                        outs,
                        args,
                        200 * unit,
                    )
                    base = results[0]
                    coef, send, next_keep = call(
                        functools.partial(lift_kernel, other),
                        [coefs, lifted, message],
                        [base, vt[other], up[other]],
                        100 * unit,
                    )
                    next_got = swap(send, 1)
                    if index and member == 0:
                        current = results[1]
                    elif index:
                        norms.append(results[1])
            if not top_stage:
                extra = [norm, norm_got] if last and number == len(stages) - 2 else []
                shape = ((half + (8 if extra else 0), rank), F32)
                lift = stages[number + 1][0] - 1 if len(stages[number + 1]) > 1 else None
                results = call(
                    functools.partial(stage_kernel, member, half, lift),
                    [shape] * (1 if lift is None else 2),
                    [upper, stage_tables[number], value] + batch + extra,
                    8 * unit,
                )
                value, risen = results[0], results[-1]
        if index == 0:
            far_table, sibling_table = call(
                far_table_kernel,
                [
                    ((2, 2, (upper.shape[1] + 1) * rank, 2 * rank), BF16),
                    ((2, 2, rank, rank), BF16),
                ],
                [upper, top_couplings, chip_feed, chip_got],
                100 * unit,
            )
        outs = [((8, columns), F32), message]
        if not last:
            outs = [message] * (3 if len(stages[0]) > 1 else 2)
        results = call(
            functools.partial(far_kernel, member, last, plan, half),
            outs,
            [upper, far_table] + ([keep, got] if last else [next_keep, next_got]) + arrived,
            20 * unit,
        )
        chip, chip_risen, mine = results[0], results[-2], results[-1]
        theirs = swap(mine, 1)
        if last:
            sums = chip + value[half:]
        else:
            keep, got = next_keep, next_got
        member = other
    solution = call(finish_kernel, [size], [u[1], down, base, mine, theirs], 30 * unit)[0]
    for stage in stages[:-1]:
        low = 2 ** stage[0]
        masks = (low,) if len(stage) == 1 else (low, 2 * low, 3 * low)
        sums = sum([swap(sums, mask) for mask in masks], sums)
    return solution, sums[:STEPS]


def stages_of(levels_up):
    return [tuple(range(level, min(level + 2, levels_up))) for level in range(1, levels_up, 2)]


def solution(mesh):
    placed = (
        P(("rows", "leaf"), None),
        P(None, ("rows", "leaf"), None, None),
        P(None, ("rows", "leaf"), None, None, None),
        P(None, ("rows", "leaf"), None, None, None),
        P(None, ("rows", "leaf"), None, None, None, None),
        P(),
    )

    return jax.shard_map(
        body,
        mesh=mesh,
        in_specs=placed,
        out_specs=(P(("rows", "leaf"), None), P()),
        check_vma=False,
    )
```

time: 172 us -> 153 us (0.89)
  Pallas kernels: 40.3 us -> 34.1 us
  local copies, waits for them, and re-layouts: 5.48 us -> 0.6 us
  waiting for transfers between devices: 60 us -> 55.4 us
  starting transfers between devices: 64.7 us -> 61.7 us
    pallas_call x28 -> x34, Pallas kernels: 40.3 us -> 34.1 us  [call(): pl.pallas_call(kernel, out_shape=[jax.ShapeDtypeStruct(shape, dtype) for...]
    unnamed x12 -> x6, local copies, waits for them, and re-layouts: 4.9 us -> 0.02 us
    ppermute x61, waiting for transfers between devices: 60 us -> 55.4 us  [swap(): return lax.ppermute(value, ('rows', 'leaf'), pairs)]
    ppermute x61, starting transfers between devices: 64.7 us -> 61.7 us  [swap(): return lax.ppermute(value, ('rows', 'leaf'), pairs)]
  transfers between devices with their start and end apart: 61 -> 61, of which waited for: 40 -> 39; matrix products, arithmetic and copies ran while one was open for 0% -> 0% of each run, Pallas kernels for 8% -> 9%
where the time goes in v3:
time: 153 us
  starting transfers between devices  61.7 us (40%)
  waiting for transfers between devices  55.4 us (36%)
  Pallas kernels  34.1 us (22%)
    ppermute x61, starting transfers between devices, swap(): return lax.ppermute(value, ('rows', 'leaf'), pairs)  61.7 us
    ppermute x61, waiting for transfers between devices, swap(): return lax.ppermute(value, ('rows', 'leaf'), pairs)  55.4 us
    pallas_call x34, Pallas kernels, call(): pl.pallas_call(kernel, out_shape=[jax.ShapeDtypeStruct(shape, dtype) for...  34.1 us
  transfers between devices with their start and end apart: 61, of which 39 were waited for; matrix products, arithmetic and copies ran while one was open for 0% of the time, Pallas kernels for 9%

profile of v3, /device:TPU:0, one launch (start us, length us, event | category | flops | bytes accessed | tf_op | source)
XLA Modules:
  0.0 152.8 jit_solution(12130536749982885076)
XLA Ops:
  0.6 2.4 %shard_map.77 = (f32[1024,128]{1,0:T(8,128)S(1)}, f32[1024,128]{1,0:T(8,128)S(1)}, bf16[4,512,128]{2,1,0:T(8,128)(2,1)S(1)}, bf16[4,512,128]{2,1,0:T(8,128)(2,1)...) custom-call(f32[2048,128]{1,0:T(8,128)} %refs_0_.7, ...), custom_call_target="tpu_custom_call" | custom-call | flops 629145600 | tf_op jit(solution)/shard_map/pallas_call | solution.py:67
  3.6 5.8 %shard_map.78 = (bf16[4,128,512]{2,1,0:T(8,128)(2,1)S(1)}, bf16[2,256,512]{2,1,0:T(8,128)(2,1)S(1)}, bf16[2,2,512,640]{3,2,1,0:T(8,128)(2,1)S(1)}, bf16[2,2,512,...) custom-call(bf16[7,3,128,128]{3,2,1,0:T(8,128)(2,1)S(1)} %get-tuple-element.90.refs_0_, ...), custom_call_target="tpu_custom_call" | custom-call | flops 1258291200 | tf_op jit(solution)/shard_map/pallas_call | solution.py:67
  9.7 3.0 %collective-permute-start.3 = (f32[320,128]{1,0:T(8,128)S(1)}, f32[320,128]{1,0:T(8,128)S(1)}, u32[]{:S(2)}, u32[]{:S(2)}) collective-permute-start(f32[320,128]{1,0:T(8,128)S(1)} %get-tuple-element.112.own_ref), channel_id=1, source_target_pairs={{0,2},{1,3},{2,0},{3,1},{4,6},{5,7},{6,4},{7,5},{8,10},{9,11},{10,... | collective-permute-start | bytes 491528 | tf_op jit(solution)/shard_map/ppermute | solution.py:462
  18.7 2.3 %collective-permute-done.5.refs_2_ = f32[64,128]{1,0:T(8,128)S(1)} collective-permute-done((f32[64,128]{1,0:T(8,128)S(1)}, f32[64,128]{1,0:T(8,128)S(1)}, u32[]{:S(2)}, u32[]{:S(2)}) %collective-permute-start.5) | collective-permute-done | bytes 32800 | tf_op jit(solution)/shard_map/ppermute | solution.py:462
  21.3 2.6 %collective-permute-start.7 = (f32[64,128]{1,0:T(8,128)S(1)}, f32[64,128]{1,0:T(8,128)S(1)}, u32[]{:S(2)}, u32[]{:S(2)}) collective-permute-start(f32[64,128]{1,0:T(8,128)S(1)} %get-tuple-element.116), channel_id=1, source_target_pairs={{0,16},{1,17},{2,18},{3,19},{4,20},{5,21},{6,22},{7,23},{8,24},{9,... | collective-permute-start | bytes 98312 | tf_op jit(solution)/shard_map/ppermute | solution.py:462
  26.7 2.5 %collective-permute-done.6.refs_3_ = f32[64,128]{1,0:T(8,128)S(1)} collective-permute-done((f32[64,128]{1,0:T(8,128)S(1)}, f32[64,128]{1,0:T(8,128)S(1)}, u32[]{:S(2)}, u32[]{:S(2)}) %collective-permute-start.6) | collective-permute-done | bytes 32800 | tf_op jit(solution)/shard_map/ppermute | solution.py:462
  31.3 2.1 %shard_map.86 = (f32[2048,128]{1,0:T(8,128)S(1)}, f32[2048,128]{1,0:T(8,128)S(1)}) custom-call(bf16[2,4,512,512]{3,2,1,0:T(8,128)(2,1)S(1)} %copy-done, bf16[4,512,128]{2,1,0:T(8,128)(2,1)S(1)} %get-tuple-element.92.refs_2_.refs_1_.refs_7_.u_ref, bf16[2,2,512,640]{3,2,1,0:T(8,128)(2,1)S(1)} %get-tuple-element.97.refs_2_.wide_ref, ...), custom_call_target="tpu_custom_call" | custom-call | flops 838860800 | tf_op jit(solution)/shard_map/pallas_call | solution.py:67
  35.3 2.3 %collective-permute-start.13 = (f32[64,128]{1,0:T(8,128)S(1)}, f32[64,128]{1,0:T(8,128)S(1)}, u32[]{:S(2)}, u32[]{:S(2)}) collective-permute-start(f32[64,128]{1,0:T(8,128)S(1)} %get-tuple-element.124), channel_id=1, source_target_pairs={{0,6},{1,7},{2,4},{3,5},{4,2},{5,3},{6,0},{7,1},{8,14},{9,15},{10,... | collective-permute-start | bytes 98312 | tf_op jit(solution)/shard_map/ppermute | solution.py:462
  40.4 2.6 %collective-permute-start.15 = (f32[64,128]{1,0:T(8,128)S(1)}, f32[64,128]{1,0:T(8,128)S(1)}, u32[]{:S(2)}, u32[]{:S(2)}) collective-permute-start(f32[64,128]{1,0:T(8,128)S(1)} %get-tuple-element.126), channel_id=1, source_target_pairs={{0,16},{1,17},{2,18},{3,19},{4,20},{5,21},{6,22},{7,23},{8,24},{9,... | collective-permute-start | bytes 98312 | tf_op jit(solution)/shard_map/ppermute | solution.py:462
  45.3 3.4 %collective-permute-done.16.refs_5_ = f32[64,128]{1,0:T(8,128)S(1)} collective-permute-done((f32[64,128]{1,0:T(8,128)S(1)}, f32[64,128]{1,0:T(8,128)S(1)}, u32[]{:S(2)}, u32[]{:S(2)}) %collective-permute-start.16) | collective-permute-done | bytes 32800 | tf_op jit(solution)/shard_map/ppermute | solution.py:462
  50.4 2.4 %shard_map.90 = (f32[2048,128]{1,0:T(8,128)S(1)}, f32[1,128]{1,0:T(1,128)S(1)}) custom-call(bf16[2,4,512,512]{3,2,1,0:T(8,128)(2,1)S(1)} %copy-done, bf16[4,512,128]{2,1,0:T(8,128)(2,1)S(1)} %get-tuple-element.89.refs_3_.refs_1_.refs_8_.u_ref, bf16[2,2,512,640]{3,2,1,0:T(8,128)(2,1)S(1)} %get-tuple-element.97.refs_2_.wide_ref, ...), custom_call_target="tpu_custom_call" | custom-call | flops 838860800 | tf_op jit(solution)/shard_map/pallas_call | solution.py:67
  59.0 2.3 %collective-permute-done.21.refs_2_ = f32[64,128]{1,0:T(8,128)S(1)} collective-permute-done((f32[64,128]{1,0:T(8,128)S(1)}, f32[64,128]{1,0:T(8,128)S(1)}, u32[]{:S(2)}, u32[]{:S(2)}) %collective-permute-start.21) | collective-permute-done | bytes 32800 | tf_op jit(solution)/shard_map/ppermute | solution.py:462
  61.6 2.4 %collective-permute-start.23 = (f32[64,128]{1,0:T(8,128)S(1)}, f32[64,128]{1,0:T(8,128)S(1)}, u32[]{:S(2)}, u32[]{:S(2)}) collective-permute-start(f32[64,128]{1,0:T(8,128)S(1)} %get-tuple-element.135), channel_id=1, source_target_pairs={{0,16},{1,17},{2,18},{3,19},{4,20},{5,21},{6,22},{7,23},{8,24},{9,... | collective-permute-start | bytes 98312 | tf_op jit(solution)/shard_map/ppermute | solution.py:462
  63.9 2.0 %collective-permute-start.24 = (f32[64,128]{1,0:T(8,128)S(1)}, f32[64,128]{1,0:T(8,128)S(1)}, u32[]{:S(2)}, u32[]{:S(2)}) collective-permute-start(f32[64,128]{1,0:T(8,128)S(1)} %get-tuple-element.135), channel_id=1, source_target_pairs={{0,24},{1,25},{2,26},{3,27},{4,28},{5,29},{6,30},{7,31},{8,16},{9,... | collective-permute-start | bytes 98312 | tf_op jit(solution)/shard_map/ppermute | solution.py:462
  66.5 3.2 %collective-permute-done.24.refs_5_ = f32[64,128]{1,0:T(8,128)S(1)} collective-permute-done((f32[64,128]{1,0:T(8,128)S(1)}, f32[64,128]{1,0:T(8,128)S(1)}, u32[]{:S(2)}, u32[]{:S(2)}) %collective-permute-start.24) | collective-permute-done | bytes 32800 | tf_op jit(solution)/shard_map/ppermute | solution.py:462
  71.3 2.1 %shard_map.94 = (f32[2048,128]{1,0:T(8,128)S(1)}, f32[2048,128]{1,0:T(8,128)S(1)}) custom-call(bf16[2,4,512,512]{3,2,1,0:T(8,128)(2,1)S(1)} %copy-done, bf16[4,512,128]{2,1,0:T(8,128)(2,1)S(1)} %get-tuple-element.92.refs_2_.refs_1_.refs_7_.u_ref, bf16[2,2,512,640]{3,2,1,0:T(8,128)(2,1)S(1)} %get-tuple-element.97.refs_2_.wide_ref, ...), custom_call_target="tpu_custom_call" | custom-call | flops 838860800 | tf_op jit(solution)/shard_map/pallas_call | solution.py:67
  75.3 2.3 %collective-permute-start.29 = (f32[64,128]{1,0:T(8,128)S(1)}, f32[64,128]{1,0:T(8,128)S(1)}, u32[]{:S(2)}, u32[]{:S(2)}) collective-permute-start(f32[64,128]{1,0:T(8,128)S(1)} %get-tuple-element.143), channel_id=1, source_target_pairs={{0,6},{1,7},{2,4},{3,5},{4,2},{5,3},{6,0},{7,1},{8,14},{9,15},{10,... | collective-permute-start | bytes 98312 | tf_op jit(solution)/shard_map/ppermute | solution.py:462
  80.4 2.6 %collective-permute-start.31 = (f32[64,128]{1,0:T(8,128)S(1)}, f32[64,128]{1,0:T(8,128)S(1)}, u32[]{:S(2)}, u32[]{:S(2)}) collective-permute-start(f32[64,128]{1,0:T(8,128)S(1)} %get-tuple-element.145), channel_id=1, source_target_pairs={{0,16},{1,17},{2,18},{3,19},{4,20},{5,21},{6,22},{7,23},{8,24},{9,... | collective-permute-start | bytes 98312 | tf_op jit(solution)/shard_map/ppermute | solution.py:462
  85.3 3.4 %collective-permute-done.32.refs_5_ = f32[64,128]{1,0:T(8,128)S(1)} collective-permute-done((f32[64,128]{1,0:T(8,128)S(1)}, f32[64,128]{1,0:T(8,128)S(1)}, u32[]{:S(2)}, u32[]{:S(2)}) %collective-permute-start.32) | collective-permute-done | bytes 32800 | tf_op jit(solution)/shard_map/ppermute | solution.py:462
  90.4 2.2 %shard_map.98 = (f32[2048,128]{1,0:T(8,128)S(1)}, f32[1,128]{1,0:T(1,128)S(1)}) custom-call(bf16[2,4,512,512]{3,2,1,0:T(8,128)(2,1)S(1)} %copy-done, bf16[4,512,128]{2,1,0:T(8,128)(2,1)S(1)} %get-tuple-element.89.refs_3_.refs_1_.refs_8_.u_ref, bf16[2,2,512,640]{3,2,1,0:T(8,128)(2,1)S(1)} %get-tuple-element.97.refs_2_.wide_ref, ...), custom_call_target="tpu_custom_call" | custom-call | flops 838860800 | tf_op jit(solution)/shard_map/pallas_call | solution.py:67
  98.8 2.3 %collective-permute-done.37.refs_2_ = f32[64,128]{1,0:T(8,128)S(1)} collective-permute-done((f32[64,128]{1,0:T(8,128)S(1)}, f32[64,128]{1,0:T(8,128)S(1)}, u32[]{:S(2)}, u32[]{:S(2)}) %collective-permute-start.37) | collective-permute-done | bytes 32800 | tf_op jit(solution)/shard_map/ppermute | solution.py:462
  101.4 2.4 %collective-permute-start.39 = (f32[64,128]{1,0:T(8,128)S(1)}, f32[64,128]{1,0:T(8,128)S(1)}, u32[]{:S(2)}, u32[]{:S(2)}) collective-permute-start(f32[64,128]{1,0:T(8,128)S(1)} %get-tuple-element.154), channel_id=1, source_target_pairs={{0,16},{1,17},{2,18},{3,19},{4,20},{5,21},{6,22},{7,23},{8,24},{9,... | collective-permute-start | bytes 98312 | tf_op jit(solution)/shard_map/ppermute | solution.py:462
  103.8 2.0 %collective-permute-start.40 = (f32[64,128]{1,0:T(8,128)S(1)}, f32[64,128]{1,0:T(8,128)S(1)}, u32[]{:S(2)}, u32[]{:S(2)}) collective-permute-start(f32[64,128]{1,0:T(8,128)S(1)} %get-tuple-element.154), channel_id=1, source_target_pairs={{0,24},{1,25},{2,26},{3,27},{4,28},{5,29},{6,30},{7,31},{8,16},{9,... | collective-permute-start | bytes 98312 | tf_op jit(solution)/shard_map/ppermute | solution.py:462
  106.3 3.2 %collective-permute-done.40.refs_5_ = f32[64,128]{1,0:T(8,128)S(1)} collective-permute-done((f32[64,128]{1,0:T(8,128)S(1)}, f32[64,128]{1,0:T(8,128)S(1)}, u32[]{:S(2)}, u32[]{:S(2)}) %collective-permute-start.40) | collective-permute-done | bytes 32800 | tf_op jit(solution)/shard_map/ppermute | solution.py:462
  111.1 2.1 %shard_map.102 = (f32[2048,128]{1,0:T(8,128)S(1)}, f32[2048,128]{1,0:T(8,128)S(1)}) custom-call(bf16[2,4,512,512]{3,2,1,0:T(8,128)(2,1)S(1)} %copy-done, bf16[4,512,128]{2,1,0:T(8,128)(2,1)S(1)} %get-tuple-element.92.refs_2_.refs_1_.refs_7_.u_ref, bf16[2,2,512,640]{3,2,1,0:T(8,128)(2,1)S(1)} %get-tuple-element.97.refs_2_.wide_ref, ...), custom_call_target="tpu_custom_call" | custom-call | flops 838860800 | tf_op jit(solution)/shard_map/pallas_call | solution.py:67
  115.1 2.3 %collective-permute-start.45 = (f32[64,128]{1,0:T(8,128)S(1)}, f32[64,128]{1,0:T(8,128)S(1)}, u32[]{:S(2)}, u32[]{:S(2)}) collective-permute-start(f32[64,128]{1,0:T(8,128)S(1)} %get-tuple-element.161), channel_id=1, source_target_pairs={{0,6},{1,7},{2,4},{3,5},{4,2},{5,3},{6,0},{7,1},{8,14},{9,15},{10,... | collective-permute-start | bytes 98312 | tf_op jit(solution)/shard_map/ppermute | solution.py:462
  120.3 2.6 %collective-permute-start.47 = (f32[64,128]{1,0:T(8,128)S(1)}, f32[64,128]{1,0:T(8,128)S(1)}, u32[]{:S(2)}, u32[]{:S(2)}) collective-permute-start(f32[64,128]{1,0:T(8,128)S(1)} %get-tuple-element.163), channel_id=1, source_target_pairs={{0,16},{1,17},{2,18},{3,19},{4,20},{5,21},{6,22},{7,23},{8,24},{9,... | collective-permute-start | bytes 98312 | tf_op jit(solution)/shard_map/ppermute | solution.py:462
  125.1 3.4 %collective-permute-done.48.refs_5_ = f32[64,128]{1,0:T(8,128)S(1)} collective-permute-done((f32[64,128]{1,0:T(8,128)S(1)}, f32[64,128]{1,0:T(8,128)S(1)}, u32[]{:S(2)}, u32[]{:S(2)}) %collective-permute-start.48) | collective-permute-done | bytes 32800 | tf_op jit(solution)/shard_map/ppermute | solution.py:462
  133.5 2.3 %collective-permute-done.50.refs_0_ = f32[64,128]{1,0:T(8,128)S(1)} collective-permute-done((f32[64,128]{1,0:T(8,128)S(1)}, f32[64,128]{1,0:T(8,128)S(1)}, u32[]{:S(2)}, u32[]{:S(2)}) %collective-permute-start.50) | collective-permute-done | bytes 32800 | tf_op jit(solution)/shard_map/ppermute | solution.py:462
  136.1 2.4 %collective-permute-start.55 = (f32[72,128]{1,0:T(8,128)S(1)}, f32[72,128]{1,0:T(8,128)S(1)}, u32[]{:S(2)}, u32[]{:S(2)}) collective-permute-start(f32[72,128]{1,0:T(8,128)S(1)} %get-tuple-element.173), channel_id=1, source_target_pairs={{0,16},{1,17},{2,18},{3,19},{4,20},{5,21},{6,22},{7,23},{8,24},{9,... | collective-permute-start | bytes 110600 | tf_op jit(solution)/shard_map/ppermute | solution.py:462
  138.5 2.0 %collective-permute-start.56 = (f32[72,128]{1,0:T(8,128)S(1)}, f32[72,128]{1,0:T(8,128)S(1)}, u32[]{:S(2)}, u32[]{:S(2)}) collective-permute-start(f32[72,128]{1,0:T(8,128)S(1)} %get-tuple-element.173), channel_id=1, source_target_pairs={{0,24},{1,25},{2,26},{3,27},{4,28},{5,29},{6,30},{7,31},{8,16},{9,... | collective-permute-start | bytes 110600 | tf_op jit(solution)/shard_map/ppermute | solution.py:462
  141.1 3.2 %collective-permute-done.56.refs_5_ = f32[72,128]{1,0:T(8,128)S(1)} collective-permute-done((f32[72,128]{1,0:T(8,128)S(1)}, f32[72,128]{1,0:T(8,128)S(1)}, u32[]{:S(2)}, u32[]{:S(2)}) %collective-permute-start.56) | collective-permute-done | bytes 36896 | tf_op jit(solution)/shard_map/ppermute | solution.py:462
  (133 shorter events, 67.7 us)
Async XLA Ops:
  3.1 6.5 %collective-permute-start = (f32[192,128]{1,0:T(8,128)S(1)}, f32[192,128]{1,0:T(8,128)S(1)}, u32[]{:S(2)}, u32[]{:S(2)}) collective-permute-start(f32[192,128]{1,0:T(8,128)S(1)} %get-tuple-element.99), channel_id=1, source_target_pairs={{0,1},{1,0},{2,3},{3,2},{4,5},{5,4},{6,7},{7,6},{8,9},{9,8},{10,11... | collective-permute-start | bytes 294920 | tf_op jit(solution)/shard_map/ppermute | solution.py:462
  9.5 16.1 %collective-permute-start.2 = (f32[4,128,128]{2,1,0:T(8,128)S(1)}, f32[4,128,128]{2,1,0:T(8,128)S(1)}, u32[]{:S(2)}, u32[]{:S(2)}) collective-permute-start(f32[4,128,128]{2,1,0:T(8,128)S(1)} %get-tuple-element.107.chip_ref), channel_id=1, source_target_pairs={{0,1},{1,0},{2,3},{3,2},{4,5},{5,4},{6,7},{7,6},{8,9},{9,8},{10,11... | collective-permute-start | bytes 786440 | tf_op jit(solution)/shard_map/ppermute | solution.py:462
  9.7 7.4 %collective-permute-start.3 = (f32[320,128]{1,0:T(8,128)S(1)}, f32[320,128]{1,0:T(8,128)S(1)}, u32[]{:S(2)}, u32[]{:S(2)}) collective-permute-start(f32[320,128]{1,0:T(8,128)S(1)} %get-tuple-element.112.own_ref), channel_id=1, source_target_pairs={{0,2},{1,3},{2,0},{3,1},{4,6},{5,7},{6,4},{7,5},{8,10},{9,11},{10,... | collective-permute-start | bytes 491528 | tf_op jit(solution)/shard_map/ppermute | solution.py:462
  12.7 5.9 %collective-permute-start.4 = (f32[320,128]{1,0:T(8,128)S(1)}, f32[320,128]{1,0:T(8,128)S(1)}, u32[]{:S(2)}, u32[]{:S(2)}) collective-permute-start(f32[320,128]{1,0:T(8,128)S(1)} %get-tuple-element.113), channel_id=1, source_target_pairs={{0,4},{1,5},{2,6},{3,7},{4,0},{5,1},{6,2},{7,3},{8,12},{9,13},{10,... | collective-permute-start | bytes 491528 | tf_op jit(solution)/shard_map/ppermute | solution.py:462
  16.1 10.6 %collective-permute-start.1 = (f32[192,128]{1,0:T(8,128)S(1)}, f32[192,128]{1,0:T(8,128)S(1)}, u32[]{:S(2)}, u32[]{:S(2)}) collective-permute-start(f32[192,128]{1,0:T(8,128)S(1)} %get-tuple-element.105), channel_id=1, source_target_pairs={{0,1},{1,0},{2,3},{3,2},{4,5},{5,4},{6,7},{7,6},{8,9},{9,8},{10,11... | collective-permute-start | bytes 294920 | tf_op jit(solution)/shard_map/ppermute | solution.py:462
  16.2 4.9 %collective-permute-start.5 = (f32[64,128]{1,0:T(8,128)S(1)}, f32[64,128]{1,0:T(8,128)S(1)}, u32[]{:S(2)}, u32[]{:S(2)}) collective-permute-start(f32[64,128]{1,0:T(8,128)S(1)} %get-tuple-element.114), channel_id=1, source_target_pairs={{0,6},{1,7},{2,4},{3,5},{4,2},{5,3},{6,0},{7,1},{8,14},{9,15},{10,... | collective-permute-start | bytes 98312 | tf_op jit(solution)/shard_map/ppermute | solution.py:462
  21.3 7.9 %collective-permute-start.7 = (f32[64,128]{1,0:T(8,128)S(1)}, f32[64,128]{1,0:T(8,128)S(1)}, u32[]{:S(2)}, u32[]{:S(2)}) collective-permute-start(f32[64,128]{1,0:T(8,128)S(1)} %get-tuple-element.116), channel_id=1, source_target_pairs={{0,16},{1,17},{2,18},{3,19},{4,20},{5,21},{6,22},{7,23},{8,24},{9,... | collective-permute-start | bytes 98312 | tf_op jit(solution)/shard_map/ppermute | solution.py:462
  23.9 5.7 %collective-permute-start.8 = (f32[64,128]{1,0:T(8,128)S(1)}, f32[64,128]{1,0:T(8,128)S(1)}, u32[]{:S(2)}, u32[]{:S(2)}) collective-permute-start(f32[64,128]{1,0:T(8,128)S(1)} %get-tuple-element.116), channel_id=1, source_target_pairs={{0,24},{1,25},{2,26},{3,27},{4,28},{5,29},{6,30},{7,31},{8,16},{9,... | collective-permute-start | bytes 98312 | tf_op jit(solution)/shard_map/ppermute | solution.py:462
  33.9 14.9 %collective-permute-start.10 = (f32[192,128]{1,0:T(8,128)S(1)}, f32[192,128]{1,0:T(8,128)S(1)}, u32[]{:S(2)}, u32[]{:S(2)}) collective-permute-start(f32[192,128]{1,0:T(8,128)S(1)} %get-tuple-element.120), channel_id=1, source_target_pairs={{0,1},{1,0},{2,3},{3,2},{4,5},{5,4},{6,7},{7,6},{8,9},{9,8},{10,11... | collective-permute-start | bytes 294920 | tf_op jit(solution)/shard_map/ppermute | solution.py:462
  35.3 4.8 %collective-permute-start.13 = (f32[64,128]{1,0:T(8,128)S(1)}, f32[64,128]{1,0:T(8,128)S(1)}, u32[]{:S(2)}, u32[]{:S(2)}) collective-permute-start(f32[64,128]{1,0:T(8,128)S(1)} %get-tuple-element.124), channel_id=1, source_target_pairs={{0,6},{1,7},{2,4},{3,5},{4,2},{5,3},{6,0},{7,1},{8,14},{9,15},{10,... | collective-permute-start | bytes 98312 | tf_op jit(solution)/shard_map/ppermute | solution.py:462
  40.4 4.9 %collective-permute-start.15 = (f32[64,128]{1,0:T(8,128)S(1)}, f32[64,128]{1,0:T(8,128)S(1)}, u32[]{:S(2)}, u32[]{:S(2)}) collective-permute-start(f32[64,128]{1,0:T(8,128)S(1)} %get-tuple-element.126), channel_id=1, source_target_pairs={{0,16},{1,17},{2,18},{3,19},{4,20},{5,21},{6,22},{7,23},{8,24},{9,... | collective-permute-start | bytes 98312 | tf_op jit(solution)/shard_map/ppermute | solution.py:462
  43.0 5.7 %collective-permute-start.16 = (f32[64,128]{1,0:T(8,128)S(1)}, f32[64,128]{1,0:T(8,128)S(1)}, u32[]{:S(2)}, u32[]{:S(2)}) collective-permute-start(f32[64,128]{1,0:T(8,128)S(1)} %get-tuple-element.126), channel_id=1, source_target_pairs={{0,24},{1,25},{2,26},{3,27},{4,28},{5,29},{6,30},{7,31},{8,16},{9,... | collective-permute-start | bytes 98312 | tf_op jit(solution)/shard_map/ppermute | solution.py:462
  53.3 16.3 %collective-permute-start.18 = (f32[192,128]{1,0:T(8,128)S(1)}, f32[192,128]{1,0:T(8,128)S(1)}, u32[]{:S(2)}, u32[]{:S(2)}) collective-permute-start(f32[192,128]{1,0:T(8,128)S(1)} %get-tuple-element.130), channel_id=1, source_target_pairs={{0,1},{1,0},{2,3},{3,2},{4,5},{5,4},{6,7},{7,6},{8,9},{9,8},{10,11... | collective-permute-start | bytes 294920 | tf_op jit(solution)/shard_map/ppermute | solution.py:462
  56.5 4.8 %collective-permute-start.21 = (f32[64,128]{1,0:T(8,128)S(1)}, f32[64,128]{1,0:T(8,128)S(1)}, u32[]{:S(2)}, u32[]{:S(2)}) collective-permute-start(f32[64,128]{1,0:T(8,128)S(1)} %get-tuple-element.133), channel_id=1, source_target_pairs={{0,6},{1,7},{2,4},{3,5},{4,2},{5,3},{6,0},{7,1},{8,14},{9,15},{10,... | collective-permute-start | bytes 98312 | tf_op jit(solution)/shard_map/ppermute | solution.py:462
  61.6 4.9 %collective-permute-start.23 = (f32[64,128]{1,0:T(8,128)S(1)}, f32[64,128]{1,0:T(8,128)S(1)}, u32[]{:S(2)}, u32[]{:S(2)}) collective-permute-start(f32[64,128]{1,0:T(8,128)S(1)} %get-tuple-element.135), channel_id=1, source_target_pairs={{0,16},{1,17},{2,18},{3,19},{4,20},{5,21},{6,22},{7,23},{8,24},{9,... | collective-permute-start | bytes 98312 | tf_op jit(solution)/shard_map/ppermute | solution.py:462
  63.9 5.7 %collective-permute-start.24 = (f32[64,128]{1,0:T(8,128)S(1)}, f32[64,128]{1,0:T(8,128)S(1)}, u32[]{:S(2)}, u32[]{:S(2)}) collective-permute-start(f32[64,128]{1,0:T(8,128)S(1)} %get-tuple-element.135), channel_id=1, source_target_pairs={{0,24},{1,25},{2,26},{3,27},{4,28},{5,29},{6,30},{7,31},{8,16},{9,... | collective-permute-start | bytes 98312 | tf_op jit(solution)/shard_map/ppermute | solution.py:462
  73.9 14.8 %collective-permute-start.26 = (f32[192,128]{1,0:T(8,128)S(1)}, f32[192,128]{1,0:T(8,128)S(1)}, u32[]{:S(2)}, u32[]{:S(2)}) collective-permute-start(f32[192,128]{1,0:T(8,128)S(1)} %get-tuple-element.139), channel_id=1, source_target_pairs={{0,1},{1,0},{2,3},{3,2},{4,5},{5,4},{6,7},{7,6},{8,9},{9,8},{10,11... | collective-permute-start | bytes 294920 | tf_op jit(solution)/shard_map/ppermute | solution.py:462
  75.3 4.8 %collective-permute-start.29 = (f32[64,128]{1,0:T(8,128)S(1)}, f32[64,128]{1,0:T(8,128)S(1)}, u32[]{:S(2)}, u32[]{:S(2)}) collective-permute-start(f32[64,128]{1,0:T(8,128)S(1)} %get-tuple-element.143), channel_id=1, source_target_pairs={{0,6},{1,7},{2,4},{3,5},{4,2},{5,3},{6,0},{7,1},{8,14},{9,15},{10,... | collective-permute-start | bytes 98312 | tf_op jit(solution)/shard_map/ppermute | solution.py:462
  80.4 4.9 %collective-permute-start.31 = (f32[64,128]{1,0:T(8,128)S(1)}, f32[64,128]{1,0:T(8,128)S(1)}, u32[]{:S(2)}, u32[]{:S(2)}) collective-permute-start(f32[64,128]{1,0:T(8,128)S(1)} %get-tuple-element.145), channel_id=1, source_target_pairs={{0,16},{1,17},{2,18},{3,19},{4,20},{5,21},{6,22},{7,23},{8,24},{9,... | collective-permute-start | bytes 98312 | tf_op jit(solution)/shard_map/ppermute | solution.py:462
  83.0 5.7 %collective-permute-start.32 = (f32[64,128]{1,0:T(8,128)S(1)}, f32[64,128]{1,0:T(8,128)S(1)}, u32[]{:S(2)}, u32[]{:S(2)}) collective-permute-start(f32[64,128]{1,0:T(8,128)S(1)} %get-tuple-element.145), channel_id=1, source_target_pairs={{0,24},{1,25},{2,26},{3,27},{4,28},{5,29},{6,30},{7,31},{8,16},{9,... | collective-permute-start | bytes 98312 | tf_op jit(solution)/shard_map/ppermute | solution.py:462
  93.2 16.3 %collective-permute-start.34 = (f32[192,128]{1,0:T(8,128)S(1)}, f32[192,128]{1,0:T(8,128)S(1)}, u32[]{:S(2)}, u32[]{:S(2)}) collective-permute-start(f32[192,128]{1,0:T(8,128)S(1)} %get-tuple-element.149), channel_id=1, source_target_pairs={{0,1},{1,0},{2,3},{3,2},{4,5},{5,4},{6,7},{7,6},{8,9},{9,8},{10,11... | collective-permute-start | bytes 294920 | tf_op jit(solution)/shard_map/ppermute | solution.py:462
  96.3 4.8 %collective-permute-start.37 = (f32[64,128]{1,0:T(8,128)S(1)}, f32[64,128]{1,0:T(8,128)S(1)}, u32[]{:S(2)}, u32[]{:S(2)}) collective-permute-start(f32[64,128]{1,0:T(8,128)S(1)} %get-tuple-element.152), channel_id=1, source_target_pairs={{0,6},{1,7},{2,4},{3,5},{4,2},{5,3},{6,0},{7,1},{8,14},{9,15},{10,... | collective-permute-start | bytes 98312 | tf_op jit(solution)/shard_map/ppermute | solution.py:462
  101.4 4.9 %collective-permute-start.39 = (f32[64,128]{1,0:T(8,128)S(1)}, f32[64,128]{1,0:T(8,128)S(1)}, u32[]{:S(2)}, u32[]{:S(2)}) collective-permute-start(f32[64,128]{1,0:T(8,128)S(1)} %get-tuple-element.154), channel_id=1, source_target_pairs={{0,16},{1,17},{2,18},{3,19},{4,20},{5,21},{6,22},{7,23},{8,24},{9,... | collective-permute-start | bytes 98312 | tf_op jit(solution)/shard_map/ppermute | solution.py:462
  103.8 5.7 %collective-permute-start.40 = (f32[64,128]{1,0:T(8,128)S(1)}, f32[64,128]{1,0:T(8,128)S(1)}, u32[]{:S(2)}, u32[]{:S(2)}) collective-permute-start(f32[64,128]{1,0:T(8,128)S(1)} %get-tuple-element.154), channel_id=1, source_target_pairs={{0,24},{1,25},{2,26},{3,27},{4,28},{5,29},{6,30},{7,31},{8,16},{9,... | collective-permute-start | bytes 98312 | tf_op jit(solution)/shard_map/ppermute | solution.py:462
  113.7 14.8 %collective-permute-start.42 = (f32[192,128]{1,0:T(8,128)S(1)}, f32[192,128]{1,0:T(8,128)S(1)}, u32[]{:S(2)}, u32[]{:S(2)}) collective-permute-start(f32[192,128]{1,0:T(8,128)S(1)} %get-tuple-element.158), channel_id=1, source_target_pairs={{0,1},{1,0},{2,3},{3,2},{4,5},{5,4},{6,7},{7,6},{8,9},{9,8},{10,11... | collective-permute-start | bytes 294920 | tf_op jit(solution)/shard_map/ppermute | solution.py:462
  120.3 4.9 %collective-permute-start.47 = (f32[64,128]{1,0:T(8,128)S(1)}, f32[64,128]{1,0:T(8,128)S(1)}, u32[]{:S(2)}, u32[]{:S(2)}) collective-permute-start(f32[64,128]{1,0:T(8,128)S(1)} %get-tuple-element.163), channel_id=1, source_target_pairs={{0,16},{1,17},{2,18},{3,19},{4,20},{5,21},{6,22},{7,23},{8,24},{9,... | collective-permute-start | bytes 98312 | tf_op jit(solution)/shard_map/ppermute | solution.py:462
  122.9 5.7 %collective-permute-start.48 = (f32[64,128]{1,0:T(8,128)S(1)}, f32[64,128]{1,0:T(8,128)S(1)}, u32[]{:S(2)}, u32[]{:S(2)}) collective-permute-start(f32[64,128]{1,0:T(8,128)S(1)} %get-tuple-element.163), channel_id=1, source_target_pairs={{0,24},{1,25},{2,26},{3,27},{4,28},{5,29},{6,30},{7,31},{8,16},{9,... | collective-permute-start | bytes 98312 | tf_op jit(solution)/shard_map/ppermute | solution.py:462
  129.0 6.8 %collective-permute-start.51 = (f32[64,128]{1,0:T(8,128)S(1)}, f32[64,128]{1,0:T(8,128)S(1)}, u32[]{:S(2)}, u32[]{:S(2)}) collective-permute-start(f32[64,128]{1,0:T(8,128)S(1)} %get-tuple-element.170), channel_id=1, source_target_pairs={{0,4},{1,5},{2,6},{3,7},{4,0},{5,1},{6,2},{7,3},{8,12},{9,13},{10,... | collective-permute-start | bytes 98312 | tf_op jit(solution)/shard_map/ppermute | solution.py:462
  130.4 5.4 %collective-permute-start.52 = (f32[64,128]{1,0:T(8,128)S(1)}, f32[64,128]{1,0:T(8,128)S(1)}, u32[]{:S(2)}, u32[]{:S(2)}) collective-permute-start(f32[64,128]{1,0:T(8,128)S(1)} %get-tuple-element.170), channel_id=1, source_target_pairs={{0,6},{1,7},{2,4},{3,5},{4,2},{5,3},{6,0},{7,1},{8,14},{9,15},{10,... | collective-permute-start | bytes 98312 | tf_op jit(solution)/shard_map/ppermute | solution.py:462
  136.1 4.9 %collective-permute-start.55 = (f32[72,128]{1,0:T(8,128)S(1)}, f32[72,128]{1,0:T(8,128)S(1)}, u32[]{:S(2)}, u32[]{:S(2)}) collective-permute-start(f32[72,128]{1,0:T(8,128)S(1)} %get-tuple-element.173), channel_id=1, source_target_pairs={{0,16},{1,17},{2,18},{3,19},{4,20},{5,21},{6,22},{7,23},{8,24},{9,... | collective-permute-start | bytes 110600 | tf_op jit(solution)/shard_map/ppermute | solution.py:462
  138.5 5.8 %collective-permute-start.56 = (f32[72,128]{1,0:T(8,128)S(1)}, f32[72,128]{1,0:T(8,128)S(1)}, u32[]{:S(2)}, u32[]{:S(2)}) collective-permute-start(f32[72,128]{1,0:T(8,128)S(1)} %get-tuple-element.173), channel_id=1, source_target_pairs={{0,24},{1,25},{2,26},{3,27},{4,28},{5,29},{6,30},{7,31},{8,16},{9,... | collective-permute-start | bytes 110600 | tf_op jit(solution)/shard_map/ppermute | solution.py:462
  144.5 5.3 %collective-permute-start.60 = (f32[8,128]{1,0:T(8,128)S(1)}, f32[8,128]{1,0:T(8,128)S(1)}, u32[]{:S(2)}, u32[]{:S(2)}) collective-permute-start(f32[8,128]{1,0:T(8,128)S(1)} %slice_add_fusion), channel_id=1, source_target_pairs={{0,6},{1,7},{2,4},{3,5},{4,2},{5,3},{6,0},{7,1},{8,14},{9,15},{10,... | collective-permute-start | bytes 12296 | tf_op jit(solution)/shard_map/ppermute | solution.py:462
  (32 other events, 126.5 us)
